TPU v7x, 256 devices: a whole 4x4x8 slice. The times are simulated.
256 devices in a mesh: seq: 64 (over z, y, core), head: 4 (over x).
Axes of the slice: x: 4, y: 4, z: 8, core: 2. Of those that a mesh axis runs over, the one named last changes fastest.
Arguments:
- queries: bfloat16 [16384, 4096], P('seq', 'head'), may hold values from -5 to 5
- keys: bfloat16 [16384, 4096], P('seq', 'head'), may hold values from -5 to 5
- values: bfloat16 [16384, 4096], P('seq', 'head'), may hold values from -6 to 6
- beta: float32 [32], P('head'), may hold values from -2 to 2
- w_out: bfloat16 [4096, 4096], P('head'), may hold values from -0.09375 to 0.09375
Outputs:
- mixed: bfloat16 [16384, 4096], P('seq', 'head')
All inputs are finite; a program needn't handle non-finite values.
Results may differ from a plain program's by a relative error of at most 0.0069.
Values may be sent and summed in bfloat16 or wider, within the bound.
No kernel may reach another device: no remote copies, remote signals or barrier semaphores. Data moves between devices by JAX's collectives and lax.ppermute only.
A program may use at most 192 MiB of HBM per device.

v0:
```python
import jax
import jax.numpy as jnp
from jax import lax
from jax.experimental import pallas as pl
from jax.experimental.pallas import tpu as pltpu
from jax.sharding import Mesh
from jax.sharding import PartitionSpec as P


HD = 128
BLK = 256
NB = 8
PLANE = ("seq_1", "seq_2")
SCALE2 = (HD**-0.5) * 1.4426950408889634
F32 = jnp.float32
BF16 = jnp.bfloat16
ANY = pl.BlockSpec(memory_space=pl.ANY)
SMEM = pl.BlockSpec(memory_space=pltpu.SMEM)
VMEM = pl.BlockSpec(memory_space=pltpu.VMEM)
HBM = pl.BlockSpec(memory_space=pltpu.HBM)
NEAR = (0, 1, 7, 2, 6)
FAR = (3, 5, 4)


def shifted(block, axis, distance, wrap=True):
    size = lax.axis_size(axis)
    if wrap:
        route = [(i, (i + distance) % size) for i in range(size)]
    else:
        route = [(i, i + distance) for i in range(size - distance)]
    return lax.ppermute(block, axis, route)


def elu_plus(inputs):
    return jnp.where(inputs > 0, inputs + 1.0, jnp.exp(jnp.minimum(inputs, 0.0)))


def slot_of(here, d):
    return lax.rem(here - d + NB, NB)


def params(flops, nbytes, room=16):
    return dict(
        cost_estimate=pl.CostEstimate(flops=flops, bytes_accessed=nbytes, transcendentals=0),
        compiler_params=pltpu.CompilerParams(vmem_limit_bytes=room * 1024 * 1024),
    )


def place_rows(here, d):
    return pl.ds(pl.multiple_of(slot_of(here, d) * BLK, BLK), BLK)


def split_kernel(*refs):
    here_ref, keys, values, queries = refs[:4]
    kvs, qs = refs[4 : 4 + NB], refs[4 + NB : 4 + 2 * NB]
    sems = refs[4 + 2 * NB]
    here = here_ref[0]
    copies = []
    for d in range(NB):
        cols = pl.ds(pl.multiple_of(lax.rem(here + d, NB) * HD, HD), HD)
        copies.append(pltpu.make_async_copy(keys.at[:, cols], kvs[d].at[0], sems.at[0, d]))
        copies.append(pltpu.make_async_copy(values.at[:, cols], kvs[d].at[1], sems.at[1, d]))
    for d in range(NB):
        cols = pl.ds(pl.multiple_of(lax.rem(here + d, NB) * HD, HD), HD)
        copies.append(pltpu.make_async_copy(queries.at[:, cols], qs[d], sems.at[2, d]))
    for copy in copies:
        copy.start()
    for copy in copies:
        copy.wait()


def split_heads(here, keys, values, queries):
    out = pl.pallas_call(
        split_kernel,
        out_shape=[jax.ShapeDtypeStruct((2, BLK, HD), BF16)] * NB
        + [jax.ShapeDtypeStruct((BLK, HD), BF16)] * NB,
        in_specs=[SMEM] + [HBM] * 3,
        out_specs=[VMEM] * (2 * NB),
        scratch_shapes=[pltpu.SemaphoreType.DMA((3, NB))],
        name="split",
        **params(0, 3 << 20),
    )(here, keys, values, queries)
    return out[:NB], out[NB:]


def pack_kernel(*refs):
    for spot, piece in enumerate(refs[:-1]):
        refs[-1][2 * spot : 2 * spot + 2] = piece[...]


def pack(pieces):
    return pl.pallas_call(
        pack_kernel,
        out_shape=jax.ShapeDtypeStruct((2 * len(pieces), BLK, HD), BF16),
        in_specs=[VMEM] * len(pieces),
        out_specs=VMEM,
        name="pack",
        **params(0, 1 << 18),
    )(*pieces)


def terms_kernel(*refs):
    pieces, out = refs[:NB], refs[NB]
    outer = jnp.zeros((HD, HD), F32)
    totals = jnp.zeros((8, HD), F32)
    for d in range(NB):
        soft = elu_plus(pieces[d][0].astype(F32)).astype(BF16)
        outer = outer + lax.dot_general(
            soft, pieces[d][1], (((0,), (0,)), ((), ())), preferred_element_type=F32
        )
        totals = totals + jnp.dot(jnp.ones((8, BLK), BF16), soft, preferred_element_type=F32)
    out[0:HD, :] = outer
    out[HD : HD + 8, :] = totals


def memory_terms(pieces):
    return pl.pallas_call(
        terms_kernel,
        out_shape=jax.ShapeDtypeStruct((HD + 8, HD), F32),
        in_specs=[VMEM] * NB,
        out_specs=VMEM,
        name="terms",
        **params(2 * 2048 * HD * HD, 1 << 20),
    )(*pieces)


def attend(query, keys, values_ones, scores, first, count, mask_at, mask, start_max=None):
    peak = start_max
    for j in range(count):
        rows = pl.ds((first + j) * BLK, BLK)
        part = lax.dot_general(
            query, keys[rows, :], (((1,), (1,)), ((), ())), preferred_element_type=F32
        )
        if j == mask_at:
            part = jnp.where(mask, part, -jnp.inf)
        scores[:, j * BLK : (j + 1) * BLK] = part
        high = jnp.maximum(part[:, :HD], part[:, HD:])
        peak = high if peak is None else jnp.maximum(peak, high)
    peak = jnp.max(peak, axis=1, keepdims=True)
    shift = peak * SCALE2
    acc = None
    for j in range(count):
        rows = pl.ds((first + j) * BLK, BLK)
        weights = jnp.exp2(scores[:, j * BLK : (j + 1) * BLK] * SCALE2 - shift).astype(BF16)
        part = jnp.dot(weights, values_ones[rows, :], preferred_element_type=F32)
        acc = part if acc is None else acc + part
    return acc, peak


def own_kernel(*refs):
    here_ref = refs[0]
    kvs, qs = refs[1 : 1 + NB], refs[1 + NB : 1 + 2 * NB]
    weight, acc_out, peak_out, weight_out = refs[1 + 2 * NB : 5 + 2 * NB]
    keys, values, query, scores_a, scores_b, sem = refs[5 + 2 * NB :]
    fetch = pltpu.make_async_copy(weight, weight_out, sem)
    fetch.start()
    here = here_ref[0]
    for d in range(NB):
        rows = place_rows(here, d)
        keys[rows, :] = kvs[d][0]
        values[rows, :HD] = kvs[d][1]
        query[rows, :] = qs[d][...]
    values[:, HD:] = jnp.ones((NB * BLK, HD), BF16)
    row = lax.broadcasted_iota(jnp.int32, (BLK, BLK), 0)
    col = lax.broadcasted_iota(jnp.int32, (BLK, BLK), 1)
    for b in range(NB):
        rows = pl.ds(b * BLK, BLK)
        acc, peak = attend(
            query[rows, :], keys, values, (scores_a, scores_b)[b % 2], 0, b + 1, b, col <= row
        )
        acc_out[rows, :] = acc
        peak_out[rows, :] = jnp.broadcast_to(peak, (BLK, HD))
    fetch.wait()


def own_part(here, kvs, qs, weight):
    rows = NB * BLK
    return pl.pallas_call(
        own_kernel,
        out_shape=(
            jax.ShapeDtypeStruct((rows, 2 * HD), F32),
            jax.ShapeDtypeStruct((rows, HD), F32),
            jax.ShapeDtypeStruct(weight.shape, BF16),
        ),
        in_specs=[SMEM] + [VMEM] * (2 * NB) + [HBM],
        out_specs=(VMEM, VMEM, VMEM),
        scratch_shapes=[
            pltpu.VMEM((rows, HD), BF16),
            pltpu.VMEM((rows, 2 * HD), BF16),
            pltpu.VMEM((rows, HD), BF16),
            pltpu.VMEM((BLK, rows), F32),
            pltpu.VMEM((BLK, rows), F32),
            pltpu.SemaphoreType.DMA,
        ],
        name="own",
        **params(36 * BLK * BLK * HD * 8, 5 << 20, 24),
    )(here, *kvs, *qs, weight)


def past_kernel(*refs):
    here_ref, beta_ref = refs[0], refs[1]
    near, far = refs[2:4]
    qs = refs[4 : 4 + NB]
    acc_in, peak_in, memory_ref, more_ref = refs[4 + NB : 8 + NB]
    outs = refs[8 + NB : 8 + 2 * NB]
    keys, values, query, scores_a, scores_b, result, acc_buf = refs[8 + 2 * NB :]
    here, segment = here_ref[0], here_ref[1]
    for d in range(NB):
        rows = place_rows(here, d)
        part, spot = (near, NEAR.index(d)) if d in NEAR else (far, FAR.index(d))
        keys[rows, :] = part[2 * spot]
        values[rows, :HD] = part[2 * spot + 1]
        query[rows, :] = qs[d][...]
    values[:, HD:] = jnp.ones((NB * BLK, HD), BF16)

    @pl.when(segment == 0)
    def _():
        acc_buf[...] = acc_in[...]

    @pl.when(segment > 0)
    def _():
        row = lax.broadcasted_iota(jnp.int32, (BLK, BLK), 0)
        col = lax.broadcasted_iota(jnp.int32, (BLK, BLK), 1)
        for b in range(NB):
            rows = pl.ds(b * BLK, BLK)
            before = peak_in[rows, :]
            acc, peak = attend(
                query[rows, :],
                keys,
                values,
                (scores_a, scores_b)[b % 2],
                b,
                NB - b,
                0,
                col > row,
                before,
            )
            fade = jnp.exp2((before - peak) * SCALE2)
            acc_buf[rows, :HD] = acc[:, :HD] + acc_in[rows, :HD] * fade
            acc_buf[rows, HD:] = acc[:, HD:] + acc_in[rows, HD:] * fade

    total = memory_ref[...] + more_ref[...]
    memory = total[0:HD, :]
    norm = jnp.transpose(jnp.broadcast_to(total[HD : HD + 1, :], (HD, HD)))
    whole = jnp.concatenate([memory, norm], axis=1)
    upper = whole.astype(BF16)
    lower = (whole - upper.astype(F32)).astype(BF16)
    split = jnp.concatenate([upper, lower], axis=0)
    gate = 1.0 / (1.0 + jnp.exp(-jnp.full((1, HD), beta_ref[here], F32)))
    for b in range(NB):
        rows = pl.ds(b * BLK, BLK)
        soft = elu_plus(query[rows, :].astype(F32)).astype(BF16)
        both = jnp.dot(jnp.concatenate([soft, soft], axis=1), split, preferred_element_type=F32)
        from_memory = both[:, :HD] / (1.0 + both[:, HD:])
        local = acc_buf[rows, :HD] / acc_buf[rows, HD:]
        result[rows, :] = (gate * from_memory + (1.0 - gate) * local).astype(BF16)
    for d in range(NB):
        outs[d][...] = result[place_rows(here, d), :]


def past_part(here, beta, kvs, qs, acc, peak, memory):
    rows = NB * BLK
    return pl.pallas_call(
        past_kernel,
        out_shape=[jax.ShapeDtypeStruct((BLK, HD), BF16)] * NB,
        in_specs=[SMEM, SMEM] + [VMEM] * (6 + NB),
        out_specs=[VMEM] * NB,
        scratch_shapes=[
            pltpu.VMEM((rows, HD), BF16),
            pltpu.VMEM((rows, 2 * HD), BF16),
            pltpu.VMEM((rows, HD), BF16),
            pltpu.VMEM((BLK, rows), F32),
            pltpu.VMEM((BLK, rows), F32),
            pltpu.VMEM((rows, HD), BF16),
            pltpu.VMEM((rows, 2 * HD), F32),
        ],
        name="past",
        **params(36 * BLK * BLK * HD * 8, 6 << 20, 24),
    )(here, beta, *kvs, *qs, acc, peak, *memory)


def project_kernel(*refs):
    spot_ref = refs[0]
    pieces, weight = refs[1 : 1 + NB], refs[1 + NB]
    out = refs[2 + NB]
    attended = refs[3 + NB]
    for d in range(NB):
        start = pl.multiple_of(lax.rem(spot_ref[0] + d, NB) * HD, HD)
        attended[:, pl.ds(start, HD)] = pieces[d][...]
    width = out.shape[1]
    cols = pl.ds(pl.multiple_of(lax.rem(spot_ref[2] + spot_ref[3], 4) * width, width), width)
    out[...] = jnp.dot(
        attended[...], weight[:, cols], preferred_element_type=F32
    ).astype(out.dtype)


def project(place, pieces, weight, dtype):
    width = weight.shape[1] // 4
    return pl.pallas_call(
        project_kernel,
        in_specs=[SMEM] + [VMEM] * (1 + NB),
        out_specs=VMEM,
        scratch_shapes=[pltpu.VMEM((BLK, NB * HD), BF16)],
        out_shape=jax.ShapeDtypeStruct((BLK, width), dtype),
        name="project",
        **params(2 * BLK * NB * HD * width, 3 << 20),
    )(place, *pieces, weight)


def layer(queries, keys, values, beta, w_out):
    here = lax.axis_index(PLANE)
    segment = lax.axis_index("seq_0")
    column = lax.axis_index("head")

    def place(e):
        return jnp.stack((here, segment, column, e)).astype(jnp.int32)

    keys, values, queries, w_out = (
        pltpu.with_memory_space_constraint(part, pltpu.HBM)
        for part in (keys, values, queries, w_out)
    )
    kv_here, q_here = split_heads(place(0), keys, values, queries)
    order = NEAR[1:] + FAR
    kvs, qs = {0: kv_here[0]}, {0: q_here[0]}
    for d in order:
        kvs[d] = shifted(kv_here[d], PLANE, d)
    kvs_past = []
    for part in (NEAR, FAR):
        kvs_past.append(shifted(pack([kvs[d] for d in part]), "seq_0", 1, wrap=False))
    for d in order:
        qs[d] = shifted(q_here[d], PLANE, d)
    kvs, qs = [kvs[d] for d in range(NB)], [qs[d] for d in range(NB)]

    terms = memory_terms(kvs)
    after = shifted(terms, "seq_0", -1)
    whole = terms + after
    wrapped = jnp.where(segment == 7, after, 0.0)
    chosen = jnp.where(segment <= 5, whole, wrapped)
    after = shifted(chosen, "seq_0", -2)
    window = jnp.where(segment <= 3, whole, wrapped) + after
    after = shifted(window, "seq_0", -4)
    memory = (jnp.where(segment <= 3, 0.0, window), after)

    acc, peak, weight = own_part(place(0), kvs, qs, w_out)
    attended = past_part(place(0), beta, kvs_past, qs, acc, peak, memory)
    heads = [attended[0]] + [shifted(attended[d], PLANE, NB - d) for d in range(1, NB)]

    total = None
    for e in (2, 1, 3, 0):
        part = project(place(e), heads, weight, BF16 if e else F32)
        if e:
            part = shifted(part, "head", e).astype(F32)
        total = part if total is None else total + part
    return total.astype(BF16)


def solution(mesh):
    torus = Mesh(
        mesh.devices.reshape(8, 4, 2, mesh.shape["head"]), ("seq_0", "seq_1", "seq_2", "head")
    )
    seq = ("seq_0", "seq_1", "seq_2")
    return jax.shard_map(
        layer,
        mesh=torus,
        in_specs=(P(seq, "head"), P(seq, "head"), P(seq, "head"), P("head"), P("head", None)),
        out_specs=P(seq, "head"),
        check_vma=False,
    )
```

profile of v0, /device:TPU:64, one launch (start us, length us, event | category | flops | bytes accessed | tf_op | source)
XLA Modules:
  0.0 101.2 jit_solution(5287763740351854018)
XLA Ops:
  0.2 2.2 %split.1 = (bf16[2,256,128]{2,1,0:T(8,128)(2,1)S(1)}, bf16[2,256,128]{2,1,0:T(8,128)(2,1)S(1)}, bf16[2,256,128]{2,1,0:T(8,128)(2,1)S(1)}, bf16[2,256,128]{2,1,0:...) custom-call(s32[4]{0:T(128)S(1)} %get-tuple-element.64.refs_0_, ...), custom_call_target="tpu_custom_call" | custom-call | bytes 3145728 | tf_op jit(solution)/shard_map/split/pallas_call | solution.py:73
  2.4 2.9 %collective-permute-start.1 = (bf16[2,256,128]{2,1,0:T(8,128)(2,1)S(1)}, bf16[2,256,128]{2,1,0:T(8,128)(2,1)S(1)}, u32[]{:S(2)}, u32[]{:S(2)}) collective-permute-start(bf16[2,256,128]{2,1,0:T(8,128)(2,1)S(1)} %get-tuple-element.34), channel_id=1, source_target_pairs={{0,28},{4,0},{8,4},{12,8},{16,12},{20,16},{24,20},{28,24},{1,29},{... | collective-permute-start | bytes 393224 | tf_op jit(solution)/shard_map/ppermute | solution.py:31
  5.7 2.9 %collective-permute-start.3 = (bf16[2,256,128]{2,1,0:T(8,128)(2,1)S(1)}, bf16[2,256,128]{2,1,0:T(8,128)(2,1)S(1)}, u32[]{:S(2)}, u32[]{:S(2)}) collective-permute-start(bf16[2,256,128]{2,1,0:T(8,128)(2,1)S(1)} %get-tuple-element.36), channel_id=1, source_target_pairs={{0,24},{4,28},{8,0},{12,4},{16,8},{20,12},{24,16},{28,20},{1,25},{... | collective-permute-start | bytes 393224 | tf_op jit(solution)/shard_map/ppermute | solution.py:31
  8.6 3.2 %collective-permute-start.6 = (bf16[2,256,128]{2,1,0:T(8,128)(2,1)S(1)}, bf16[2,256,128]{2,1,0:T(8,128)(2,1)S(1)}, u32[]{:S(2)}, u32[]{:S(2)}) collective-permute-start(bf16[2,256,128]{2,1,0:T(8,128)(2,1)S(1)} %get-tuple-element.38), channel_id=1, source_target_pairs={{0,20},{4,24},{8,28},{12,0},{16,4},{20,8},{24,12},{28,16},{1,21},{... | collective-permute-start | bytes 393224 | tf_op jit(solution)/shard_map/ppermute | solution.py:31
  12.6 2.1 %collective-permute-done.3.refs_4_.refs_7_.refs_6_ = bf16[2,256,128]{2,1,0:T(8,128)(2,1)S(1)} collective-permute-done((bf16[2,256,128]{2,1,0:T(8,128)(2,1)S(1)}, bf16[2,256,128]{2,1,0:T(8,128)(2,1)S(1)}, u32[]{:S(2)}, u32[]{:S(2)}) %collective-permute-start.3) | collective-permute-done | bytes 131104 | tf_op jit(solution)/shard_map/ppermute | solution.py:31
  16.1 3.0 %collective-permute-done.7.refs_2_.refs_5_.refs_4_ = bf16[2,256,128]{2,1,0:T(8,128)(2,1)S(1)} collective-permute-done((bf16[2,256,128]{2,1,0:T(8,128)(2,1)S(1)}, bf16[2,256,128]{2,1,0:T(8,128)(2,1)S(1)}, u32[]{:S(2)}, u32[]{:S(2)}) %collective-permute-start.7) | collective-permute-done | bytes 131104 | tf_op jit(solution)/shard_map/ppermute | solution.py:31
  21.0 3.8 %collective-permute-start.4 = (bf16[10,256,128]{2,1,0:T(8,128)(2,1)S(1)}, bf16[10,256,128]{2,1,0:T(8,128)(2,1)S(1)}, u32[]{:S(2)}, u32[]{:S(2)}) collective-permute-start(bf16[10,256,128]{2,1,0:T(8,128)(2,1)S(1)} %pack.2), channel_id=1, source_target_pairs={{0,32},{32,64},{64,96},{96,128},{128,160},{160,192},{192,224},{1,3... | collective-permute-start | bytes 1966088 | tf_op jit(solution)/shard_map/ppermute | solution.py:31
  24.9 3.0 %collective-permute-start.17 = (f32[136,128]{1,0:T(8,128)S(1)}, f32[136,128]{1,0:T(8,128)S(1)}, u32[]{:S(2)}, u32[]{:S(2)}) collective-permute-start(f32[136,128]{1,0:T(8,128)S(1)} %select_select_fusion), channel_id=1, source_target_pairs={{0,192},{32,224},{64,0},{96,32},{128,64},{160,96},{192,128},{224,1... | collective-permute-start | bytes 208904 | tf_op jit(solution)/shard_map/ppermute | solution.py:31
  27.9 2.9 %collective-permute-start.12 = (bf16[256,128]{1,0:T(8,128)(2,1)S(1)}, bf16[256,128]{1,0:T(8,128)(2,1)S(1)}, u32[]{:S(2)}, u32[]{:S(2)}) collective-permute-start(bf16[256,128]{1,0:T(8,128)(2,1)S(1)} %get-tuple-element.44), channel_id=1, source_target_pairs={{0,16},{4,20},{8,24},{12,28},{16,0},{20,4},{24,8},{28,12},{1,17},{... | collective-permute-start | bytes 196616 | tf_op jit(solution)/shard_map/ppermute | solution.py:31
  30.8 3.0 %collective-permute-start.13 = (bf16[256,128]{1,0:T(8,128)(2,1)S(1)}, bf16[256,128]{1,0:T(8,128)(2,1)S(1)}, u32[]{:S(2)}, u32[]{:S(2)}) collective-permute-start(bf16[256,128]{1,0:T(8,128)(2,1)S(1)} %get-tuple-element.45), channel_id=1, source_target_pairs={{0,20},{4,24},{8,28},{12,0},{16,4},{20,8},{24,12},{28,16},{1,21},{... | collective-permute-start | bytes 196616 | tf_op jit(solution)/shard_map/ppermute | solution.py:31
  36.5 2.2 %collective-permute-start.8 = (bf16[6,256,128]{2,1,0:T(8,128)(2,1)S(1)}, bf16[6,256,128]{2,1,0:T(8,128)(2,1)S(1)}, u32[]{:S(2)}, u32[]{:S(2)}) collective-permute-start(bf16[6,256,128]{2,1,0:T(8,128)(2,1)S(1)} %pack.3), channel_id=1, source_target_pairs={{0,32},{32,64},{64,96},{96,128},{128,160},{160,192},{192,224},{1,3... | collective-permute-start | bytes 1179656 | tf_op jit(solution)/shard_map/ppermute | solution.py:31
  38.7 4.9 %collective-permute-start.18 = (f32[136,128]{1,0:T(8,128)S(1)}, f32[136,128]{1,0:T(8,128)S(1)}, u32[]{:S(2)}, u32[]{:S(2)}) collective-permute-start(f32[136,128]{1,0:T(8,128)S(1)} %get-tuple-element.62), channel_id=1, source_target_pairs={{0,128},{32,160},{64,192},{96,224},{128,0},{160,32},{192,64},{224,... | collective-permute-start | bytes 208904 | tf_op jit(solution)/shard_map/ppermute | solution.py:31
  43.6 5.3 %own.1 = (f32[2048,256]{1,0:T(8,128)S(1)}, f32[2048,128]{1,0:T(8,128)S(1)}, bf16[1024,4096]{1,0:T(8,128)(2,1)S(1)}) custom-call(s32[4]{0:T(128)S(1)} %get-tuple-element.64.refs_0_, bf16[2,256,128]{2,1,0:T(8,128)(2,1)S(1)} %get-tuple-element.32.refs_0_.refs_1_, bf16[2,256,128]{2,1,0:T(8,128)(2,1)S(1)} %collective-permute-done.refs_1_.refs_2_, ...), custom_call_target="tpu_custom_call" | custom-call | flops 2415919104 | bytes 5242880 | tf_op jit(solution)/shard_map/own/pallas_call | solution.py:178
  49.0 5.7 %collective-permute-done.18.refs_15_ = f32[136,128]{1,0:T(8,128)S(1)} collective-permute-done((f32[136,128]{1,0:T(8,128)S(1)}, f32[136,128]{1,0:T(8,128)S(1)}, u32[]{:S(2)}, u32[]{:S(2)}) %collective-permute-start.18) | collective-permute-done | bytes 69664 | tf_op jit(solution)/shard_map/ppermute | solution.py:31
  54.7 5.1 %past.1 = (bf16[256,128]{1,0:T(8,128)(2,1)S(1)}, bf16[256,128]{1,0:T(8,128)(2,1)S(1)}, bf16[256,128]{1,0:T(8,128)(2,1)S(1)}, bf16[256,128]{1,0:T(8,128)(2,1)S(1)...) custom-call(s32[4]{0:T(128)S(1)} %get-tuple-element.64.refs_0_, ...), custom_call_target="tpu_custom_call" | custom-call | flops 2415919104 | bytes 6291456 | tf_op jit(solution)/shard_map/past/pallas_call | solution.py:263
  62.2 3.2 %collective-permute-start.22 = (bf16[256,128]{1,0:T(8,128)(2,1)S(1)}, bf16[256,128]{1,0:T(8,128)(2,1)S(1)}, u32[]{:S(2)}, u32[]{:S(2)}) collective-permute-start(bf16[256,128]{1,0:T(8,128)(2,1)S(1)} %get-tuple-element.54), channel_id=1, source_target_pairs={{0,16},{4,20},{8,24},{12,28},{16,0},{20,4},{24,8},{28,12},{1,17},{... | collective-permute-start | bytes 196616 | tf_op jit(solution)/shard_map/ppermute | solution.py:31
  66.7 2.3 %collective-permute-done.22.refs_5_ = bf16[256,128]{1,0:T(8,128)(2,1)S(1)} collective-permute-done((bf16[256,128]{1,0:T(8,128)(2,1)S(1)}, bf16[256,128]{1,0:T(8,128)(2,1)S(1)}, u32[]{:S(2)}, u32[]{:S(2)}) %collective-permute-start.22) | collective-permute-done | bytes 65568 | tf_op jit(solution)/shard_map/ppermute | solution.py:31
  69.0 1.7 %collective-permute-done.23.refs_6_ = bf16[256,128]{1,0:T(8,128)(2,1)S(1)} collective-permute-done((bf16[256,128]{1,0:T(8,128)(2,1)S(1)}, bf16[256,128]{1,0:T(8,128)(2,1)S(1)}, u32[]{:S(2)}, u32[]{:S(2)}) %collective-permute-start.23) | collective-permute-done | bytes 65568 | tf_op jit(solution)/shard_map/ppermute | solution.py:31
  70.8 1.9 %collective-permute-done.24.refs_7_ = bf16[256,128]{1,0:T(8,128)(2,1)S(1)} collective-permute-done((bf16[256,128]{1,0:T(8,128)(2,1)S(1)}, bf16[256,128]{1,0:T(8,128)(2,1)S(1)}, u32[]{:S(2)}, u32[]{:S(2)}) %collective-permute-start.24) | collective-permute-done | bytes 65568 | tf_op jit(solution)/shard_map/ppermute | solution.py:31
  74.3 3.1 %collective-permute-start.26 = (bf16[256,1024]{1,0:T(8,128)(2,1)S(1)}, bf16[256,1024]{1,0:T(8,128)(2,1)S(1)}, u32[]{:S(2)}, u32[]{:S(2)}) collective-permute-start(bf16[256,1024]{1,0:T(8,128)(2,1)S(1)} %project.4), channel_id=1, source_target_pairs={{0,2},{1,3},{2,0},{3,1},{4,6},{5,7},{6,4},{7,5},{8,10},{9,11},{10,... | collective-permute-start | bytes 1572872 | tf_op jit(solution)/shard_map/ppermute | solution.py:31
  79.5 1.4 %project.6 = bf16[256,1024]{1,0:T(8,128)(2,1)S(1)} custom-call(s32[4]{0:T(128)S(1)} %get-tuple-element.65.refs_0_, bf16[256,128]{1,0:T(8,128)(2,1)S(1)} %get-tuple-element.50.refs_1_, bf16[256,128]{1,0:T(8,128)(2,1)S(1)} %collective-permute-done.19.refs_2_, bf16[256,128]{1,0:T(8,128)(2,1)S(1)} %collective-permute-done.20.refs_3_, ...), custom_call_target="tpu_custom_call" | custom-call | flops 536870912 | bytes 3145728 | tf_op jit(solution)/shard_map/project/pallas_call | solution.py:299
  80.8 2.7 %collective-permute-start.28 = (bf16[256,1024]{1,0:T(8,128)(2,1)S(1)}, bf16[256,1024]{1,0:T(8,128)(2,1)S(1)}, u32[]{:S(2)}, u32[]{:S(2)}) collective-permute-start(bf16[256,1024]{1,0:T(8,128)(2,1)S(1)} %project.6), channel_id=1, source_target_pairs={{0,3},{1,0},{2,1},{3,2},{4,7},{5,4},{6,5},{7,6},{8,11},{9,8},{10,9... | collective-permute-start | bytes 1572872 | tf_op jit(solution)/shard_map/ppermute | solution.py:31
  84.9 5.8 %collective-permute-done.26 = bf16[256,1024]{1,0:T(8,128)(2,1)S(1)} collective-permute-done((bf16[256,1024]{1,0:T(8,128)(2,1)S(1)}, bf16[256,1024]{1,0:T(8,128)(2,1)S(1)}, u32[]{:S(2)}, u32[]{:S(2)}) %collective-permute-start.26) | collective-permute-done | bytes 524320 | tf_op jit(solution)/shard_map/ppermute | solution.py:31
  90.7 9.2 %collective-permute-done.27 = bf16[256,1024]{1,0:T(8,128)(2,1)S(1)} collective-permute-done((bf16[256,1024]{1,0:T(8,128)(2,1)S(1)}, bf16[256,1024]{1,0:T(8,128)(2,1)S(1)}, u32[]{:S(2)}, u32[]{:S(2)}) %collective-permute-start.27) | collective-permute-done | bytes 524320 | tf_op jit(solution)/shard_map/ppermute | solution.py:31
  (51 shorter events, 17.4 us)
Async XLA Ops:
  2.4 6.2 %collective-permute-start = (bf16[2,256,128]{2,1,0:T(8,128)(2,1)S(1)}, bf16[2,256,128]{2,1,0:T(8,128)(2,1)S(1)}, u32[]{:S(2)}, u32[]{:S(2)}) collective-permute-start(bf16[2,256,128]{2,1,0:T(8,128)(2,1)S(1)} %get-tuple-element.33), channel_id=1, source_target_pairs={{0,4},{4,8},{8,12},{12,16},{16,20},{20,24},{24,28},{28,0},{1,5},{5... | collective-permute-start | bytes 393224 | tf_op jit(solution)/shard_map/ppermute | solution.py:31
  2.4 9.4 %collective-permute-start.1 = (bf16[2,256,128]{2,1,0:T(8,128)(2,1)S(1)}, bf16[2,256,128]{2,1,0:T(8,128)(2,1)S(1)}, u32[]{:S(2)}, u32[]{:S(2)}) collective-permute-start(bf16[2,256,128]{2,1,0:T(8,128)(2,1)S(1)} %get-tuple-element.34), channel_id=1, source_target_pairs={{0,28},{4,0},{8,4},{12,8},{16,12},{20,16},{24,20},{28,24},{1,29},{... | collective-permute-start | bytes 393224 | tf_op jit(solution)/shard_map/ppermute | solution.py:31
  5.3 7.3 %collective-permute-start.2 = (bf16[2,256,128]{2,1,0:T(8,128)(2,1)S(1)}, bf16[2,256,128]{2,1,0:T(8,128)(2,1)S(1)}, u32[]{:S(2)}, u32[]{:S(2)}) collective-permute-start(bf16[2,256,128]{2,1,0:T(8,128)(2,1)S(1)} %get-tuple-element.35), channel_id=1, source_target_pairs={{0,8},{4,12},{8,16},{12,20},{16,24},{20,28},{24,0},{28,4},{1,9},{5... | collective-permute-start | bytes 393224 | tf_op jit(solution)/shard_map/ppermute | solution.py:31
  5.7 9.0 %collective-permute-start.3 = (bf16[2,256,128]{2,1,0:T(8,128)(2,1)S(1)}, bf16[2,256,128]{2,1,0:T(8,128)(2,1)S(1)}, u32[]{:S(2)}, u32[]{:S(2)}) collective-permute-start(bf16[2,256,128]{2,1,0:T(8,128)(2,1)S(1)} %get-tuple-element.36), channel_id=1, source_target_pairs={{0,24},{4,28},{8,0},{12,4},{16,8},{20,12},{24,16},{28,20},{1,25},{... | collective-permute-start | bytes 393224 | tf_op jit(solution)/shard_map/ppermute | solution.py:31
  8.6 7.0 %collective-permute-start.5 = (bf16[2,256,128]{2,1,0:T(8,128)(2,1)S(1)}, bf16[2,256,128]{2,1,0:T(8,128)(2,1)S(1)}, u32[]{:S(2)}, u32[]{:S(2)}) collective-permute-start(bf16[2,256,128]{2,1,0:T(8,128)(2,1)S(1)} %get-tuple-element.37), channel_id=1, source_target_pairs={{0,12},{4,16},{8,20},{12,24},{16,28},{20,0},{24,4},{28,8},{1,13},{... | collective-permute-start | bytes 393224 | tf_op jit(solution)/shard_map/ppermute | solution.py:31
  8.6 7.5 %collective-permute-start.6 = (bf16[2,256,128]{2,1,0:T(8,128)(2,1)S(1)}, bf16[2,256,128]{2,1,0:T(8,128)(2,1)S(1)}, u32[]{:S(2)}, u32[]{:S(2)}) collective-permute-start(bf16[2,256,128]{2,1,0:T(8,128)(2,1)S(1)} %get-tuple-element.38), channel_id=1, source_target_pairs={{0,20},{4,24},{8,28},{12,0},{16,4},{20,8},{24,12},{28,16},{1,21},{... | collective-permute-start | bytes 393224 | tf_op jit(solution)/shard_map/ppermute | solution.py:31
  11.8 7.2 %collective-permute-start.7 = (bf16[2,256,128]{2,1,0:T(8,128)(2,1)S(1)}, bf16[2,256,128]{2,1,0:T(8,128)(2,1)S(1)}, u32[]{:S(2)}, u32[]{:S(2)}) collective-permute-start(bf16[2,256,128]{2,1,0:T(8,128)(2,1)S(1)} %get-tuple-element.39), channel_id=1, source_target_pairs={{0,16},{4,20},{8,24},{12,28},{16,0},{20,4},{24,8},{28,12},{1,17},{... | collective-permute-start | bytes 393224 | tf_op jit(solution)/shard_map/ppermute | solution.py:31
  19.7 11.1 %collective-permute-start.10 = (bf16[256,128]{1,0:T(8,128)(2,1)S(1)}, bf16[256,128]{1,0:T(8,128)(2,1)S(1)}, u32[]{:S(2)}, u32[]{:S(2)}) collective-permute-start(bf16[256,128]{1,0:T(8,128)(2,1)S(1)} %get-tuple-element.42), channel_id=1, source_target_pairs={{0,8},{4,12},{8,16},{12,20},{16,24},{20,28},{24,0},{28,4},{1,9},{5... | collective-permute-start | bytes 196616 | tf_op jit(solution)/shard_map/ppermute | solution.py:31
  21.0 33.7 %collective-permute-start.4 = (bf16[10,256,128]{2,1,0:T(8,128)(2,1)S(1)}, bf16[10,256,128]{2,1,0:T(8,128)(2,1)S(1)}, u32[]{:S(2)}, u32[]{:S(2)}) collective-permute-start(bf16[10,256,128]{2,1,0:T(8,128)(2,1)S(1)} %pack.2), channel_id=1, source_target_pairs={{0,32},{32,64},{64,96},{96,128},{128,160},{160,192},{192,224},{1,3... | collective-permute-start | bytes 1966088 | tf_op jit(solution)/shard_map/ppermute | solution.py:31
  24.9 11.6 %collective-permute-start.17 = (f32[136,128]{1,0:T(8,128)S(1)}, f32[136,128]{1,0:T(8,128)S(1)}, u32[]{:S(2)}, u32[]{:S(2)}) collective-permute-start(f32[136,128]{1,0:T(8,128)S(1)} %select_select_fusion), channel_id=1, source_target_pairs={{0,192},{32,224},{64,0},{96,32},{128,64},{160,96},{192,128},{224,1... | collective-permute-start | bytes 208904 | tf_op jit(solution)/shard_map/ppermute | solution.py:31
  27.9 5.9 %collective-permute-start.11 = (bf16[256,128]{1,0:T(8,128)(2,1)S(1)}, bf16[256,128]{1,0:T(8,128)(2,1)S(1)}, u32[]{:S(2)}, u32[]{:S(2)}) collective-permute-start(bf16[256,128]{1,0:T(8,128)(2,1)S(1)} %get-tuple-element.43), channel_id=1, source_target_pairs={{0,12},{4,16},{8,20},{12,24},{16,28},{20,0},{24,4},{28,8},{1,13},{... | collective-permute-start | bytes 196616 | tf_op jit(solution)/shard_map/ppermute | solution.py:31
  27.9 7.3 %collective-permute-start.12 = (bf16[256,128]{1,0:T(8,128)(2,1)S(1)}, bf16[256,128]{1,0:T(8,128)(2,1)S(1)}, u32[]{:S(2)}, u32[]{:S(2)}) collective-permute-start(bf16[256,128]{1,0:T(8,128)(2,1)S(1)} %get-tuple-element.44), channel_id=1, source_target_pairs={{0,16},{4,20},{8,24},{12,28},{16,0},{20,4},{24,8},{28,12},{1,17},{... | collective-permute-start | bytes 196616 | tf_op jit(solution)/shard_map/ppermute | solution.py:31
  35.2 8.5 %collective-permute-start.15 = (bf16[256,128]{1,0:T(8,128)(2,1)S(1)}, bf16[256,128]{1,0:T(8,128)(2,1)S(1)}, u32[]{:S(2)}, u32[]{:S(2)}) collective-permute-start(bf16[256,128]{1,0:T(8,128)(2,1)S(1)} %get-tuple-element.47), channel_id=1, source_target_pairs={{0,28},{4,0},{8,4},{12,8},{16,12},{20,16},{24,20},{28,24},{1,29},{... | collective-permute-start | bytes 196616 | tf_op jit(solution)/shard_map/ppermute | solution.py:31
  36.0 7.6 %collective-permute-start.9 = (bf16[256,128]{1,0:T(8,128)(2,1)S(1)}, bf16[256,128]{1,0:T(8,128)(2,1)S(1)}, u32[]{:S(2)}, u32[]{:S(2)}) collective-permute-start(bf16[256,128]{1,0:T(8,128)(2,1)S(1)} %get-tuple-element.41), channel_id=1, source_target_pairs={{0,4},{4,8},{8,12},{12,16},{16,20},{20,24},{24,28},{28,0},{1,5},{5... | collective-permute-start | bytes 196616 | tf_op jit(solution)/shard_map/ppermute | solution.py:31
  36.5 18.2 %collective-permute-start.8 = (bf16[6,256,128]{2,1,0:T(8,128)(2,1)S(1)}, bf16[6,256,128]{2,1,0:T(8,128)(2,1)S(1)}, u32[]{:S(2)}, u32[]{:S(2)}) collective-permute-start(bf16[6,256,128]{2,1,0:T(8,128)(2,1)S(1)} %pack.3), channel_id=1, source_target_pairs={{0,32},{32,64},{64,96},{96,128},{128,160},{160,192},{192,224},{1,3... | collective-permute-start | bytes 1179656 | tf_op jit(solution)/shard_map/ppermute | solution.py:31
  38.7 16.0 %collective-permute-start.18 = (f32[136,128]{1,0:T(8,128)S(1)}, f32[136,128]{1,0:T(8,128)S(1)}, u32[]{:S(2)}, u32[]{:S(2)}) collective-permute-start(f32[136,128]{1,0:T(8,128)S(1)} %get-tuple-element.62), channel_id=1, source_target_pairs={{0,128},{32,160},{64,192},{96,224},{128,0},{160,32},{192,64},{224,... | collective-permute-start | bytes 208904 | tf_op jit(solution)/shard_map/ppermute | solution.py:31
  59.8 5.6 %collective-permute-start.19 = (bf16[256,128]{1,0:T(8,128)(2,1)S(1)}, bf16[256,128]{1,0:T(8,128)(2,1)S(1)}, u32[]{:S(2)}, u32[]{:S(2)}) collective-permute-start(bf16[256,128]{1,0:T(8,128)(2,1)S(1)} %get-tuple-element.51), channel_id=1, source_target_pairs={{0,28},{4,0},{8,4},{12,8},{16,12},{20,16},{24,20},{28,24},{1,29},{... | collective-permute-start | bytes 196616 | tf_op jit(solution)/shard_map/ppermute | solution.py:31
  62.2 6.8 %collective-permute-start.22 = (bf16[256,128]{1,0:T(8,128)(2,1)S(1)}, bf16[256,128]{1,0:T(8,128)(2,1)S(1)}, u32[]{:S(2)}, u32[]{:S(2)}) collective-permute-start(bf16[256,128]{1,0:T(8,128)(2,1)S(1)} %get-tuple-element.54), channel_id=1, source_target_pairs={{0,16},{4,20},{8,24},{12,28},{16,0},{20,4},{24,8},{28,12},{1,17},{... | collective-permute-start | bytes 196616 | tf_op jit(solution)/shard_map/ppermute | solution.py:31
  65.4 5.4 %collective-permute-start.23 = (bf16[256,128]{1,0:T(8,128)(2,1)S(1)}, bf16[256,128]{1,0:T(8,128)(2,1)S(1)}, u32[]{:S(2)}, u32[]{:S(2)}) collective-permute-start(bf16[256,128]{1,0:T(8,128)(2,1)S(1)} %get-tuple-element.55), channel_id=1, source_target_pairs={{0,12},{4,16},{8,20},{12,24},{16,28},{20,0},{24,4},{28,8},{1,13},{... | collective-permute-start | bytes 196616 | tf_op jit(solution)/shard_map/ppermute | solution.py:31
  65.4 7.3 %collective-permute-start.24 = (bf16[256,128]{1,0:T(8,128)(2,1)S(1)}, bf16[256,128]{1,0:T(8,128)(2,1)S(1)}, u32[]{:S(2)}, u32[]{:S(2)}) collective-permute-start(bf16[256,128]{1,0:T(8,128)(2,1)S(1)} %get-tuple-element.56), channel_id=1, source_target_pairs={{0,8},{4,12},{8,16},{12,20},{16,24},{20,28},{24,0},{28,4},{1,9},{5... | collective-permute-start | bytes 196616 | tf_op jit(solution)/shard_map/ppermute | solution.py:31
  65.7 7.2 %collective-permute-start.25 = (bf16[256,128]{1,0:T(8,128)(2,1)S(1)}, bf16[256,128]{1,0:T(8,128)(2,1)S(1)}, u32[]{:S(2)}, u32[]{:S(2)}) collective-permute-start(bf16[256,128]{1,0:T(8,128)(2,1)S(1)} %get-tuple-element.57), channel_id=1, source_target_pairs={{0,4},{4,8},{8,12},{12,16},{16,20},{20,24},{24,28},{28,0},{1,5},{5... | collective-permute-start | bytes 196616 | tf_op jit(solution)/shard_map/ppermute | solution.py:31
  74.3 16.4 %collective-permute-start.26 = (bf16[256,1024]{1,0:T(8,128)(2,1)S(1)}, bf16[256,1024]{1,0:T(8,128)(2,1)S(1)}, u32[]{:S(2)}, u32[]{:S(2)}) collective-permute-start(bf16[256,1024]{1,0:T(8,128)(2,1)S(1)} %project.4), channel_id=1, source_target_pairs={{0,2},{1,3},{2,0},{3,1},{4,6},{5,7},{6,4},{7,5},{8,10},{9,11},{10,... | collective-permute-start | bytes 1572872 | tf_op jit(solution)/shard_map/ppermute | solution.py:31
  78.8 21.2 %collective-permute-start.27 = (bf16[256,1024]{1,0:T(8,128)(2,1)S(1)}, bf16[256,1024]{1,0:T(8,128)(2,1)S(1)}, u32[]{:S(2)}, u32[]{:S(2)}) collective-permute-start(bf16[256,1024]{1,0:T(8,128)(2,1)S(1)} %project.5), channel_id=1, source_target_pairs={{0,1},{1,2},{2,3},{3,0},{4,5},{5,6},{6,7},{7,4},{8,9},{9,10},{10,1... | collective-permute-start | bytes 1572872 | tf_op jit(solution)/shard_map/ppermute | solution.py:31
  80.8 19.2 %collective-permute-start.28 = (bf16[256,1024]{1,0:T(8,128)(2,1)S(1)}, bf16[256,1024]{1,0:T(8,128)(2,1)S(1)}, u32[]{:S(2)}, u32[]{:S(2)}) collective-permute-start(bf16[256,1024]{1,0:T(8,128)(2,1)S(1)} %project.6), channel_id=1, source_target_pairs={{0,3},{1,0},{2,1},{3,2},{4,7},{5,4},{6,5},{7,6},{8,11},{9,8},{10,9... | collective-permute-start | bytes 1572872 | tf_op jit(solution)/shard_map/ppermute | solution.py:31
  (6 other events, 79.3 us)
where the time goes:
time: 102 us; the launch traced here: 101 us
  starting transfers between devices  47.5 us (47%)
  waiting for transfers between devices  33.6 us (33%)
  Pallas kernels  18.6 us (18%)
  other arithmetic  1.31 us (1%)
    ppermute x29, starting transfers between devices, shifted(): return lax.ppermute(block, axis, route)  47.5 us
    ppermute x29, waiting for transfers between devices, shifted(): return lax.ppermute(block, axis, route)  33.6 us
    pallas_call x4, Pallas kernels, project(): pl.pallas_call(project_kernel, in_specs=[SMEM] + [VMEM] * (1 + NB), out_s...  5.48 us
    pallas_call x1, Pallas kernels, own_part(): pl.pallas_call(own_kernel, out_shape=(jax.ShapeDtypeStruct((rows, 2 * HD)...  5.34 us
    pallas_call x1, Pallas kernels, past_part(): pl.pallas_call(past_kernel, out_shape=[jax.ShapeDtypeStruct((BLK, HD), BF...  5.06 us
    pallas_call x1, Pallas kernels, split_heads(): pl.pallas_call(split_kernel, out_shape=[jax.ShapeDtypeStruct((2, BLK, HD)...  2.21 us
  transfers between devices with their start and end apart: 29, of which 12 were waited for; matrix products, arithmetic and copies ran while one was open for 0% of the time, Pallas kernels for 9%

commit v1 on v0

v1 whole, which is shorter than its diff:
```python
import jax
import jax.numpy as jnp
from jax import lax
from jax.experimental import pallas as pl
from jax.experimental.pallas import tpu as pltpu
from jax.sharding import Mesh
from jax.sharding import PartitionSpec as P


HD = 128
BLK = 256
NB = 8
PLANE = ("seq_1", "seq_2")
SCALE2 = (HD**-0.5) * 1.4426950408889634
F32 = jnp.float32
BF16 = jnp.bfloat16
ANY = pl.BlockSpec(memory_space=pl.ANY)
SMEM = pl.BlockSpec(memory_space=pltpu.SMEM)
VMEM = pl.BlockSpec(memory_space=pltpu.VMEM)
HBM = pl.BlockSpec(memory_space=pltpu.HBM)
NEAR = (0, 1, 7, 2, 6)
FAR = (3, 5, 4)
SPLIT = 6


def shifted(block, axis, distance, wrap=True):
    size = lax.axis_size(axis)
    if wrap:
        route = [(i, (i + distance) % size) for i in range(size)]
    else:
        route = [(i, i + distance) for i in range(size - distance)]
    return lax.ppermute(block, axis, route)


def elu_plus(inputs):
    return jnp.where(inputs > 0, inputs + 1.0, jnp.exp(jnp.minimum(inputs, 0.0)))


def slot_of(here, d):
    return lax.rem(here - d + NB, NB)


def params(flops, nbytes, room=16):
    return dict(
        cost_estimate=pl.CostEstimate(flops=flops, bytes_accessed=nbytes, transcendentals=0),
        compiler_params=pltpu.CompilerParams(vmem_limit_bytes=room * 1024 * 1024),
    )


def place_rows(here, d):
    return pl.ds(pl.multiple_of(slot_of(here, d) * BLK, BLK), BLK)


def split_kernel(*refs):
    here_ref, arrays, pieces = refs[0], refs[1:4], refs[4 : 4 + NB]
    whole, sems = refs[4 + NB :]
    here = here_ref[0]
    copies = [
        pltpu.make_async_copy(array, whole.at[n], sems.at[n]) for n, array in enumerate(arrays)
    ]
    for copy in copies:
        copy.start()
    for n, copy in enumerate(copies):
        copy.wait()
        for d in range(NB):
            cols = pl.ds(pl.multiple_of(lax.rem(here + d, NB) * HD, HD), HD)
            pieces[d][n] = whole[n, :, cols]


def split_heads(here, keys, values, queries):
    return pl.pallas_call(
        split_kernel,
        out_shape=[jax.ShapeDtypeStruct((3, BLK, HD), BF16)] * NB,
        in_specs=[SMEM] + [HBM] * 3,
        out_specs=[VMEM] * NB,
        scratch_shapes=[
            pltpu.VMEM((3, BLK, NB * HD), BF16),
            pltpu.SemaphoreType.DMA((3,)),
        ],
        name="split",
        **params(0, 3 << 20),
    )(here, keys, values, queries)


def pack_kernel(*refs):
    for spot, piece in enumerate(refs[:-1]):
        refs[-1][2 * spot : 2 * spot + 2] = piece[0:2]


def pack(pieces):
    return pl.pallas_call(
        pack_kernel,
        out_shape=jax.ShapeDtypeStruct((2 * len(pieces), BLK, HD), BF16),
        in_specs=[VMEM] * len(pieces),
        out_specs=VMEM,
        name="pack",
        **params(0, 1 << 18),
    )(*pieces)


def terms_kernel(*refs):
    pieces, out = refs[:NB], refs[NB]
    outer = jnp.zeros((HD, HD), F32)
    totals = jnp.zeros((8, HD), F32)
    for d in range(NB):
        soft = elu_plus(pieces[d][0].astype(F32)).astype(BF16)
        outer = outer + lax.dot_general(
            soft, pieces[d][1], (((0,), (0,)), ((), ())), preferred_element_type=F32
        )
        totals = totals + jnp.dot(jnp.ones((8, BLK), BF16), soft, preferred_element_type=F32)
    out[0:HD, :] = outer
    out[HD : HD + 8, :] = totals


def memory_terms(pieces):
    return pl.pallas_call(
        terms_kernel,
        out_shape=jax.ShapeDtypeStruct((HD + 8, HD), F32),
        in_specs=[VMEM] * NB,
        out_specs=VMEM,
        name="terms",
        **params(2 * 2048 * HD * HD, 1 << 20),
    )(*pieces)


def attend(query, keys, values_ones, scores, first, count, mask_at, mask, start_max=None):
    peak = start_max
    for j in range(count):
        rows = pl.ds((first + j) * BLK, BLK)
        part = lax.dot_general(
            query, keys[rows, :], (((1,), (1,)), ((), ())), preferred_element_type=F32
        )
        if j == mask_at:
            part = jnp.where(mask, part, -jnp.inf)
        scores[:, j * BLK : (j + 1) * BLK] = part
        high = jnp.maximum(part[:, :HD], part[:, HD:])
        peak = high if peak is None else jnp.maximum(peak, high)
    peak = jnp.max(peak, axis=1, keepdims=True)
    shift = peak * SCALE2
    acc = None
    for j in range(count):
        rows = pl.ds((first + j) * BLK, BLK)
        weights = jnp.exp2(scores[:, j * BLK : (j + 1) * BLK] * SCALE2 - shift).astype(BF16)
        part = jnp.dot(weights, values_ones[rows, :], preferred_element_type=F32)
        acc = part if acc is None else acc + part
    return acc, peak


def tile_mask():
    row = lax.broadcasted_iota(jnp.int32, (BLK, BLK), 0)
    col = lax.broadcasted_iota(jnp.int32, (BLK, BLK), 1)
    return col <= row


def own_blocks(blocks, query, keys, values, scores, acc_out, peak_out):
    mask = tile_mask()
    for n, b in enumerate(blocks):
        acc, peak = attend(
            query[pl.ds(b * BLK, BLK), :], keys, values, scores[n % 2], 0, b + 1, b, mask
        )
        rows = pl.ds(n * BLK, BLK)
        acc_out[rows, :] = acc
        peak_out[rows, :] = jnp.broadcast_to(peak, (BLK, HD))


def own_first_kernel(*refs):
    here_ref, pieces, weight = refs[0], refs[1 : 1 + NB], refs[1 + NB]
    keys, values, query, acc_out, peak_out, weight_out = refs[2 + NB : 8 + NB]
    scores_a, scores_b, sem = refs[8 + NB :]
    fetch = pltpu.make_async_copy(weight, weight_out, sem)
    fetch.start()
    here = here_ref[0]
    for d in range(NB):
        rows = place_rows(here, d)
        keys[rows, :] = pieces[d][0]
        values[rows, :HD] = pieces[d][1]
        query[rows, :] = pieces[d][2]
    values[:, HD:] = jnp.ones((NB * BLK, HD), BF16)
    own_blocks(range(SPLIT), query, keys, values, (scores_a, scores_b), acc_out, peak_out)
    fetch.wait()


def own_second_kernel(keys, values, query, acc_out, peak_out, scores_a, scores_b):
    own_blocks(range(SPLIT, NB), query, keys, values, (scores_a, scores_b), acc_out, peak_out)


def own_first(here, pieces, weight):
    rows = NB * BLK
    return pl.pallas_call(
        own_first_kernel,
        out_shape=(
            jax.ShapeDtypeStruct((rows, HD), BF16),
            jax.ShapeDtypeStruct((rows, 2 * HD), BF16),
            jax.ShapeDtypeStruct((rows, HD), BF16),
            jax.ShapeDtypeStruct((SPLIT * BLK, 2 * HD), F32),
            jax.ShapeDtypeStruct((SPLIT * BLK, HD), F32),
            jax.ShapeDtypeStruct(weight.shape, BF16),
        ),
        in_specs=[SMEM] + [VMEM] * NB + [HBM],
        out_specs=(VMEM,) * 6,
        scratch_shapes=[
            pltpu.VMEM((BLK, SPLIT * BLK), F32),
            pltpu.VMEM((BLK, SPLIT * BLK), F32),
            pltpu.SemaphoreType.DMA,
        ],
        name="own_first",
        **params(21 * BLK * BLK * HD * 8, 5 << 20),
    )(here, *pieces, weight)


def own_second(keys, values, query):
    rows = NB * BLK
    return pl.pallas_call(
        own_second_kernel,
        out_shape=(
            jax.ShapeDtypeStruct((rows - SPLIT * BLK, 2 * HD), F32),
            jax.ShapeDtypeStruct((rows - SPLIT * BLK, HD), F32),
        ),
        in_specs=[VMEM] * 3,
        out_specs=(VMEM, VMEM),
        scratch_shapes=[pltpu.VMEM((BLK, rows), F32)] * 2,
        name="own_second",
        **params(15 * BLK * BLK * HD * 8, 3 << 20),
    )(keys, values, query)


def prefix_kernel(place_ref, terms, after, chosen, kept):
    segment = place_ref[1]
    whole = terms[...] + after[...]
    wrapped = jnp.where(segment == 7, after[...], 0.0)
    chosen[...] = jnp.where(segment <= 5, whole, wrapped)
    kept[...] = jnp.where(segment <= 3, whole, wrapped)


def prefix_step(place, terms, after):
    shape = jax.ShapeDtypeStruct(terms.shape, F32)
    return pl.pallas_call(
        prefix_kernel,
        out_shape=(shape, shape),
        in_specs=[SMEM, VMEM, VMEM],
        out_specs=(VMEM, VMEM),
        name="prefix",
        **params(0, 1 << 18),
    )(place, terms, after)


def add_kernel(left, right, out):
    out[...] = (left[...] + right[...].astype(F32)).astype(out.dtype)


def added(left, right, dtype):
    return pl.pallas_call(
        add_kernel,
        out_shape=jax.ShapeDtypeStruct(left.shape, dtype),
        in_specs=[VMEM, VMEM],
        out_specs=VMEM,
        name="added",
        **params(0, 1 << 18),
    )(left, right)


def past_kernel(*refs):
    here_ref, beta_ref, near, far, query = refs[:5]
    acc_a, peak_a, acc_b, peak_b, memory_ref, more_ref = refs[5:11]
    outs = refs[11 : 11 + NB]
    keys, values, scores_a, scores_b, result, acc_buf = refs[11 + NB :]
    here, segment = here_ref[0], here_ref[1]

    def own(b):
        if b < SPLIT:
            rows = pl.ds(b * BLK, BLK)
            return acc_a, peak_a, rows
        return acc_b, peak_b, pl.ds((b - SPLIT) * BLK, BLK)

    @pl.when(segment == 0)
    def _():
        acc_buf[: SPLIT * BLK, :] = acc_a[...]
        acc_buf[SPLIT * BLK :, :] = acc_b[...]

    @pl.when(segment > 0)
    def _():
        for d in range(NB):
            rows = place_rows(here, d)
            part, spot = (near, NEAR.index(d)) if d in NEAR else (far, FAR.index(d))
            keys[rows, :] = part[2 * spot]
            values[rows, :HD] = part[2 * spot + 1]
        values[:, HD:] = jnp.ones((NB * BLK, HD), BF16)
        mask = jnp.logical_not(tile_mask())
        for b in range(NB):
            rows = pl.ds(b * BLK, BLK)
            acc_in, peak_in, own_rows = own(b)
            before = peak_in[own_rows, :]
            acc, peak = attend(
                query[rows, :],
                keys,
                values,
                (scores_a, scores_b)[b % 2],
                b,
                NB - b,
                0,
                mask,
                before,
            )
            fade = jnp.exp2((before - peak) * SCALE2)
            acc_buf[rows, :HD] = acc[:, :HD] + acc_in[own_rows, :HD] * fade
            acc_buf[rows, HD:] = acc[:, HD:] + acc_in[own_rows, HD:] * fade

    total = jnp.where(segment <= 3, 0.0, memory_ref[...]) + more_ref[...]
    memory = total[0:HD, :]
    norm = jnp.transpose(jnp.broadcast_to(total[HD : HD + 1, :], (HD, HD)))
    whole = jnp.concatenate([memory, norm], axis=1)
    upper = whole.astype(BF16)
    lower = (whole - upper.astype(F32)).astype(BF16)
    split = jnp.concatenate([upper, lower], axis=0)
    gate = 1.0 / (1.0 + jnp.exp(-jnp.full((1, HD), beta_ref[here], F32)))
    for b in range(NB):
        rows = pl.ds(b * BLK, BLK)
        soft = elu_plus(query[rows, :].astype(F32)).astype(BF16)
        both = jnp.dot(jnp.concatenate([soft, soft], axis=1), split, preferred_element_type=F32)
        from_memory = both[:, :HD] / (1.0 + both[:, HD:])
        local = acc_buf[rows, :HD] / acc_buf[rows, HD:]
        result[rows, :] = (gate * from_memory + (1.0 - gate) * local).astype(BF16)
    for d in range(NB):
        outs[d][...] = result[place_rows(here, d), :]


def past_part(here, beta, kvs, query, own, memory):
    rows = NB * BLK
    return pl.pallas_call(
        past_kernel,
        out_shape=[jax.ShapeDtypeStruct((BLK, HD), BF16)] * NB,
        in_specs=[SMEM, SMEM] + [VMEM] * 9,
        out_specs=[VMEM] * NB,
        scratch_shapes=[
            pltpu.VMEM((rows, HD), BF16),
            pltpu.VMEM((rows, 2 * HD), BF16),
            pltpu.VMEM((BLK, rows), F32),
            pltpu.VMEM((BLK, rows), F32),
            pltpu.VMEM((rows, HD), BF16),
            pltpu.VMEM((rows, 2 * HD), F32),
        ],
        name="past",
        **params(36 * BLK * BLK * HD * 8, 6 << 20),
    )(here, beta, *kvs, query, *own, *memory)


def project_kernel(*refs):
    spot_ref = refs[0]
    pieces, weight = refs[1 : 1 + NB], refs[1 + NB]
    upper, lower = refs[2 + NB : 4 + NB]
    attended = refs[4 + NB]
    for d in range(NB):
        start = pl.multiple_of(lax.rem(spot_ref[0] + d, NB) * HD, HD)
        attended[:, pl.ds(start, HD)] = pieces[d][...]
    width = upper.shape[1]
    cols = pl.ds(pl.multiple_of(lax.rem(spot_ref[2] + spot_ref[3], 4) * width, width), width)
    whole = jnp.dot(attended[...], weight[:, cols], preferred_element_type=F32)
    upper[...] = whole[: BLK // 2].astype(upper.dtype)
    lower[...] = whole[BLK // 2 :].astype(lower.dtype)


def project(place, pieces, weight, upper, lower):
    width = weight.shape[1] // 4
    return pl.pallas_call(
        project_kernel,
        in_specs=[SMEM] + [VMEM] * (1 + NB),
        out_specs=(VMEM, VMEM),
        scratch_shapes=[pltpu.VMEM((BLK, NB * HD), BF16)],
        out_shape=(
            jax.ShapeDtypeStruct((BLK // 2, width), upper),
            jax.ShapeDtypeStruct((BLK // 2, width), lower),
        ),
        name="project",
        **params(2 * BLK * NB * HD * width, 3 << 20),
    )(place, *pieces, weight)


def finish_kernel(own_up, own_low, up_a, up_b, low_a, low_b, out):
    half = BLK // 2
    out[:half] = (own_up[...] + up_a[...].astype(F32) + up_b[...].astype(F32)).astype(BF16)
    out[half:] = (own_low[...] + low_a[...].astype(F32) + low_b[...].astype(F32)).astype(BF16)


def finish(*parts):
    return pl.pallas_call(
        finish_kernel,
        in_specs=[VMEM] * 6,
        out_specs=VMEM,
        out_shape=jax.ShapeDtypeStruct((BLK, parts[0].shape[1]), BF16),
        name="finish",
        **params(0, 3 << 20),
    )(*parts)


def layer(queries, keys, values, beta, w_out):
    here = lax.axis_index(PLANE)
    segment = lax.axis_index("seq_0")
    column = lax.axis_index("head")

    def place(e):
        return jnp.stack((here, segment, column, e)).astype(jnp.int32)

    keys, values, queries, w_out = (
        pltpu.with_memory_space_constraint(part, pltpu.HBM)
        for part in (keys, values, queries, w_out)
    )
    sent = split_heads(place(0), keys, values, queries)
    pieces = {0: sent[0]}
    for d in NEAR[1:] + FAR:
        pieces[d] = shifted(sent[d], PLANE, d)
    kvs_past = []
    for part in (NEAR, FAR):
        kvs_past.append(shifted(pack([pieces[d] for d in part]), "seq_0", 1, wrap=False))
    pieces = [pieces[d] for d in range(NB)]

    terms = memory_terms(pieces)
    after = shifted(terms, "seq_0", -1)
    chosen, kept = prefix_step(place(0), terms, after)
    after = shifted(chosen, "seq_0", -2)
    window = added(kept, after, F32)
    after = shifted(window, "seq_0", -4)

    k_all, v_all, q_all, acc_a, peak_a, weight = own_first(place(0), pieces, w_out)
    acc_b, peak_b = own_second(k_all, v_all, q_all)
    own = (acc_a, peak_a, acc_b, peak_b)
    attended = past_part(place(0), beta, kvs_past, q_all, own, (window, after))
    heads = [attended[0]] + [shifted(attended[d], PLANE, NB - d) for d in range(1, NB)]

    def send(part, distance):
        return shifted(part, "head", distance)

    far_up, far_low = project(place(2), heads, weight, BF16, BF16)
    far_up, far_low = send(far_up, 1), send(far_low, -1)
    right_up, right_low = project(place(1), heads, weight, F32, BF16)
    got_low = send(right_low, 1)
    left_up, left_low = project(place(3), heads, weight, BF16, F32)
    got_up = send(left_up, -1)
    more_up = send(added(right_up, far_up, BF16), 1)
    more_low = send(added(left_low, far_low, BF16), -1)
    own_up, own_low = project(place(0), heads, weight, F32, F32)
    return finish(own_up, own_low, got_up, more_up, got_low, more_low)


def solution(mesh):
    torus = Mesh(
        mesh.devices.reshape(8, 4, 2, mesh.shape["head"]), ("seq_0", "seq_1", "seq_2", "head")
    )
    seq = ("seq_0", "seq_1", "seq_2")
    return jax.shard_map(
        layer,
        mesh=torus,
        in_specs=(P(seq, "head"), P(seq, "head"), P(seq, "head"), P("head"), P("head", None)),
        out_specs=P(seq, "head"),
        check_vma=False,
    )
```

time: 102 us -> 102 us (level)
  starting transfers between devices: 47.5 us -> 37.2 us
  waiting for transfers between devices: 33.6 us -> 42.7 us
  Pallas kernels: 18.6 us -> 21.3 us
  other arithmetic: 1.31 us -> 0.15 us
    ppermute x29 -> x25, starting transfers between devices: 47.5 us -> 37.2 us  [shifted(): return lax.ppermute(block, axis, route)]
    ppermute x29 -> x25, waiting for transfers between devices: 33.6 us -> 42.7 us  [shifted(): return lax.ppermute(block, axis, route)]
    pallas_call x2 -> x8, Pallas kernels: 7.55 us -> 10 us  [the longest x1 4.2 us: own_first(): pl.pallas_call(own_first_kernel, out_shape=(jax.ShapeDtypeStruct((rows, H...]
    convert_element_type x1 -> x0, other arithmetic: 1.12 us -> none  [layer(): return total.astype(BF16)]
  transfers between devices with their start and end apart: 29 -> 25, of which waited for: 12 -> 19; matrix products, arithmetic and copies ran while one was open for 0% -> 0% of each run, Pallas kernels for 9% -> 11%
where the time goes in v1:
time: 102 us
  waiting for transfers between devices  42.7 us (42%)
  starting transfers between devices  37.2 us (36%)
  Pallas kernels  21.3 us (21%)
    ppermute x25, waiting for transfers between devices, shifted(): return lax.ppermute(block, axis, route)  42.7 us
    ppermute x25, starting transfers between devices, shifted(): return lax.ppermute(block, axis, route)  37.2 us
    pallas_call x4, Pallas kernels, project(): pl.pallas_call(project_kernel, in_specs=[SMEM] + [VMEM] * (1 + NB), out_s...  5.54 us
    pallas_call x1, Pallas kernels, past_part(): pl.pallas_call(past_kernel, out_shape=[jax.ShapeDtypeStruct((BLK, HD), BF...  5.17 us
    pallas_call x1, Pallas kernels, own_first(): pl.pallas_call(own_first_kernel, out_shape=(jax.ShapeDtypeStruct((rows, H...  4.2 us
    pallas_call x1, Pallas kernels, own_second(): pl.pallas_call(own_second_kernel, out_shape=(jax.ShapeDtypeStruct((rows -...  2.11 us
    pallas_call x1, Pallas kernels, split_heads(): pl.pallas_call(split_kernel, out_shape=[jax.ShapeDtypeStruct((3, BLK, HD)...  2.06 us
  transfers between devices with their start and end apart: 25, of which 19 were waited for; matrix products, arithmetic and copies ran while one was open for 0% of the time, Pallas kernels for 11%

profile of v1, /device:TPU:64, one launch (start us, length us, event | category | flops | bytes accessed | tf_op | source)
XLA Modules:
  0.0 101.6 jit_solution(15032264310315628578)
XLA Ops:
  2.2 2.9 %collective-permute-start.1 = (bf16[3,256,128]{2,1,0:T(8,128)(2,1)S(1)}, bf16[3,256,128]{2,1,0:T(8,128)(2,1)S(1)}, u32[]{:S(2)}, u32[]{:S(2)}) collective-permute-start(bf16[3,256,128]{2,1,0:T(8,128)(2,1)S(1)} %get-tuple-element.41), channel_id=1, source_target_pairs={{0,28},{4,0},{8,4},{12,8},{16,12},{20,16},{24,20},{28,24},{1,29},{... | collective-permute-start | bytes 589832 | tf_op jit(solution)/shard_map/ppermute | solution.py:32
  5.6 2.9 %collective-permute-start.3 = (bf16[3,256,128]{2,1,0:T(8,128)(2,1)S(1)}, bf16[3,256,128]{2,1,0:T(8,128)(2,1)S(1)}, u32[]{:S(2)}, u32[]{:S(2)}) collective-permute-start(bf16[3,256,128]{2,1,0:T(8,128)(2,1)S(1)} %get-tuple-element.43), channel_id=1, source_target_pairs={{0,24},{4,28},{8,0},{12,4},{16,8},{20,12},{24,16},{28,20},{1,25},{... | collective-permute-start | bytes 589832 | tf_op jit(solution)/shard_map/ppermute | solution.py:32
  9.8 3.0 %collective-permute-done.2.refs_3_.refs_2_ = bf16[3,256,128]{2,1,0:T(8,128)(2,1)S(1)} collective-permute-done((bf16[3,256,128]{2,1,0:T(8,128)(2,1)S(1)}, bf16[3,256,128]{2,1,0:T(8,128)(2,1)S(1)}, u32[]{:S(2)}, u32[]{:S(2)}) %collective-permute-start.2) | collective-permute-done | bytes 196640 | tf_op jit(solution)/shard_map/ppermute | solution.py:32
  13.5 3.8 %collective-permute-start.4 = (bf16[10,256,128]{2,1,0:T(8,128)(2,1)S(1)}, bf16[10,256,128]{2,1,0:T(8,128)(2,1)S(1)}, u32[]{:S(2)}, u32[]{:S(2)}) collective-permute-start(bf16[10,256,128]{2,1,0:T(8,128)(2,1)S(1)} %pack.2), channel_id=1, source_target_pairs={{0,32},{32,64},{64,96},{96,128},{128,160},{160,192},{192,224},{1,3... | collective-permute-start | bytes 1966088 | tf_op jit(solution)/shard_map/ppermute | solution.py:32
  17.4 3.2 %collective-permute-start.6 = (bf16[3,256,128]{2,1,0:T(8,128)(2,1)S(1)}, bf16[3,256,128]{2,1,0:T(8,128)(2,1)S(1)}, u32[]{:S(2)}, u32[]{:S(2)}) collective-permute-start(bf16[3,256,128]{2,1,0:T(8,128)(2,1)S(1)} %get-tuple-element.45), channel_id=1, source_target_pairs={{0,20},{4,24},{8,28},{12,0},{16,4},{20,8},{24,12},{28,16},{1,21},{... | collective-permute-start | bytes 589832 | tf_op jit(solution)/shard_map/ppermute | solution.py:32
  20.6 2.5 %collective-permute-start.7 = (bf16[3,256,128]{2,1,0:T(8,128)(2,1)S(1)}, bf16[3,256,128]{2,1,0:T(8,128)(2,1)S(1)}, u32[]{:S(2)}, u32[]{:S(2)}) collective-permute-start(bf16[3,256,128]{2,1,0:T(8,128)(2,1)S(1)} %get-tuple-element.46), channel_id=1, source_target_pairs={{0,16},{4,20},{8,24},{12,28},{16,0},{20,4},{24,8},{28,12},{1,17},{... | collective-permute-start | bytes 589832 | tf_op jit(solution)/shard_map/ppermute | solution.py:32
  23.1 3.1 %collective-permute-done.5.refs_0_.refs_4_.refs_3_ = bf16[3,256,128]{2,1,0:T(8,128)(2,1)S(1)} collective-permute-done((bf16[3,256,128]{2,1,0:T(8,128)(2,1)S(1)}, bf16[3,256,128]{2,1,0:T(8,128)(2,1)S(1)}, u32[]{:S(2)}, u32[]{:S(2)}) %collective-permute-start.5) | collective-permute-done | bytes 196640 | tf_op jit(solution)/shard_map/ppermute | solution.py:32
  26.2 2.7 %collective-permute-done.6.refs_1_.refs_6_.refs_5_ = bf16[3,256,128]{2,1,0:T(8,128)(2,1)S(1)} collective-permute-done((bf16[3,256,128]{2,1,0:T(8,128)(2,1)S(1)}, bf16[3,256,128]{2,1,0:T(8,128)(2,1)S(1)}, u32[]{:S(2)}, u32[]{:S(2)}) %collective-permute-start.6) | collective-permute-done | bytes 196640 | tf_op jit(solution)/shard_map/ppermute | solution.py:32
  28.9 3.1 %collective-permute-done.7.refs_2_.refs_5_.refs_4_ = bf16[3,256,128]{2,1,0:T(8,128)(2,1)S(1)} collective-permute-done((bf16[3,256,128]{2,1,0:T(8,128)(2,1)S(1)}, bf16[3,256,128]{2,1,0:T(8,128)(2,1)S(1)}, u32[]{:S(2)}, u32[]{:S(2)}) %collective-permute-start.7) | collective-permute-done | bytes 196640 | tf_op jit(solution)/shard_map/ppermute | solution.py:32
  32.1 5.0 %collective-permute-start.8 = (bf16[6,256,128]{2,1,0:T(8,128)(2,1)S(1)}, bf16[6,256,128]{2,1,0:T(8,128)(2,1)S(1)}, u32[]{:S(2)}, u32[]{:S(2)}) collective-permute-start(bf16[6,256,128]{2,1,0:T(8,128)(2,1)S(1)} %pack.3), channel_id=1, source_target_pairs={{0,32},{32,64},{64,96},{96,128},{128,160},{160,192},{192,224},{1,3... | collective-permute-start | bytes 1179656 | tf_op jit(solution)/shard_map/ppermute | solution.py:32
  37.7 4.3 %collective-permute-done.9.after = f32[136,128]{1,0:T(8,128)S(1)} collective-permute-done((f32[136,128]{1,0:T(8,128)S(1)}, f32[136,128]{1,0:T(8,128)S(1)}, u32[]{:S(2)}, u32[]{:S(2)}) %collective-permute-start.9) | collective-permute-done | bytes 69664 | tf_op jit(solution)/shard_map/ppermute | solution.py:32
  42.6 4.2 %own_first.1 = (bf16[2048,128]{1,0:T(8,128)(2,1)S(1)}, bf16[2048,256]{1,0:T(8,128)(2,1)S(1)}, bf16[2048,128]{1,0:T(8,128)(2,1)S(1)}, f32[1536,256]{1,0:T(8,128)S...) custom-call(s32[4]{0:T(128)S(1)} %get-tuple-element.77.refs_0_.place_ref, ...), custom_call_target="tpu_custom_call" | custom-call | flops 1409286144 | bytes 5242880 | tf_op jit(solution)/shard_map/own_first/pallas_call | solution.py:189
  46.8 2.8 %collective-permute-done.10.right = f32[136,128]{1,0:T(8,128)S(1)} collective-permute-done((f32[136,128]{1,0:T(8,128)S(1)}, f32[136,128]{1,0:T(8,128)S(1)}, u32[]{:S(2)}, u32[]{:S(2)}) %collective-permute-start.10) | collective-permute-done | bytes 69664 | tf_op jit(solution)/shard_map/ppermute | solution.py:32
  50.8 2.1 %own_second.1 = (f32[512,256]{1,0:T(8,128)S(1)}, f32[512,128]{1,0:T(8,128)S(1)}) custom-call(bf16[2048,128]{1,0:T(8,128)(2,1)S(1)} %get-tuple-element.50.keys, bf16[2048,256]{1,0:T(8,128)(2,1)S(1)} %get-tuple-element.51.values, bf16[2048,128]{1,0:T(8,128)(2,1)S(1)} %get-tuple-element.47.query.refs_4_), custom_call_target="tpu_custom_call" | custom-call | flops 1006632960 | bytes 3145728 | tf_op jit(solution)/shard_map/own_second/pallas_call | solution.py:213
  53.0 5.0 %collective-permute-done.11.refs_10_ = f32[136,128]{1,0:T(8,128)S(1)} collective-permute-done((f32[136,128]{1,0:T(8,128)S(1)}, f32[136,128]{1,0:T(8,128)S(1)}, u32[]{:S(2)}, u32[]{:S(2)}) %collective-permute-start.11) | collective-permute-done | bytes 69664 | tf_op jit(solution)/shard_map/ppermute | solution.py:32
  58.0 5.2 %past.1 = (bf16[256,128]{1,0:T(8,128)(2,1)S(1)}, bf16[256,128]{1,0:T(8,128)(2,1)S(1)}, bf16[256,128]{1,0:T(8,128)(2,1)S(1)}, bf16[256,128]{1,0:T(8,128)(2,1)S(1)...) custom-call(s32[4]{0:T(128)S(1)} %get-tuple-element.77.refs_0_.place, ...), custom_call_target="tpu_custom_call" | custom-call | flops 2415919104 | bytes 6291456 | tf_op jit(solution)/shard_map/past/pallas_call | solution.py:329
  63.2 2.8 %collective-permute-start.13 = (bf16[256,128]{1,0:T(8,128)(2,1)S(1)}, bf16[256,128]{1,0:T(8,128)(2,1)S(1)}, u32[]{:S(2)}, u32[]{:S(2)}) collective-permute-start(bf16[256,128]{1,0:T(8,128)(2,1)S(1)} %get-tuple-element.58), channel_id=1, source_target_pairs={{0,24},{4,28},{8,0},{12,4},{16,8},{20,12},{24,16},{28,20},{1,25},{... | collective-permute-start | bytes 196616 | tf_op jit(solution)/shard_map/ppermute | solution.py:32
  66.5 2.8 %collective-permute-start.15 = (bf16[256,128]{1,0:T(8,128)(2,1)S(1)}, bf16[256,128]{1,0:T(8,128)(2,1)S(1)}, u32[]{:S(2)}, u32[]{:S(2)}) collective-permute-start(bf16[256,128]{1,0:T(8,128)(2,1)S(1)} %get-tuple-element.60), channel_id=1, source_target_pairs={{0,16},{4,20},{8,24},{12,28},{16,0},{20,4},{24,8},{28,12},{1,17},{... | collective-permute-start | bytes 196616 | tf_op jit(solution)/shard_map/ppermute | solution.py:32
  72.4 2.7 %collective-permute-done.16.refs_6_ = bf16[256,128]{1,0:T(8,128)(2,1)S(1)} collective-permute-done((bf16[256,128]{1,0:T(8,128)(2,1)S(1)}, bf16[256,128]{1,0:T(8,128)(2,1)S(1)}, u32[]{:S(2)}, u32[]{:S(2)}) %collective-permute-start.16) | collective-permute-done | bytes 65568 | tf_op jit(solution)/shard_map/ppermute | solution.py:32
  78.0 2.8 %collective-permute-start.23 = (bf16[128,1024]{1,0:T(8,128)(2,1)S(1)}, bf16[128,1024]{1,0:T(8,128)(2,1)S(1)}, u32[]{:S(2)}, u32[]{:S(2)}) collective-permute-start(bf16[128,1024]{1,0:T(8,128)(2,1)S(1)} %get-tuple-element.72), channel_id=1, source_target_pairs={{0,3},{1,0},{2,1},{3,2},{4,7},{5,4},{6,5},{7,6},{8,11},{9,8},{10,9... | collective-permute-start | bytes 786440 | tf_op jit(solution)/shard_map/ppermute | solution.py:32
  84.5 2.6 %collective-permute-start.19 = (bf16[128,1024]{1,0:T(8,128)(2,1)S(1)}, bf16[128,1024]{1,0:T(8,128)(2,1)S(1)}, u32[]{:S(2)}, u32[]{:S(2)}) collective-permute-start(bf16[128,1024]{1,0:T(8,128)(2,1)S(1)} %get-tuple-element.67), channel_id=1, source_target_pairs={{0,3},{1,0},{2,1},{3,2},{4,7},{5,4},{6,5},{7,6},{8,11},{9,8},{10,9... | collective-permute-start | bytes 786440 | tf_op jit(solution)/shard_map/ppermute | solution.py:32
  87.1 2.7 %collective-permute-start.24 = (bf16[128,1024]{1,0:T(8,128)(2,1)S(1)}, bf16[128,1024]{1,0:T(8,128)(2,1)S(1)}, u32[]{:S(2)}, u32[]{:S(2)}) collective-permute-start(bf16[128,1024]{1,0:T(8,128)(2,1)S(1)} %added.5), channel_id=1, source_target_pairs={{0,3},{1,0},{2,1},{3,2},{4,7},{5,4},{6,5},{7,6},{8,11},{9,8},{10,9... | collective-permute-start | bytes 786440 | tf_op jit(solution)/shard_map/ppermute | solution.py:32
  92.8 4.1 %collective-permute-done.22.low_a = bf16[128,1024]{1,0:T(8,128)(2,1)S(1)} collective-permute-done((bf16[128,1024]{1,0:T(8,128)(2,1)S(1)}, bf16[128,1024]{1,0:T(8,128)(2,1)S(1)}, u32[]{:S(2)}, u32[]{:S(2)}) %collective-permute-start.22) | collective-permute-done | bytes 262176 | tf_op jit(solution)/shard_map/ppermute | solution.py:32
  97.2 3.4 %collective-permute-done.21.up_b = bf16[128,1024]{1,0:T(8,128)(2,1)S(1)} collective-permute-done((bf16[128,1024]{1,0:T(8,128)(2,1)S(1)}, bf16[128,1024]{1,0:T(8,128)(2,1)S(1)}, u32[]{:S(2)}, u32[]{:S(2)}) %collective-permute-start.21) | collective-permute-done | bytes 262176 | tf_op jit(solution)/shard_map/ppermute | solution.py:32
  (46 shorter events, 21.7 us)
Async XLA Ops:
  2.2 6.3 %collective-permute-start = (bf16[3,256,128]{2,1,0:T(8,128)(2,1)S(1)}, bf16[3,256,128]{2,1,0:T(8,128)(2,1)S(1)}, u32[]{:S(2)}, u32[]{:S(2)}) collective-permute-start(bf16[3,256,128]{2,1,0:T(8,128)(2,1)S(1)} %get-tuple-element.40), channel_id=1, source_target_pairs={{0,4},{4,8},{8,12},{12,16},{16,20},{20,24},{24,28},{28,0},{1,5},{5... | collective-permute-start | bytes 589832 | tf_op jit(solution)/shard_map/ppermute | solution.py:32
  2.2 7.5 %collective-permute-start.1 = (bf16[3,256,128]{2,1,0:T(8,128)(2,1)S(1)}, bf16[3,256,128]{2,1,0:T(8,128)(2,1)S(1)}, u32[]{:S(2)}, u32[]{:S(2)}) collective-permute-start(bf16[3,256,128]{2,1,0:T(8,128)(2,1)S(1)} %get-tuple-element.41), channel_id=1, source_target_pairs={{0,28},{4,0},{8,4},{12,8},{16,12},{20,16},{24,20},{28,24},{1,29},{... | collective-permute-start | bytes 589832 | tf_op jit(solution)/shard_map/ppermute | solution.py:32
  5.2 7.6 %collective-permute-start.2 = (bf16[3,256,128]{2,1,0:T(8,128)(2,1)S(1)}, bf16[3,256,128]{2,1,0:T(8,128)(2,1)S(1)}, u32[]{:S(2)}, u32[]{:S(2)}) collective-permute-start(bf16[3,256,128]{2,1,0:T(8,128)(2,1)S(1)} %get-tuple-element.42), channel_id=1, source_target_pairs={{0,8},{4,12},{8,16},{12,20},{16,24},{20,28},{24,0},{28,4},{1,9},{5... | collective-permute-start | bytes 589832 | tf_op jit(solution)/shard_map/ppermute | solution.py:32
  5.6 7.9 %collective-permute-start.3 = (bf16[3,256,128]{2,1,0:T(8,128)(2,1)S(1)}, bf16[3,256,128]{2,1,0:T(8,128)(2,1)S(1)}, u32[]{:S(2)}, u32[]{:S(2)}) collective-permute-start(bf16[3,256,128]{2,1,0:T(8,128)(2,1)S(1)} %get-tuple-element.43), channel_id=1, source_target_pairs={{0,24},{4,28},{8,0},{12,4},{16,8},{20,12},{24,16},{28,20},{1,25},{... | collective-permute-start | bytes 589832 | tf_op jit(solution)/shard_map/ppermute | solution.py:32
  13.5 44.5 %collective-permute-start.4 = (bf16[10,256,128]{2,1,0:T(8,128)(2,1)S(1)}, bf16[10,256,128]{2,1,0:T(8,128)(2,1)S(1)}, u32[]{:S(2)}, u32[]{:S(2)}) collective-permute-start(bf16[10,256,128]{2,1,0:T(8,128)(2,1)S(1)} %pack.2), channel_id=1, source_target_pairs={{0,32},{32,64},{64,96},{96,128},{128,160},{160,192},{192,224},{1,3... | collective-permute-start | bytes 1966088 | tf_op jit(solution)/shard_map/ppermute | solution.py:32
  17.3 8.9 %collective-permute-start.5 = (bf16[3,256,128]{2,1,0:T(8,128)(2,1)S(1)}, bf16[3,256,128]{2,1,0:T(8,128)(2,1)S(1)}, u32[]{:S(2)}, u32[]{:S(2)}) collective-permute-start(bf16[3,256,128]{2,1,0:T(8,128)(2,1)S(1)} %get-tuple-element.44), channel_id=1, source_target_pairs={{0,12},{4,16},{8,20},{12,24},{16,28},{20,0},{24,4},{28,8},{1,13},{... | collective-permute-start | bytes 589832 | tf_op jit(solution)/shard_map/ppermute | solution.py:32
  17.4 11.5 %collective-permute-start.6 = (bf16[3,256,128]{2,1,0:T(8,128)(2,1)S(1)}, bf16[3,256,128]{2,1,0:T(8,128)(2,1)S(1)}, u32[]{:S(2)}, u32[]{:S(2)}) collective-permute-start(bf16[3,256,128]{2,1,0:T(8,128)(2,1)S(1)} %get-tuple-element.45), channel_id=1, source_target_pairs={{0,20},{4,24},{8,28},{12,0},{16,4},{20,8},{24,12},{28,16},{1,21},{... | collective-permute-start | bytes 589832 | tf_op jit(solution)/shard_map/ppermute | solution.py:32
  20.6 11.4 %collective-permute-start.7 = (bf16[3,256,128]{2,1,0:T(8,128)(2,1)S(1)}, bf16[3,256,128]{2,1,0:T(8,128)(2,1)S(1)}, u32[]{:S(2)}, u32[]{:S(2)}) collective-permute-start(bf16[3,256,128]{2,1,0:T(8,128)(2,1)S(1)} %get-tuple-element.46), channel_id=1, source_target_pairs={{0,16},{4,20},{8,24},{12,28},{16,0},{20,4},{24,8},{28,12},{1,17},{... | collective-permute-start | bytes 589832 | tf_op jit(solution)/shard_map/ppermute | solution.py:32
  32.1 25.9 %collective-permute-start.8 = (bf16[6,256,128]{2,1,0:T(8,128)(2,1)S(1)}, bf16[6,256,128]{2,1,0:T(8,128)(2,1)S(1)}, u32[]{:S(2)}, u32[]{:S(2)}) collective-permute-start(bf16[6,256,128]{2,1,0:T(8,128)(2,1)S(1)} %pack.3), channel_id=1, source_target_pairs={{0,32},{32,64},{64,96},{96,128},{128,160},{160,192},{192,224},{1,3... | collective-permute-start | bytes 1179656 | tf_op jit(solution)/shard_map/ppermute | solution.py:32
  42.5 7.1 %collective-permute-start.10 = (f32[136,128]{1,0:T(8,128)S(1)}, f32[136,128]{1,0:T(8,128)S(1)}, u32[]{:S(2)}, u32[]{:S(2)}) collective-permute-start(f32[136,128]{1,0:T(8,128)S(1)} %get-tuple-element.55), channel_id=1, source_target_pairs={{0,192},{32,224},{64,0},{96,32},{128,64},{160,96},{192,128},{224,1... | collective-permute-start | bytes 208904 | tf_op jit(solution)/shard_map/ppermute | solution.py:32
  49.7 8.3 %collective-permute-start.11 = (f32[136,128]{1,0:T(8,128)S(1)}, f32[136,128]{1,0:T(8,128)S(1)}, u32[]{:S(2)}, u32[]{:S(2)}) collective-permute-start(f32[136,128]{1,0:T(8,128)S(1)} %added.3.refs_9_), channel_id=1, source_target_pairs={{0,128},{32,160},{64,192},{96,224},{128,0},{160,32},{192,64},{224,... | collective-permute-start | bytes 208904 | tf_op jit(solution)/shard_map/ppermute | solution.py:32
  63.2 6.1 %collective-permute-start.12 = (bf16[256,128]{1,0:T(8,128)(2,1)S(1)}, bf16[256,128]{1,0:T(8,128)(2,1)S(1)}, u32[]{:S(2)}, u32[]{:S(2)}) collective-permute-start(bf16[256,128]{1,0:T(8,128)(2,1)S(1)} %get-tuple-element.57), channel_id=1, source_target_pairs={{0,28},{4,0},{8,4},{12,8},{16,12},{20,16},{24,20},{28,24},{1,29},{... | collective-permute-start | bytes 196616 | tf_op jit(solution)/shard_map/ppermute | solution.py:32
  63.2 7.2 %collective-permute-start.13 = (bf16[256,128]{1,0:T(8,128)(2,1)S(1)}, bf16[256,128]{1,0:T(8,128)(2,1)S(1)}, u32[]{:S(2)}, u32[]{:S(2)}) collective-permute-start(bf16[256,128]{1,0:T(8,128)(2,1)S(1)} %get-tuple-element.58), channel_id=1, source_target_pairs={{0,24},{4,28},{8,0},{12,4},{16,8},{20,12},{24,16},{28,20},{1,25},{... | collective-permute-start | bytes 196616 | tf_op jit(solution)/shard_map/ppermute | solution.py:32
  66.0 4.5 %collective-permute-start.14 = (bf16[256,128]{1,0:T(8,128)(2,1)S(1)}, bf16[256,128]{1,0:T(8,128)(2,1)S(1)}, u32[]{:S(2)}, u32[]{:S(2)}) collective-permute-start(bf16[256,128]{1,0:T(8,128)(2,1)S(1)} %get-tuple-element.59), channel_id=1, source_target_pairs={{0,20},{4,24},{8,28},{12,0},{16,4},{20,8},{24,12},{28,16},{1,21},{... | collective-permute-start | bytes 196616 | tf_op jit(solution)/shard_map/ppermute | solution.py:32
  66.5 6.0 %collective-permute-start.15 = (bf16[256,128]{1,0:T(8,128)(2,1)S(1)}, bf16[256,128]{1,0:T(8,128)(2,1)S(1)}, u32[]{:S(2)}, u32[]{:S(2)}) collective-permute-start(bf16[256,128]{1,0:T(8,128)(2,1)S(1)} %get-tuple-element.60), channel_id=1, source_target_pairs={{0,16},{4,20},{8,24},{12,28},{16,0},{20,4},{24,8},{28,12},{1,17},{... | collective-permute-start | bytes 196616 | tf_op jit(solution)/shard_map/ppermute | solution.py:32
  69.2 5.9 %collective-permute-start.16 = (bf16[256,128]{1,0:T(8,128)(2,1)S(1)}, bf16[256,128]{1,0:T(8,128)(2,1)S(1)}, u32[]{:S(2)}, u32[]{:S(2)}) collective-permute-start(bf16[256,128]{1,0:T(8,128)(2,1)S(1)} %get-tuple-element.61), channel_id=1, source_target_pairs={{0,12},{4,16},{8,20},{12,24},{16,28},{20,0},{24,4},{28,8},{1,13},{... | collective-permute-start | bytes 196616 | tf_op jit(solution)/shard_map/ppermute | solution.py:32
  69.2 6.7 %collective-permute-start.17 = (bf16[256,128]{1,0:T(8,128)(2,1)S(1)}, bf16[256,128]{1,0:T(8,128)(2,1)S(1)}, u32[]{:S(2)}, u32[]{:S(2)}) collective-permute-start(bf16[256,128]{1,0:T(8,128)(2,1)S(1)} %get-tuple-element.62), channel_id=1, source_target_pairs={{0,8},{4,12},{8,16},{12,20},{16,24},{20,28},{24,0},{28,4},{1,9},{5... | collective-permute-start | bytes 196616 | tf_op jit(solution)/shard_map/ppermute | solution.py:32
  70.4 6.2 %collective-permute-start.18 = (bf16[256,128]{1,0:T(8,128)(2,1)S(1)}, bf16[256,128]{1,0:T(8,128)(2,1)S(1)}, u32[]{:S(2)}, u32[]{:S(2)}) collective-permute-start(bf16[256,128]{1,0:T(8,128)(2,1)S(1)} %get-tuple-element.63), channel_id=1, source_target_pairs={{0,4},{4,8},{8,12},{12,16},{16,20},{20,24},{24,28},{28,0},{1,5},{5... | collective-permute-start | bytes 196616 | tf_op jit(solution)/shard_map/ppermute | solution.py:32
  78.0 9.0 %collective-permute-start.23 = (bf16[128,1024]{1,0:T(8,128)(2,1)S(1)}, bf16[128,1024]{1,0:T(8,128)(2,1)S(1)}, u32[]{:S(2)}, u32[]{:S(2)}) collective-permute-start(bf16[128,1024]{1,0:T(8,128)(2,1)S(1)} %get-tuple-element.72), channel_id=1, source_target_pairs={{0,3},{1,0},{2,1},{3,2},{4,7},{5,4},{6,5},{7,6},{8,11},{9,8},{10,9... | collective-permute-start | bytes 786440 | tf_op jit(solution)/shard_map/ppermute | solution.py:32
  80.9 10.4 %collective-permute-start.20 = (bf16[128,1024]{1,0:T(8,128)(2,1)S(1)}, bf16[128,1024]{1,0:T(8,128)(2,1)S(1)}, u32[]{:S(2)}, u32[]{:S(2)}) collective-permute-start(bf16[128,1024]{1,0:T(8,128)(2,1)S(1)} %get-tuple-element.69), channel_id=1, source_target_pairs={{0,1},{1,2},{2,3},{3,0},{4,5},{5,6},{6,7},{7,4},{8,9},{9,10},{10,1... | collective-permute-start | bytes 786440 | tf_op jit(solution)/shard_map/ppermute | solution.py:32
  82.3 14.6 %collective-permute-start.22 = (bf16[128,1024]{1,0:T(8,128)(2,1)S(1)}, bf16[128,1024]{1,0:T(8,128)(2,1)S(1)}, u32[]{:S(2)}, u32[]{:S(2)}) collective-permute-start(bf16[128,1024]{1,0:T(8,128)(2,1)S(1)} %get-tuple-element.70), channel_id=1, source_target_pairs={{0,1},{1,2},{2,3},{3,0},{4,5},{5,6},{6,7},{7,4},{8,9},{9,10},{10,1... | collective-permute-start | bytes 786440 | tf_op jit(solution)/shard_map/ppermute | solution.py:32
  84.5 12.4 %collective-permute-start.19 = (bf16[128,1024]{1,0:T(8,128)(2,1)S(1)}, bf16[128,1024]{1,0:T(8,128)(2,1)S(1)}, u32[]{:S(2)}, u32[]{:S(2)}) collective-permute-start(bf16[128,1024]{1,0:T(8,128)(2,1)S(1)} %get-tuple-element.67), channel_id=1, source_target_pairs={{0,3},{1,0},{2,1},{3,2},{4,7},{5,4},{6,5},{7,6},{8,11},{9,8},{10,9... | collective-permute-start | bytes 786440 | tf_op jit(solution)/shard_map/ppermute | solution.py:32
  87.1 10.1 %collective-permute-start.24 = (bf16[128,1024]{1,0:T(8,128)(2,1)S(1)}, bf16[128,1024]{1,0:T(8,128)(2,1)S(1)}, u32[]{:S(2)}, u32[]{:S(2)}) collective-permute-start(bf16[128,1024]{1,0:T(8,128)(2,1)S(1)} %added.5), channel_id=1, source_target_pairs={{0,3},{1,0},{2,1},{3,2},{4,7},{5,4},{6,5},{7,6},{8,11},{9,8},{10,9... | collective-permute-start | bytes 786440 | tf_op jit(solution)/shard_map/ppermute | solution.py:32
  91.3 9.3 %collective-permute-start.21 = (bf16[128,1024]{1,0:T(8,128)(2,1)S(1)}, bf16[128,1024]{1,0:T(8,128)(2,1)S(1)}, u32[]{:S(2)}, u32[]{:S(2)}) collective-permute-start(bf16[128,1024]{1,0:T(8,128)(2,1)S(1)} %added.4), channel_id=1, source_target_pairs={{0,1},{1,2},{2,3},{3,0},{4,5},{5,6},{6,7},{7,4},{8,9},{9,10},{10,1... | collective-permute-start | bytes 786440 | tf_op jit(solution)/shard_map/ppermute | solution.py:32
  (2 other events, 48.9 us)

commit v2 on v1

--- a/solution.py
+++ b/solution.py
@@ -18,8 +18,10 @@
 SMEM = pl.BlockSpec(memory_space=pltpu.SMEM)
 VMEM = pl.BlockSpec(memory_space=pltpu.VMEM)
 HBM = pl.BlockSpec(memory_space=pltpu.HBM)
-NEAR = (0, 1, 7, 2, 6)
-FAR = (3, 5, 4)
+NY = 4
+PAIR = 2 * BLK
+STEPS = (1, 3, 2)
+LEAVE = (4, 3, 5, 2, 6, 1, 7)
 SPLIT = 6
 
 
@@ -40,6 +42,11 @@
     return lax.rem(here - d + NB, NB)
 
 
+def pair_rows(here, step, half):
+    row = lax.rem(here // 2 - step + NY, NY) * PAIR + half * BLK
+    return pl.ds(pl.multiple_of(row, BLK), BLK)
+
+
 def params(flops, nbytes, room=16):
     return dict(
         cost_estimate=pl.CostEstimate(flops=flops, bytes_accessed=nbytes, transcendentals=0),
@@ -51,28 +58,31 @@
     return pl.ds(pl.multiple_of(slot_of(here, d) * BLK, BLK), BLK)
 
 
-def split_kernel(*refs):
-    here_ref, arrays, pieces = refs[0], refs[1:4], refs[4 : 4 + NB]
-    whole, sems = refs[4 + NB :]
+def split_kernel(here_ref, keys, values, queries, stay, leave, whole, sems):
     here = here_ref[0]
     copies = [
-        pltpu.make_async_copy(array, whole.at[n], sems.at[n]) for n, array in enumerate(arrays)
+        pltpu.make_async_copy(array, whole.at[n], sems.at[n])
+        for n, array in enumerate((keys, values, queries))
     ]
     for copy in copies:
         copy.start()
+    own_core = lax.rem(here, 2)
     for n, copy in enumerate(copies):
         copy.wait()
-        for d in range(NB):
-            cols = pl.ds(pl.multiple_of(lax.rem(here + d, NB) * HD, HD), HD)
-            pieces[d][n] = whole[n, :, cols]
+        for step in range(NY):
+            pair = lax.rem(here // 2 + step, NY) * 2
+            for out, core in ((leave, 1 - own_core), (stay, own_core)):
+                cols = pl.ds(pl.multiple_of((pair + core) * HD, HD), HD)
+                out[step, n] = whole[n, :, cols]
 
 
 def split_heads(here, keys, values, queries):
+    half = jax.ShapeDtypeStruct((NY, 3, BLK, HD), BF16)
     return pl.pallas_call(
         split_kernel,
-        out_shape=[jax.ShapeDtypeStruct((3, BLK, HD), BF16)] * NB,
+        out_shape=(half, half),
         in_specs=[SMEM] + [HBM] * 3,
-        out_specs=[VMEM] * NB,
+        out_specs=(VMEM, VMEM),
         scratch_shapes=[
             pltpu.VMEM((3, BLK, NB * HD), BF16),
             pltpu.SemaphoreType.DMA((3,)),
@@ -82,42 +92,71 @@
     )(here, keys, values, queries)
 
 
-def pack_kernel(*refs):
-    for spot, piece in enumerate(refs[:-1]):
-        refs[-1][2 * spot : 2 * spot + 2] = piece[0:2]
-
-
-def pack(pieces):
+def pair_kernel(*refs):
+    here_ref, stay, got = refs[:3]
+    kvs, qs = refs[3 : 3 + NY], refs[3 + NY : 3 + 2 * NY]
+    core = lax.rem(here_ref[0], 2)
+    for step in range(NY):
+        for part, half in ((stay, core), (got, 1 - core)):
+            kvs[step][half] = part[step, 0:2]
+            qs[step][half] = part[step, 2]
+
+
+def pair_up(here, stay, got):
+    out = pl.pallas_call(
+        pair_kernel,
+        out_shape=[jax.ShapeDtypeStruct((2, 2, BLK, HD), BF16)] * NY
+        + [jax.ShapeDtypeStruct((2, BLK, HD), BF16)] * NY,
+        in_specs=[SMEM, VMEM, VMEM],
+        out_specs=[VMEM] * (2 * NY),
+        name="pair_up",
+        **params(0, 3 << 20),
+    )(here, stay, got)
+    return out[:NY], out[NY:]
+
+
+def pack_kernel(first, second, out):
+    out[0] = first[...]
+    out[1] = second[...]
+
+
+def pack(first, second):
     return pl.pallas_call(
         pack_kernel,
-        out_shape=jax.ShapeDtypeStruct((2 * len(pieces), BLK, HD), BF16),
-        in_specs=[VMEM] * len(pieces),
+        out_shape=jax.ShapeDtypeStruct((2, *first.shape), BF16),
+        in_specs=[VMEM, VMEM],
         out_specs=VMEM,
         name="pack",
-        **params(0, 1 << 18),
-    )(*pieces)
+        **params(0, 1 << 20),
+    )(first, second)
 
 
 def terms_kernel(*refs):
-    pieces, out = refs[:NB], refs[NB]
+    pieces, out, wire = refs[:NY], refs[NY], refs[NY + 1]
     outer = jnp.zeros((HD, HD), F32)
     totals = jnp.zeros((8, HD), F32)
-    for d in range(NB):
-        soft = elu_plus(pieces[d][0].astype(F32)).astype(BF16)
-        outer = outer + lax.dot_general(
-            soft, pieces[d][1], (((0,), (0,)), ((), ())), preferred_element_type=F32
-        )
-        totals = totals + jnp.dot(jnp.ones((8, BLK), BF16), soft, preferred_element_type=F32)
+    for piece in pieces:
+        for half in range(2):
+            soft = elu_plus(piece[half, 0].astype(F32)).astype(BF16)
+            outer = outer + lax.dot_general(
+                soft, piece[half, 1], (((0,), (0,)), ((), ())), preferred_element_type=F32
+            )
+            totals = totals + jnp.dot(jnp.ones((8, BLK), BF16), soft, preferred_element_type=F32)
     out[0:HD, :] = outer
     out[HD : HD + 8, :] = totals
+    wire[0:HD, :] = outer.astype(BF16)
+    wire[HD : HD + 8, :] = totals.astype(BF16)
 
 
 def memory_terms(pieces):
     return pl.pallas_call(
         terms_kernel,
-        out_shape=jax.ShapeDtypeStruct((HD + 8, HD), F32),
-        in_specs=[VMEM] * NB,
-        out_specs=VMEM,
+        out_shape=(
+            jax.ShapeDtypeStruct((HD + 8, HD), F32),
+            jax.ShapeDtypeStruct((HD + 8, HD), BF16),
+        ),
+        in_specs=[VMEM] * NY,
+        out_specs=(VMEM, VMEM),
         name="terms",
         **params(2 * 2048 * HD * HD, 1 << 20),
     )(*pieces)
@@ -164,17 +203,18 @@
 
 
 def own_first_kernel(*refs):
-    here_ref, pieces, weight = refs[0], refs[1 : 1 + NB], refs[1 + NB]
-    keys, values, query, acc_out, peak_out, weight_out = refs[2 + NB : 8 + NB]
-    scores_a, scores_b, sem = refs[8 + NB :]
+    here_ref, kvs, qs = refs[0], refs[1 : 1 + NY], refs[1 + NY : 1 + 2 * NY]
+    weight, keys, values, query, acc_out, peak_out, weight_out = refs[1 + 2 * NY : 8 + 2 * NY]
+    scores_a, scores_b, sem = refs[8 + 2 * NY :]
     fetch = pltpu.make_async_copy(weight, weight_out, sem)
     fetch.start()
     here = here_ref[0]
-    for d in range(NB):
-        rows = place_rows(here, d)
-        keys[rows, :] = pieces[d][0]
-        values[rows, :HD] = pieces[d][1]
-        query[rows, :] = pieces[d][2]
+    for step in range(NY):
+        for half in range(2):
+            rows = pair_rows(here, step, half)
+            keys[rows, :] = kvs[step][half, 0]
+            values[rows, :HD] = kvs[step][half, 1]
+            query[rows, :] = qs[step][half]
     values[:, HD:] = jnp.ones((NB * BLK, HD), BF16)
     own_blocks(range(SPLIT), query, keys, values, (scores_a, scores_b), acc_out, peak_out)
     fetch.wait()
@@ -184,7 +224,7 @@
     own_blocks(range(SPLIT, NB), query, keys, values, (scores_a, scores_b), acc_out, peak_out)
 
 
-def own_first(here, pieces, weight):
+def own_first(here, kvs, qs, weight):
     rows = NB * BLK
     return pl.pallas_call(
         own_first_kernel,
@@ -196,7 +236,7 @@
             jax.ShapeDtypeStruct((SPLIT * BLK, HD), F32),
             jax.ShapeDtypeStruct(weight.shape, BF16),
         ),
-        in_specs=[SMEM] + [VMEM] * NB + [HBM],
+        in_specs=[SMEM] + [VMEM] * (2 * NY) + [HBM],
         out_specs=(VMEM,) * 6,
         scratch_shapes=[
             pltpu.VMEM((BLK, SPLIT * BLK), F32),
@@ -205,7 +245,7 @@
         ],
         name="own_first",
         **params(21 * BLK * BLK * HD * 8, 5 << 20),
-    )(here, *pieces, weight)
+    )(here, *kvs, *qs, weight)
 
 
 def own_second(keys, values, query):
@@ -226,9 +266,10 @@
 
 def prefix_kernel(place_ref, terms, after, chosen, kept):
     segment = place_ref[1]
-    whole = terms[...] + after[...]
-    wrapped = jnp.where(segment == 7, after[...], 0.0)
-    chosen[...] = jnp.where(segment <= 5, whole, wrapped)
+    passed = after[...].astype(F32)
+    whole = terms[...] + passed
+    wrapped = jnp.where(segment == 7, passed, 0.0)
+    chosen[...] = jnp.where(segment <= 5, whole, wrapped).astype(BF16)
     kept[...] = jnp.where(segment <= 3, whole, wrapped)
 
 
@@ -236,12 +277,31 @@
     shape = jax.ShapeDtypeStruct(terms.shape, F32)
     return pl.pallas_call(
         prefix_kernel,
-        out_shape=(shape, shape),
+        out_shape=(jax.ShapeDtypeStruct(terms.shape, BF16), shape),
         in_specs=[SMEM, VMEM, VMEM],
         out_specs=(VMEM, VMEM),
         name="prefix",
         **params(0, 1 << 18),
     )(place, terms, after)
+
+
+def window_kernel(kept, after, out, wire):
+    out[...] = kept[...] + after[...].astype(F32)
+    wire[...] = out[...].astype(BF16)
+
+
+def window_step(kept, after):
+    return pl.pallas_call(
+        window_kernel,
+        out_shape=(
+            jax.ShapeDtypeStruct(kept.shape, F32),
+            jax.ShapeDtypeStruct(kept.shape, BF16),
+        ),
+        in_specs=[VMEM, VMEM],
+        out_specs=(VMEM, VMEM),
+        name="window",
+        **params(0, 1 << 18),
+    )(kept, after)
 
 
 def add_kernel(left, right, out):
@@ -260,10 +320,10 @@
 
 
 def past_kernel(*refs):
-    here_ref, beta_ref, near, far, query = refs[:5]
-    acc_a, peak_a, acc_b, peak_b, memory_ref, more_ref = refs[5:11]
-    outs = refs[11 : 11 + NB]
-    keys, values, scores_a, scores_b, result, acc_buf = refs[11 + NB :]
+    here_ref, beta_ref, same, near, far, query = refs[:6]
+    acc_a, peak_a, acc_b, peak_b, memory_ref, more_ref = refs[6:12]
+    outs = refs[12 : 12 + NB]
+    keys, values, scores_a, scores_b, result, acc_buf = refs[12 + NB :]
     here, segment = here_ref[0], here_ref[1]
 
     def own(b):
@@ -279,11 +339,11 @@
 
     @pl.when(segment > 0)
     def _():
-        for d in range(NB):
-            rows = place_rows(here, d)
-            part, spot = (near, NEAR.index(d)) if d in NEAR else (far, FAR.index(d))
-            keys[rows, :] = part[2 * spot]
-            values[rows, :HD] = part[2 * spot + 1]
+        for step, part in ((0, same), (1, near.at[0]), (3, near.at[1]), (2, far)):
+            for half in range(2):
+                rows = pair_rows(here, step, half)
+                keys[rows, :] = part[half, 0]
+                values[rows, :HD] = part[half, 1]
         values[:, HD:] = jnp.ones((NB * BLK, HD), BF16)
         mask = jnp.logical_not(tile_mask())
         for b in range(NB):
@@ -305,7 +365,7 @@
             acc_buf[rows, :HD] = acc[:, :HD] + acc_in[own_rows, :HD] * fade
             acc_buf[rows, HD:] = acc[:, HD:] + acc_in[own_rows, HD:] * fade
 
-    total = jnp.where(segment <= 3, 0.0, memory_ref[...]) + more_ref[...]
+    total = jnp.where(segment <= 3, 0.0, memory_ref[...]) + more_ref[...].astype(F32)
     memory = total[0:HD, :]
     norm = jnp.transpose(jnp.broadcast_to(total[HD : HD + 1, :], (HD, HD)))
     whole = jnp.concatenate([memory, norm], axis=1)
@@ -329,7 +389,7 @@
     return pl.pallas_call(
         past_kernel,
         out_shape=[jax.ShapeDtypeStruct((BLK, HD), BF16)] * NB,
-        in_specs=[SMEM, SMEM] + [VMEM] * 9,
+        in_specs=[SMEM, SMEM] + [VMEM] * 10,
         out_specs=[VMEM] * NB,
         scratch_shapes=[
             pltpu.VMEM((rows, HD), BF16),
@@ -404,27 +464,31 @@
         pltpu.with_memory_space_constraint(part, pltpu.HBM)
         for part in (keys, values, queries, w_out)
     )
-    sent = split_heads(place(0), keys, values, queries)
-    pieces = {0: sent[0]}
-    for d in NEAR[1:] + FAR:
-        pieces[d] = shifted(sent[d], PLANE, d)
-    kvs_past = []
-    for part in (NEAR, FAR):
-        kvs_past.append(shifted(pack([pieces[d] for d in part]), "seq_0", 1, wrap=False))
-    pieces = [pieces[d] for d in range(NB)]
-
-    terms = memory_terms(pieces)
-    after = shifted(terms, "seq_0", -1)
+    stay, leave = split_heads(place(0), keys, values, queries)
+    got = shifted(leave, "seq_2", 1)
+    kvs, qs = map(list, pair_up(place(0), stay, got))
+    past = [shifted(kvs[0], "seq_0", 1)]
+    for step in STEPS:
+        kvs[step] = shifted(kvs[step], "seq_1", step)
+    past.append(shifted(pack(kvs[1], kvs[3]), "seq_0", 1))
+    past.append(shifted(kvs[2], "seq_0", 1))
+    for step in STEPS:
+        qs[step] = shifted(qs[step], "seq_1", step)
+
+    terms, wire = memory_terms(kvs)
+    after = shifted(wire, "seq_0", -1)
     chosen, kept = prefix_step(place(0), terms, after)
     after = shifted(chosen, "seq_0", -2)
-    window = added(kept, after, F32)
-    after = shifted(window, "seq_0", -4)
-
-    k_all, v_all, q_all, acc_a, peak_a, weight = own_first(place(0), pieces, w_out)
+    window, wire = window_step(kept, after)
+    after = shifted(wire, "seq_0", -4)
+
+    k_all, v_all, q_all, acc_a, peak_a, weight = own_first(place(0), kvs, qs, w_out)
     acc_b, peak_b = own_second(k_all, v_all, q_all)
     own = (acc_a, peak_a, acc_b, peak_b)
-    attended = past_part(place(0), beta, kvs_past, q_all, own, (window, after))
-    heads = [attended[0]] + [shifted(attended[d], PLANE, NB - d) for d in range(1, NB)]
+    attended = past_part(place(0), beta, past, q_all, own, (window, after))
+    heads = [attended[0]] + [None] * (NB - 1)
+    for d in LEAVE:
+        heads[d] = shifted(attended[d], PLANE, NB - d)
 
     def send(part, distance):
         return shifted(part, "head", distance)

time: 102 us -> 95.4 us (0.935)
  waiting for transfers between devices: 42.7 us -> 33.6 us
  starting transfers between devices: 37.2 us -> 39.2 us
    ppermute x25 -> x26, waiting for transfers between devices: 42.7 us -> 33.6 us  [shifted(): return lax.ppermute(block, axis, route)]
    ppermute x25 -> x26, starting transfers between devices: 37.2 us -> 39.2 us  [shifted(): return lax.ppermute(block, axis, route)]
    pallas_call x5 -> x6, Pallas kernels: 3.15 us -> 3.78 us  [the longest x1 2.06 us: split_heads(): pl.pallas_call(split_kernel, out_shape=(half, half), in_specs=[SMEM] + [H...]
  transfers between devices with their start and end apart: 25 -> 26, of which waited for: 19 -> 14; matrix products, arithmetic and copies ran while one was open for 0% -> 0% of each run, Pallas kernels for 11% -> 13%
where the time goes in v2:
time: 95.4 us; the launch traced here: 95.3 us
  starting transfers between devices  39.2 us (41%)
  waiting for transfers between devices  33.6 us (35%)
  Pallas kernels  22.1 us (23%)
    ppermute x26, starting transfers between devices, shifted(): return lax.ppermute(block, axis, route)  39.2 us
    ppermute x26, waiting for transfers between devices, shifted(): return lax.ppermute(block, axis, route)  33.6 us
    pallas_call x4, Pallas kernels, project(): pl.pallas_call(project_kernel, in_specs=[SMEM] + [VMEM] * (1 + NB), out_s...  5.54 us
    pallas_call x1, Pallas kernels, past_part(): pl.pallas_call(past_kernel, out_shape=[jax.ShapeDtypeStruct((BLK, HD), BF...  5 us
    pallas_call x1, Pallas kernels, own_first(): pl.pallas_call(own_first_kernel, out_shape=(jax.ShapeDtypeStruct((rows, H...  4.58 us
    pallas_call x1, Pallas kernels, own_second(): pl.pallas_call(own_second_kernel, out_shape=(jax.ShapeDtypeStruct((rows -...  2.12 us
    pallas_call x1, Pallas kernels, split_heads(): pl.pallas_call(split_kernel, out_shape=(half, half), in_specs=[SMEM] + [H...  2.06 us
  transfers between devices with their start and end apart: 26, of which 14 were waited for; matrix products, arithmetic and copies ran while one was open for 0% of the time, Pallas kernels for 13%

profile of v2, /device:TPU:64, one launch (start us, length us, event | category | flops | bytes accessed | tf_op | source)
XLA Modules:
  0.0 95.3 jit_solution(16473642722962472038)
XLA Ops:
  0.2 2.1 %split.1 = (bf16[4,3,256,128]{3,2,1,0:T(8,128)(2,1)S(1)}, bf16[4,3,256,128]{3,2,1,0:T(8,128)(2,1)S(1)}) custom-call(s32[4]{0:T(128)S(1)} %get-tuple-element.89.here_ref.refs_0_.place_ref, bf16[256,1024]{1,0:T(8,128)(2,1)} %keys.1, bf16[256,1024]{1,0:T(8,128)(2,1)} %values.1, bf16[256,1024]{1,0:T(8,128)(2,1)} %queries.1), custom_call_target="tpu_custom_call" | custom-call | bytes 3145728 | tf_op jit(solution)/shard_map/split/pallas_call | solution.py:81
  2.3 2.3 %collective-permute-done.refs_2_ = bf16[4,3,256,128]{3,2,1,0:T(8,128)(2,1)S(1)} collective-permute-done((bf16[4,3,256,128]{3,2,1,0:T(8,128)(2,1)S(1)}, bf16[4,3,256,128]{3,2,1,0:T(8,128)(2,1)S(1)}, u32[]{:S(2)}, u32[]{:S(2)}) %collective-permute-start) | collective-permute-done | bytes 786464 | tf_op jit(solution)/shard_map/ppermute | solution.py:34
  5.3 1.7 %collective-permute-start.2 = (bf16[2,2,256,128]{3,2,1,0:T(8,128)(2,1)S(1)}, bf16[2,2,256,128]{3,2,1,0:T(8,128)(2,1)S(1)}, u32[]{:S(2)}, u32[]{:S(2)}) collective-permute-start(bf16[2,2,256,128]{3,2,1,0:T(8,128)(2,1)S(1)} %get-tuple-element.48), channel_id=1, source_target_pairs={{0,8},{8,16},{16,24},{24,0},{1,9},{9,17},{17,25},{25,1},{2,10},{10... | collective-permute-start | bytes 786440 | tf_op jit(solution)/shard_map/ppermute | solution.py:34
  6.9 1.7 %collective-permute-start.3 = (bf16[2,2,256,128]{3,2,1,0:T(8,128)(2,1)S(1)}, bf16[2,2,256,128]{3,2,1,0:T(8,128)(2,1)S(1)}, u32[]{:S(2)}, u32[]{:S(2)}) collective-permute-start(bf16[2,2,256,128]{3,2,1,0:T(8,128)(2,1)S(1)} %get-tuple-element.49), channel_id=1, source_target_pairs={{0,24},{8,0},{16,8},{24,16},{1,25},{9,1},{17,9},{25,17},{2,26},{10... | collective-permute-start | bytes 786440 | tf_op jit(solution)/shard_map/ppermute | solution.py:34
  8.6 2.0 %collective-permute-start.5 = (bf16[2,2,256,128]{3,2,1,0:T(8,128)(2,1)S(1)}, bf16[2,2,256,128]{3,2,1,0:T(8,128)(2,1)S(1)}, u32[]{:S(2)}, u32[]{:S(2)}) collective-permute-start(bf16[2,2,256,128]{3,2,1,0:T(8,128)(2,1)S(1)} %get-tuple-element.50), channel_id=1, source_target_pairs={{0,16},{8,24},{16,0},{24,8},{1,17},{9,25},{17,1},{25,9},{2,18},{10... | collective-permute-start | bytes 786440 | tf_op jit(solution)/shard_map/ppermute | solution.py:34
  10.6 4.4 %collective-permute-done.2.first.refs_2_.refs_1_ = bf16[2,2,256,128]{3,2,1,0:T(8,128)(2,1)S(1)} collective-permute-done((bf16[2,2,256,128]{3,2,1,0:T(8,128)(2,1)S(1)}, bf16[2,2,256,128]{3,2,1,0:T(8,128)(2,1)S(1)}, u32[]{:S(2)}, u32[]{:S(2)}) %collective-permute-start.2) | collective-permute-done | bytes 262176 | tf_op jit(solution)/shard_map/ppermute | solution.py:34
  15.0 5.0 %collective-permute-done.3.second.refs_4_.refs_3_ = bf16[2,2,256,128]{3,2,1,0:T(8,128)(2,1)S(1)} collective-permute-done((bf16[2,2,256,128]{3,2,1,0:T(8,128)(2,1)S(1)}, bf16[2,2,256,128]{3,2,1,0:T(8,128)(2,1)S(1)}, u32[]{:S(2)}, u32[]{:S(2)}) %collective-permute-start.3) | collective-permute-done | bytes 262176 | tf_op jit(solution)/shard_map/ppermute | solution.py:34
  20.0 2.0 %collective-permute-start.4 = (bf16[2,2,2,256,128]{4,3,2,1,0:T(8,128)(2,1)S(1)}, bf16[2,2,2,256,128]{4,3,2,1,0:T(8,128)(2,1)S(1)}, u32[]{:S(2)}, u32[]{:S(2)}) collective-permute-start(bf16[2,2,2,256,128]{4,3,2,1,0:T(8,128)(2,1)S(1)} %pack.1), channel_id=1, source_target_pairs={{0,32},{32,64},{64,96},{96,128},{128,160},{160,192},{192,224},{224... | collective-permute-start | bytes 1572872 | tf_op jit(solution)/shard_map/ppermute | solution.py:34
  22.0 5.1 %collective-permute-start.8 = (bf16[2,256,128]{2,1,0:T(8,128)(2,1)S(1)}, bf16[2,256,128]{2,1,0:T(8,128)(2,1)S(1)}, u32[]{:S(2)}, u32[]{:S(2)}) collective-permute-start(bf16[2,256,128]{2,1,0:T(8,128)(2,1)S(1)} %get-tuple-element.53), channel_id=1, source_target_pairs={{0,16},{8,24},{16,0},{24,8},{1,17},{9,25},{17,1},{25,9},{2,18},{10... | collective-permute-start | bytes 393224 | tf_op jit(solution)/shard_map/ppermute | solution.py:34
  27.7 1.7 %collective-permute-start.10 = (bf16[136,128]{1,0:T(8,128)(2,1)S(1)}, bf16[136,128]{1,0:T(8,128)(2,1)S(1)}, u32[]{:S(2)}, u32[]{:S(2)}) collective-permute-start(bf16[136,128]{1,0:T(8,128)(2,1)S(1)} %get-tuple-element.63), channel_id=1, source_target_pairs={{0,224},{32,0},{64,32},{96,64},{128,96},{160,128},{192,160},{224,1... | collective-permute-start | bytes 104456 | tf_op jit(solution)/shard_map/ppermute | solution.py:34
  29.3 4.1 %collective-permute-start.1 = (bf16[2,2,256,128]{3,2,1,0:T(8,128)(2,1)S(1)}, bf16[2,2,256,128]{3,2,1,0:T(8,128)(2,1)S(1)}, u32[]{:S(2)}, u32[]{:S(2)}) collective-permute-start(bf16[2,2,256,128]{3,2,1,0:T(8,128)(2,1)S(1)} %get-tuple-element.47.refs_1_.refs_0_), channel_id=1, source_target_pairs={{0,32},{32,64},{64,96},{96,128},{128,160},{160,192},{192,224},{224... | collective-permute-start | bytes 786440 | tf_op jit(solution)/shard_map/ppermute | solution.py:34
  34.4 3.2 %collective-permute-start.6 = (bf16[2,2,256,128]{3,2,1,0:T(8,128)(2,1)S(1)}, bf16[2,2,256,128]{3,2,1,0:T(8,128)(2,1)S(1)}, u32[]{:S(2)}, u32[]{:S(2)}) collective-permute-start(bf16[2,2,256,128]{3,2,1,0:T(8,128)(2,1)S(1)} %collective-permute-done.5.refs_3_.refs_2_), channel_id=1, source_target_pairs={{0,32},{32,64},{64,96},{96,128},{128,160},{160,192},{192,224},{224... | collective-permute-start | bytes 786440 | tf_op jit(solution)/shard_map/ppermute | solution.py:34
  38.5 4.6 %own_first.1 = (bf16[2048,128]{1,0:T(8,128)(2,1)S(1)}, bf16[2048,256]{1,0:T(8,128)(2,1)S(1)}, bf16[2048,128]{1,0:T(8,128)(2,1)S(1)}, f32[1536,256]{1,0:T(8,128)S...) custom-call(s32[4]{0:T(128)S(1)} %get-tuple-element.89.here_ref.refs_0_.place_ref, ...), custom_call_target="tpu_custom_call" | custom-call | flops 1409286144 | bytes 5242880 | tf_op jit(solution)/shard_map/own_first/pallas_call | solution.py:229
  45.7 2.1 %own_second.1 = (f32[512,256]{1,0:T(8,128)S(1)}, f32[512,128]{1,0:T(8,128)S(1)}) custom-call(bf16[2048,128]{1,0:T(8,128)(2,1)S(1)} %get-tuple-element.58.keys, bf16[2048,256]{1,0:T(8,128)(2,1)S(1)} %get-tuple-element.59.values, bf16[2048,128]{1,0:T(8,128)(2,1)S(1)} %get-tuple-element.55.query.refs_5_), custom_call_target="tpu_custom_call" | custom-call | flops 1006632960 | bytes 3145728 | tf_op jit(solution)/shard_map/own_second/pallas_call | solution.py:253
  47.9 4.5 %collective-permute-done.12.refs_11_ = bf16[136,128]{1,0:T(8,128)(2,1)S(1)} collective-permute-done((bf16[136,128]{1,0:T(8,128)(2,1)S(1)}, bf16[136,128]{1,0:T(8,128)(2,1)S(1)}, u32[]{:S(2)}, u32[]{:S(2)}) %collective-permute-start.12) | collective-permute-done | bytes 34848 | tf_op jit(solution)/shard_map/ppermute | solution.py:34
  52.4 5.0 %past.1 = (bf16[256,128]{1,0:T(8,128)(2,1)S(1)}, bf16[256,128]{1,0:T(8,128)(2,1)S(1)}, bf16[256,128]{1,0:T(8,128)(2,1)S(1)}, bf16[256,128]{1,0:T(8,128)(2,1)S(1)...) custom-call(s32[4]{0:T(128)S(1)} %get-tuple-element.89.here_ref.refs, ...), custom_call_target="tpu_custom_call" | custom-call | flops 2415919104 | bytes 6291456 | tf_op jit(solution)/shard_map/past/pallas_call | solution.py:389
  58.1 3.3 %collective-permute-start.15 = (bf16[256,128]{1,0:T(8,128)(2,1)S(1)}, bf16[256,128]{1,0:T(8,128)(2,1)S(1)}, u32[]{:S(2)}, u32[]{:S(2)}) collective-permute-start(bf16[256,128]{1,0:T(8,128)(2,1)S(1)} %get-tuple-element.71), channel_id=1, source_target_pairs={{0,20},{4,24},{8,28},{12,0},{16,4},{20,8},{24,12},{28,16},{1,21},{... | collective-permute-start | bytes 196616 | tf_op jit(solution)/shard_map/ppermute | solution.py:34
  65.1 2.6 %collective-permute-done.16.refs_5_ = bf16[256,128]{1,0:T(8,128)(2,1)S(1)} collective-permute-done((bf16[256,128]{1,0:T(8,128)(2,1)S(1)}, bf16[256,128]{1,0:T(8,128)(2,1)S(1)}, u32[]{:S(2)}, u32[]{:S(2)}) %collective-permute-start.16) | collective-permute-done | bytes 65568 | tf_op jit(solution)/shard_map/ppermute | solution.py:34
  71.6 3.2 %collective-permute-start.24 = (bf16[128,1024]{1,0:T(8,128)(2,1)S(1)}, bf16[128,1024]{1,0:T(8,128)(2,1)S(1)}, u32[]{:S(2)}, u32[]{:S(2)}) collective-permute-start(bf16[128,1024]{1,0:T(8,128)(2,1)S(1)} %get-tuple-element.84), channel_id=1, source_target_pairs={{0,3},{1,0},{2,1},{3,2},{4,7},{5,4},{6,5},{7,6},{8,11},{9,8},{10,9... | collective-permute-start | bytes 786440 | tf_op jit(solution)/shard_map/ppermute | solution.py:34
  78.5 2.6 %collective-permute-start.20 = (bf16[128,1024]{1,0:T(8,128)(2,1)S(1)}, bf16[128,1024]{1,0:T(8,128)(2,1)S(1)}, u32[]{:S(2)}, u32[]{:S(2)}) collective-permute-start(bf16[128,1024]{1,0:T(8,128)(2,1)S(1)} %get-tuple-element.79), channel_id=1, source_target_pairs={{0,3},{1,0},{2,1},{3,2},{4,7},{5,4},{6,5},{7,6},{8,11},{9,8},{10,9... | collective-permute-start | bytes 786440 | tf_op jit(solution)/shard_map/ppermute | solution.py:34
  81.1 2.4 %collective-permute-start.25 = (bf16[128,1024]{1,0:T(8,128)(2,1)S(1)}, bf16[128,1024]{1,0:T(8,128)(2,1)S(1)}, u32[]{:S(2)}, u32[]{:S(2)}) collective-permute-start(bf16[128,1024]{1,0:T(8,128)(2,1)S(1)} %added.3), channel_id=1, source_target_pairs={{0,3},{1,0},{2,1},{3,2},{4,7},{5,4},{6,5},{7,6},{8,11},{9,8},{10,9... | collective-permute-start | bytes 786440 | tf_op jit(solution)/shard_map/ppermute | solution.py:34
  83.5 1.7 %collective-permute-done.21.right = bf16[128,1024]{1,0:T(8,128)(2,1)S(1)} collective-permute-done((bf16[128,1024]{1,0:T(8,128)(2,1)S(1)}, bf16[128,1024]{1,0:T(8,128)(2,1)S(1)}, u32[]{:S(2)}, u32[]{:S(2)}) %collective-permute-start.21) | collective-permute-done | bytes 262176 | tf_op jit(solution)/shard_map/ppermute | solution.py:34
  86.8 4.1 %collective-permute-done.23.low_a = bf16[128,1024]{1,0:T(8,128)(2,1)S(1)} collective-permute-done((bf16[128,1024]{1,0:T(8,128)(2,1)S(1)}, bf16[128,1024]{1,0:T(8,128)(2,1)S(1)}, u32[]{:S(2)}, u32[]{:S(2)}) %collective-permute-start.23) | collective-permute-done | bytes 262176 | tf_op jit(solution)/shard_map/ppermute | solution.py:34
  90.9 3.4 %collective-permute-done.22.up_b = bf16[128,1024]{1,0:T(8,128)(2,1)S(1)} collective-permute-done((bf16[128,1024]{1,0:T(8,128)(2,1)S(1)}, bf16[128,1024]{1,0:T(8,128)(2,1)S(1)}, u32[]{:S(2)}, u32[]{:S(2)}) %collective-permute-start.22) | collective-permute-done | bytes 262176 | tf_op jit(solution)/shard_map/ppermute | solution.py:34
  (48 shorter events, 20.6 us)
Async XLA Ops:
  5.3 9.7 %collective-permute-start.2 = (bf16[2,2,256,128]{3,2,1,0:T(8,128)(2,1)S(1)}, bf16[2,2,256,128]{3,2,1,0:T(8,128)(2,1)S(1)}, u32[]{:S(2)}, u32[]{:S(2)}) collective-permute-start(bf16[2,2,256,128]{3,2,1,0:T(8,128)(2,1)S(1)} %get-tuple-element.48), channel_id=1, source_target_pairs={{0,8},{8,16},{16,24},{24,0},{1,9},{9,17},{17,25},{25,1},{2,10},{10... | collective-permute-start | bytes 786440 | tf_op jit(solution)/shard_map/ppermute | solution.py:34
  6.9 13.0 %collective-permute-start.3 = (bf16[2,2,256,128]{3,2,1,0:T(8,128)(2,1)S(1)}, bf16[2,2,256,128]{3,2,1,0:T(8,128)(2,1)S(1)}, u32[]{:S(2)}, u32[]{:S(2)}) collective-permute-start(bf16[2,2,256,128]{3,2,1,0:T(8,128)(2,1)S(1)} %get-tuple-element.49), channel_id=1, source_target_pairs={{0,24},{8,0},{16,8},{24,16},{1,25},{9,1},{17,9},{25,17},{2,26},{10... | collective-permute-start | bytes 786440 | tf_op jit(solution)/shard_map/ppermute | solution.py:34
  8.6 18.6 %collective-permute-start.5 = (bf16[2,2,256,128]{3,2,1,0:T(8,128)(2,1)S(1)}, bf16[2,2,256,128]{3,2,1,0:T(8,128)(2,1)S(1)}, u32[]{:S(2)}, u32[]{:S(2)}) collective-permute-start(bf16[2,2,256,128]{3,2,1,0:T(8,128)(2,1)S(1)} %get-tuple-element.50), channel_id=1, source_target_pairs={{0,16},{8,24},{16,0},{24,8},{1,17},{9,25},{17,1},{25,9},{2,18},{10... | collective-permute-start | bytes 786440 | tf_op jit(solution)/shard_map/ppermute | solution.py:34
  20.0 32.4 %collective-permute-start.4 = (bf16[2,2,2,256,128]{4,3,2,1,0:T(8,128)(2,1)S(1)}, bf16[2,2,2,256,128]{4,3,2,1,0:T(8,128)(2,1)S(1)}, u32[]{:S(2)}, u32[]{:S(2)}) collective-permute-start(bf16[2,2,2,256,128]{4,3,2,1,0:T(8,128)(2,1)S(1)} %pack.1), channel_id=1, source_target_pairs={{0,32},{32,64},{64,96},{96,128},{128,160},{160,192},{192,224},{224... | collective-permute-start | bytes 1572872 | tf_op jit(solution)/shard_map/ppermute | solution.py:34
  22.0 7.3 %collective-permute-start.7 = (bf16[2,256,128]{2,1,0:T(8,128)(2,1)S(1)}, bf16[2,256,128]{2,1,0:T(8,128)(2,1)S(1)}, u32[]{:S(2)}, u32[]{:S(2)}) collective-permute-start(bf16[2,256,128]{2,1,0:T(8,128)(2,1)S(1)} %get-tuple-element.52), channel_id=1, source_target_pairs={{0,8},{8,16},{16,24},{24,0},{1,9},{9,17},{17,25},{25,1},{2,10},{10... | collective-permute-start | bytes 393224 | tf_op jit(solution)/shard_map/ppermute | solution.py:34
  22.0 16.2 %collective-permute-start.8 = (bf16[2,256,128]{2,1,0:T(8,128)(2,1)S(1)}, bf16[2,256,128]{2,1,0:T(8,128)(2,1)S(1)}, u32[]{:S(2)}, u32[]{:S(2)}) collective-permute-start(bf16[2,256,128]{2,1,0:T(8,128)(2,1)S(1)} %get-tuple-element.53), channel_id=1, source_target_pairs={{0,16},{8,24},{16,0},{24,8},{1,17},{9,25},{17,1},{25,9},{2,18},{10... | collective-permute-start | bytes 393224 | tf_op jit(solution)/shard_map/ppermute | solution.py:34
  27.1 11.3 %collective-permute-start.9 = (bf16[2,256,128]{2,1,0:T(8,128)(2,1)S(1)}, bf16[2,256,128]{2,1,0:T(8,128)(2,1)S(1)}, u32[]{:S(2)}, u32[]{:S(2)}) collective-permute-start(bf16[2,256,128]{2,1,0:T(8,128)(2,1)S(1)} %get-tuple-element.54), channel_id=1, source_target_pairs={{0,24},{8,0},{16,8},{24,16},{1,25},{9,1},{17,9},{25,17},{2,26},{10... | collective-permute-start | bytes 393224 | tf_op jit(solution)/shard_map/ppermute | solution.py:34
  27.7 6.7 %collective-permute-start.10 = (bf16[136,128]{1,0:T(8,128)(2,1)S(1)}, bf16[136,128]{1,0:T(8,128)(2,1)S(1)}, u32[]{:S(2)}, u32[]{:S(2)}) collective-permute-start(bf16[136,128]{1,0:T(8,128)(2,1)S(1)} %get-tuple-element.63), channel_id=1, source_target_pairs={{0,224},{32,0},{64,32},{96,64},{128,96},{160,128},{192,160},{224,1... | collective-permute-start | bytes 104456 | tf_op jit(solution)/shard_map/ppermute | solution.py:34
  29.3 18.5 %collective-permute-start.1 = (bf16[2,2,256,128]{3,2,1,0:T(8,128)(2,1)S(1)}, bf16[2,2,256,128]{3,2,1,0:T(8,128)(2,1)S(1)}, u32[]{:S(2)}, u32[]{:S(2)}) collective-permute-start(bf16[2,2,256,128]{3,2,1,0:T(8,128)(2,1)S(1)} %get-tuple-element.47.refs_1_.refs_0_), channel_id=1, source_target_pairs={{0,32},{32,64},{64,96},{96,128},{128,160},{160,192},{192,224},{224... | collective-permute-start | bytes 786440 | tf_op jit(solution)/shard_map/ppermute | solution.py:34
  34.4 18.1 %collective-permute-start.6 = (bf16[2,2,256,128]{3,2,1,0:T(8,128)(2,1)S(1)}, bf16[2,2,256,128]{3,2,1,0:T(8,128)(2,1)S(1)}, u32[]{:S(2)}, u32[]{:S(2)}) collective-permute-start(bf16[2,2,256,128]{3,2,1,0:T(8,128)(2,1)S(1)} %collective-permute-done.5.refs_3_.refs_2_), channel_id=1, source_target_pairs={{0,32},{32,64},{64,96},{96,128},{128,160},{160,192},{192,224},{224... | collective-permute-start | bytes 786440 | tf_op jit(solution)/shard_map/ppermute | solution.py:34
  38.2 6.3 %collective-permute-start.11 = (bf16[136,128]{1,0:T(8,128)(2,1)S(1)}, bf16[136,128]{1,0:T(8,128)(2,1)S(1)}, u32[]{:S(2)}, u32[]{:S(2)}) collective-permute-start(bf16[136,128]{1,0:T(8,128)(2,1)S(1)} %get-tuple-element.65), channel_id=1, source_target_pairs={{0,192},{32,224},{64,0},{96,32},{128,64},{160,96},{192,128},{224,1... | collective-permute-start | bytes 104456 | tf_op jit(solution)/shard_map/ppermute | solution.py:34
  44.5 7.9 %collective-permute-start.12 = (bf16[136,128]{1,0:T(8,128)(2,1)S(1)}, bf16[136,128]{1,0:T(8,128)(2,1)S(1)}, u32[]{:S(2)}, u32[]{:S(2)}) collective-permute-start(bf16[136,128]{1,0:T(8,128)(2,1)S(1)} %get-tuple-element.67), channel_id=1, source_target_pairs={{0,128},{32,160},{64,192},{96,224},{128,0},{160,32},{192,64},{224,... | collective-permute-start | bytes 104456 | tf_op jit(solution)/shard_map/ppermute | solution.py:34
  57.5 6.2 %collective-permute-start.14 = (bf16[256,128]{1,0:T(8,128)(2,1)S(1)}, bf16[256,128]{1,0:T(8,128)(2,1)S(1)}, u32[]{:S(2)}, u32[]{:S(2)}) collective-permute-start(bf16[256,128]{1,0:T(8,128)(2,1)S(1)} %get-tuple-element.70), channel_id=1, source_target_pairs={{0,24},{4,28},{8,0},{12,4},{16,8},{20,12},{24,16},{28,20},{1,25},{... | collective-permute-start | bytes 196616 | tf_op jit(solution)/shard_map/ppermute | solution.py:34
  58.1 7.0 %collective-permute-start.15 = (bf16[256,128]{1,0:T(8,128)(2,1)S(1)}, bf16[256,128]{1,0:T(8,128)(2,1)S(1)}, u32[]{:S(2)}, u32[]{:S(2)}) collective-permute-start(bf16[256,128]{1,0:T(8,128)(2,1)S(1)} %get-tuple-element.71), channel_id=1, source_target_pairs={{0,20},{4,24},{8,28},{12,0},{16,4},{20,8},{24,12},{28,16},{1,21},{... | collective-permute-start | bytes 196616 | tf_op jit(solution)/shard_map/ppermute | solution.py:34
  61.4 6.3 %collective-permute-start.16 = (bf16[256,128]{1,0:T(8,128)(2,1)S(1)}, bf16[256,128]{1,0:T(8,128)(2,1)S(1)}, u32[]{:S(2)}, u32[]{:S(2)}) collective-permute-start(bf16[256,128]{1,0:T(8,128)(2,1)S(1)} %get-tuple-element.72), channel_id=1, source_target_pairs={{0,16},{4,20},{8,24},{12,28},{16,0},{20,4},{24,8},{28,12},{1,17},{... | collective-permute-start | bytes 196616 | tf_op jit(solution)/shard_map/ppermute | solution.py:34
  61.7 6.0 %collective-permute-start.17 = (bf16[256,128]{1,0:T(8,128)(2,1)S(1)}, bf16[256,128]{1,0:T(8,128)(2,1)S(1)}, u32[]{:S(2)}, u32[]{:S(2)}) collective-permute-start(bf16[256,128]{1,0:T(8,128)(2,1)S(1)} %get-tuple-element.73), channel_id=1, source_target_pairs={{0,12},{4,16},{8,20},{12,24},{16,28},{20,0},{24,4},{28,8},{1,13},{... | collective-permute-start | bytes 196616 | tf_op jit(solution)/shard_map/ppermute | solution.py:34
  62.5 6.2 %collective-permute-start.18 = (bf16[256,128]{1,0:T(8,128)(2,1)S(1)}, bf16[256,128]{1,0:T(8,128)(2,1)S(1)}, u32[]{:S(2)}, u32[]{:S(2)}) collective-permute-start(bf16[256,128]{1,0:T(8,128)(2,1)S(1)} %get-tuple-element.74), channel_id=1, source_target_pairs={{0,8},{4,12},{8,16},{12,20},{16,24},{20,28},{24,0},{28,4},{1,9},{5... | collective-permute-start | bytes 196616 | tf_op jit(solution)/shard_map/ppermute | solution.py:34
  63.7 6.6 %collective-permute-start.19 = (bf16[256,128]{1,0:T(8,128)(2,1)S(1)}, bf16[256,128]{1,0:T(8,128)(2,1)S(1)}, u32[]{:S(2)}, u32[]{:S(2)}) collective-permute-start(bf16[256,128]{1,0:T(8,128)(2,1)S(1)} %get-tuple-element.75), channel_id=1, source_target_pairs={{0,4},{4,8},{8,12},{12,16},{16,20},{20,24},{24,28},{28,0},{1,5},{5... | collective-permute-start | bytes 196616 | tf_op jit(solution)/shard_map/ppermute | solution.py:34
  71.6 9.4 %collective-permute-start.24 = (bf16[128,1024]{1,0:T(8,128)(2,1)S(1)}, bf16[128,1024]{1,0:T(8,128)(2,1)S(1)}, u32[]{:S(2)}, u32[]{:S(2)}) collective-permute-start(bf16[128,1024]{1,0:T(8,128)(2,1)S(1)} %get-tuple-element.84), channel_id=1, source_target_pairs={{0,3},{1,0},{2,1},{3,2},{4,7},{5,4},{6,5},{7,6},{8,11},{9,8},{10,9... | collective-permute-start | bytes 786440 | tf_op jit(solution)/shard_map/ppermute | solution.py:34
  74.8 10.4 %collective-permute-start.21 = (bf16[128,1024]{1,0:T(8,128)(2,1)S(1)}, bf16[128,1024]{1,0:T(8,128)(2,1)S(1)}, u32[]{:S(2)}, u32[]{:S(2)}) collective-permute-start(bf16[128,1024]{1,0:T(8,128)(2,1)S(1)} %get-tuple-element.81), channel_id=1, source_target_pairs={{0,1},{1,2},{2,3},{3,0},{4,5},{5,6},{6,7},{7,4},{8,9},{9,10},{10,1... | collective-permute-start | bytes 786440 | tf_op jit(solution)/shard_map/ppermute | solution.py:34
  76.2 14.6 %collective-permute-start.23 = (bf16[128,1024]{1,0:T(8,128)(2,1)S(1)}, bf16[128,1024]{1,0:T(8,128)(2,1)S(1)}, u32[]{:S(2)}, u32[]{:S(2)}) collective-permute-start(bf16[128,1024]{1,0:T(8,128)(2,1)S(1)} %get-tuple-element.82), channel_id=1, source_target_pairs={{0,1},{1,2},{2,3},{3,0},{4,5},{5,6},{6,7},{7,4},{8,9},{9,10},{10,1... | collective-permute-start | bytes 786440 | tf_op jit(solution)/shard_map/ppermute | solution.py:34
  78.5 12.4 %collective-permute-start.20 = (bf16[128,1024]{1,0:T(8,128)(2,1)S(1)}, bf16[128,1024]{1,0:T(8,128)(2,1)S(1)}, u32[]{:S(2)}, u32[]{:S(2)}) collective-permute-start(bf16[128,1024]{1,0:T(8,128)(2,1)S(1)} %get-tuple-element.79), channel_id=1, source_target_pairs={{0,3},{1,0},{2,1},{3,2},{4,7},{5,4},{6,5},{7,6},{8,11},{9,8},{10,9... | collective-permute-start | bytes 786440 | tf_op jit(solution)/shard_map/ppermute | solution.py:34
  81.1 9.8 %collective-permute-start.25 = (bf16[128,1024]{1,0:T(8,128)(2,1)S(1)}, bf16[128,1024]{1,0:T(8,128)(2,1)S(1)}, u32[]{:S(2)}, u32[]{:S(2)}) collective-permute-start(bf16[128,1024]{1,0:T(8,128)(2,1)S(1)} %added.3), channel_id=1, source_target_pairs={{0,3},{1,0},{2,1},{3,2},{4,7},{5,4},{6,5},{7,6},{8,11},{9,8},{10,9... | collective-permute-start | bytes 786440 | tf_op jit(solution)/shard_map/ppermute | solution.py:34
  85.3 9.0 %collective-permute-start.22 = (bf16[128,1024]{1,0:T(8,128)(2,1)S(1)}, bf16[128,1024]{1,0:T(8,128)(2,1)S(1)}, u32[]{:S(2)}, u32[]{:S(2)}) collective-permute-start(bf16[128,1024]{1,0:T(8,128)(2,1)S(1)} %added.2), channel_id=1, source_target_pairs={{0,1},{1,2},{2,3},{3,0},{4,5},{5,6},{6,7},{7,4},{8,9},{9,10},{10,1... | collective-permute-start | bytes 786440 | tf_op jit(solution)/shard_map/ppermute | solution.py:34
  (3 other events, 54.6 us)

commit v3 on v2

--- a/solution.py
+++ b/solution.py
@@ -21,7 +21,7 @@
 NY = 4
 PAIR = 2 * BLK
 STEPS = (1, 3, 2)
-LEAVE = (4, 3, 5, 2, 6, 1, 7)
+LEAVE = (2, 1, 3)
 SPLIT = 6
 
 
@@ -38,10 +38,6 @@
     return jnp.where(inputs > 0, inputs + 1.0, jnp.exp(jnp.minimum(inputs, 0.0)))
 
 
-def slot_of(here, d):
-    return lax.rem(here - d + NB, NB)
-
-
 def pair_rows(here, step, half):
     row = lax.rem(here // 2 - step + NY, NY) * PAIR + half * BLK
     return pl.ds(pl.multiple_of(row, BLK), BLK)
@@ -52,10 +48,6 @@
         cost_estimate=pl.CostEstimate(flops=flops, bytes_accessed=nbytes, transcendentals=0),
         compiler_params=pltpu.CompilerParams(vmem_limit_bytes=room * 1024 * 1024),
     )
-
-
-def place_rows(here, d):
-    return pl.ds(pl.multiple_of(slot_of(here, d) * BLK, BLK), BLK)
 
 
 def split_kernel(here_ref, keys, values, queries, stay, leave, whole, sems):
@@ -175,13 +167,18 @@
         high = jnp.maximum(part[:, :HD], part[:, HD:])
         peak = high if peak is None else jnp.maximum(peak, high)
     peak = jnp.max(peak, axis=1, keepdims=True)
-    shift = peak * SCALE2
-    acc = None
+    half = query.shape[0] // 2
+    upper = lower = None
     for j in range(count):
         rows = pl.ds((first + j) * BLK, BLK)
-        weights = jnp.exp2(scores[:, j * BLK : (j + 1) * BLK] * SCALE2 - shift).astype(BF16)
-        part = jnp.dot(weights, values_ones[rows, :], preferred_element_type=F32)
-        acc = part if acc is None else acc + part
+        weights = scores[:, j * BLK : (j + 1) * BLK] - peak
+        weights = jnp.exp2(weights * SCALE2).astype(BF16)
+        value = values_ones[rows, :]
+        above = jnp.dot(weights[:half], value, preferred_element_type=F32)
+        below = jnp.dot(weights[half:], value, preferred_element_type=F32)
+        upper = above if upper is None else upper + above
+        lower = below if lower is None else lower + below
+    acc = jnp.concatenate([upper, lower], axis=0)
     return acc, peak
 
 
@@ -320,10 +317,9 @@
 
 
 def past_kernel(*refs):
-    here_ref, beta_ref, same, near, far, query = refs[:6]
-    acc_a, peak_a, acc_b, peak_b, memory_ref, more_ref = refs[6:12]
-    outs = refs[12 : 12 + NB]
-    keys, values, scores_a, scores_b, result, acc_buf = refs[12 + NB :]
+    here_ref, same, near, far, query = refs[:5]
+    acc_a, peak_a, acc_b, peak_b, local_out = refs[5:10]
+    keys, values, scores_a, scores_b, acc_buf = refs[10:]
     here, segment = here_ref[0], here_ref[1]
 
     def own(b):
@@ -365,6 +361,13 @@
             acc_buf[rows, :HD] = acc[:, :HD] + acc_in[own_rows, :HD] * fade
             acc_buf[rows, HD:] = acc[:, HD:] + acc_in[own_rows, HD:] * fade
 
+    local_out[...] = acc_buf[:, :HD] / acc_buf[:, HD:]
+
+
+def blend_kernel(*refs):
+    here_ref, beta_ref, query, local_ref, memory_ref, more_ref = refs[:6]
+    outs, result = refs[6:-1], refs[-1]
+    here, segment = here_ref[0], here_ref[1]
     total = jnp.where(segment <= 3, 0.0, memory_ref[...]) + more_ref[...].astype(F32)
     memory = total[0:HD, :]
     norm = jnp.transpose(jnp.broadcast_to(total[HD : HD + 1, :], (HD, HD)))
@@ -378,40 +381,73 @@
         soft = elu_plus(query[rows, :].astype(F32)).astype(BF16)
         both = jnp.dot(jnp.concatenate([soft, soft], axis=1), split, preferred_element_type=F32)
         from_memory = both[:, :HD] / (1.0 + both[:, HD:])
-        local = acc_buf[rows, :HD] / acc_buf[rows, HD:]
+        local = local_ref[rows, :]
         result[rows, :] = (gate * from_memory + (1.0 - gate) * local).astype(BF16)
-    for d in range(NB):
-        outs[d][...] = result[place_rows(here, d), :]
-
-
-def past_part(here, beta, kvs, query, own, memory):
+    for step in range(NY):
+        for half in range(2):
+            outs[step][half] = result[pair_rows(here, step, half), :]
+
+
+def past_part(here, past, query, own):
     rows = NB * BLK
     return pl.pallas_call(
         past_kernel,
-        out_shape=[jax.ShapeDtypeStruct((BLK, HD), BF16)] * NB,
-        in_specs=[SMEM, SMEM] + [VMEM] * 10,
-        out_specs=[VMEM] * NB,
+        out_shape=jax.ShapeDtypeStruct((rows, HD), F32),
+        in_specs=[SMEM] + [VMEM] * 8,
+        out_specs=VMEM,
         scratch_shapes=[
             pltpu.VMEM((rows, HD), BF16),
             pltpu.VMEM((rows, 2 * HD), BF16),
             pltpu.VMEM((BLK, rows), F32),
             pltpu.VMEM((BLK, rows), F32),
-            pltpu.VMEM((rows, HD), BF16),
             pltpu.VMEM((rows, 2 * HD), F32),
         ],
         name="past",
-        **params(36 * BLK * BLK * HD * 8, 6 << 20),
-    )(here, beta, *kvs, query, *own, *memory)
+        **params(36 * BLK * BLK * HD * 8, 6 << 20, 24),
+    )(here, *past, query, *own)
+
+
+def blend(here, beta, query, local, memory):
+    return pl.pallas_call(
+        blend_kernel,
+        out_shape=[jax.ShapeDtypeStruct((2, BLK, HD), BF16)] * NY,
+        in_specs=[SMEM, SMEM] + [VMEM] * 4,
+        out_specs=[VMEM] * NY,
+        scratch_shapes=[pltpu.VMEM((NB * BLK, HD), BF16)],
+        name="blend",
+        **params(1 << 28, 3 << 20),
+    )(here, beta, query, local, *memory)
+
+
+def turn_kernel(*refs):
+    core = lax.rem(refs[0][0], 2)
+    for step in range(NY):
+        refs[-1][step] = refs[1 + step][1 - core]
+
+
+def turn(here, pieces):
+    return pl.pallas_call(
+        turn_kernel,
+        out_shape=jax.ShapeDtypeStruct((NY, BLK, HD), BF16),
+        in_specs=[SMEM] + [VMEM] * NY,
+        out_specs=VMEM,
+        name="turn",
+        **params(0, 1 << 18),
+    )(here, *pieces)
 
 
 def project_kernel(*refs):
     spot_ref = refs[0]
-    pieces, weight = refs[1 : 1 + NB], refs[1 + NB]
-    upper, lower = refs[2 + NB : 4 + NB]
-    attended = refs[4 + NB]
-    for d in range(NB):
-        start = pl.multiple_of(lax.rem(spot_ref[0] + d, NB) * HD, HD)
-        attended[:, pl.ds(start, HD)] = pieces[d][...]
+    pieces, other, weight = refs[1 : 1 + NY], refs[1 + NY], refs[2 + NY]
+    upper, lower = refs[3 + NY : 5 + NY]
+    attended = refs[5 + NY]
+    core = lax.rem(spot_ref[0], 2)
+    for step in range(NY):
+        pair = lax.rem(spot_ref[0] // 2 + step, NY) * 2
+        start = pl.multiple_of((pair + core) * HD, HD)
+        attended[:, pl.ds(start, HD)] = pieces[step][core]
+        start = pl.multiple_of((pair + 1 - core) * HD, HD)
+        attended[:, pl.ds(start, HD)] = other[step]
     width = upper.shape[1]
     cols = pl.ds(pl.multiple_of(lax.rem(spot_ref[2] + spot_ref[3], 4) * width, width), width)
     whole = jnp.dot(attended[...], weight[:, cols], preferred_element_type=F32)
@@ -423,7 +459,7 @@
     width = weight.shape[1] // 4
     return pl.pallas_call(
         project_kernel,
-        in_specs=[SMEM] + [VMEM] * (1 + NB),
+        in_specs=[SMEM] + [VMEM] * (2 + NY),
         out_specs=(VMEM, VMEM),
         scratch_shapes=[pltpu.VMEM((BLK, NB * HD), BF16)],
         out_shape=(
@@ -485,10 +521,12 @@
     k_all, v_all, q_all, acc_a, peak_a, weight = own_first(place(0), kvs, qs, w_out)
     acc_b, peak_b = own_second(k_all, v_all, q_all)
     own = (acc_a, peak_a, acc_b, peak_b)
-    attended = past_part(place(0), beta, past, q_all, own, (window, after))
-    heads = [attended[0]] + [None] * (NB - 1)
-    for d in LEAVE:
-        heads[d] = shifted(attended[d], PLANE, NB - d)
+    local = past_part(place(0), past, q_all, own)
+    attended = blend(place(0), beta, q_all, local, (window, after))
+    heads = list(attended)
+    for step in LEAVE:
+        heads[step] = shifted(heads[step], "seq_1", -step)
+    heads.append(shifted(turn(place(0), heads), "seq_2", 1))
 
     def send(part, distance):
         return shifted(part, "head", distance)

time: 95.4 us -> 94.5 us (level)
  starting transfers between devices: 39.2 us -> 35.7 us
  waiting for transfers between devices: 33.6 us -> 35.5 us
    ppermute x26 -> x23, starting transfers between devices: 39.2 us -> 35.7 us  [shifted(): return lax.ppermute(block, axis, route)]
    ppermute x26 -> x23, waiting for transfers between devices: 33.6 us -> 35.5 us  [shifted(): return lax.ppermute(block, axis, route)]
    pallas_call x5 -> x7, Pallas kernels: 10.5 us -> 11.9 us  [the longest x4 5.58 us: project(): pl.pallas_call(project_kernel, in_specs=[SMEM] + [VMEM] * (2 + NY), out_s...]
  transfers between devices with their start and end apart: 26 -> 23, of which waited for: 14 -> 14; matrix products, arithmetic and copies ran while one was open for 0% -> 0% of each run, Pallas kernels for 13% -> 17%
where the time goes in v3:
time: 94.5 us; the launch traced here: 94.4 us
  starting transfers between devices  35.7 us (38%)
  waiting for transfers between devices  35.5 us (38%)
  Pallas kernels  22.9 us (24%)
    ppermute x23, starting transfers between devices, shifted(): return lax.ppermute(block, axis, route)  35.7 us
    ppermute x23, waiting for transfers between devices, shifted(): return lax.ppermute(block, axis, route)  35.5 us
    pallas_call x4, Pallas kernels, project(): pl.pallas_call(project_kernel, in_specs=[SMEM] + [VMEM] * (2 + NY), out_s...  5.58 us
    pallas_call x1, Pallas kernels, past_part(): pl.pallas_call(past_kernel, out_shape=jax.ShapeDtypeStruct((rows, HD), F3...  4.55 us
    pallas_call x1, Pallas kernels, own_first(): pl.pallas_call(own_first_kernel, out_shape=(jax.ShapeDtypeStruct((rows, H...  4.48 us
    pallas_call x1, Pallas kernels, split_heads(): pl.pallas_call(split_kernel, out_shape=(half, half), in_specs=[SMEM] + [H...  2.06 us
  transfers between devices with their start and end apart: 23, of which 14 were waited for; matrix products, arithmetic and copies ran while one was open for 0% of the time, Pallas kernels for 17%

profile of v3, /device:TPU:64, one launch (start us, length us, event | category | flops | bytes accessed | tf_op | source)
XLA Modules:
  0.0 94.4 jit_solution(10124720022221189390)
XLA Ops:
  0.2 2.1 %split.1 = (bf16[4,3,256,128]{3,2,1,0:T(8,128)(2,1)S(1)}, bf16[4,3,256,128]{3,2,1,0:T(8,128)(2,1)S(1)}) custom-call(s32[4]{0:T(128)S(1)} %get-tuple-element.81.here_ref.refs_0_.place_ref, bf16[256,1024]{1,0:T(8,128)(2,1)} %keys.1, bf16[256,1024]{1,0:T(8,128)(2,1)} %values.1, bf16[256,1024]{1,0:T(8,128)(2,1)} %queries.1), custom_call_target="tpu_custom_call" | custom-call | bytes 3145728 | tf_op jit(solution)/shard_map/split/pallas_call | solution.py:73
  2.3 2.3 %collective-permute-done.refs_2_ = bf16[4,3,256,128]{3,2,1,0:T(8,128)(2,1)S(1)} collective-permute-done((bf16[4,3,256,128]{3,2,1,0:T(8,128)(2,1)S(1)}, bf16[4,3,256,128]{3,2,1,0:T(8,128)(2,1)S(1)}, u32[]{:S(2)}, u32[]{:S(2)}) %collective-permute-start) | collective-permute-done | bytes 786464 | tf_op jit(solution)/shard_map/ppermute | solution.py:34
  5.3 1.7 %collective-permute-start.1 = (bf16[2,2,256,128]{3,2,1,0:T(8,128)(2,1)S(1)}, bf16[2,2,256,128]{3,2,1,0:T(8,128)(2,1)S(1)}, u32[]{:S(2)}, u32[]{:S(2)}) collective-permute-start(bf16[2,2,256,128]{3,2,1,0:T(8,128)(2,1)S(1)} %get-tuple-element.44), channel_id=1, source_target_pairs={{0,8},{8,16},{16,24},{24,0},{1,9},{9,17},{17,25},{25,1},{2,10},{10... | collective-permute-start | bytes 786440 | tf_op jit(solution)/shard_map/ppermute | solution.py:34
  6.9 1.7 %collective-permute-start.3 = (bf16[2,2,256,128]{3,2,1,0:T(8,128)(2,1)S(1)}, bf16[2,2,256,128]{3,2,1,0:T(8,128)(2,1)S(1)}, u32[]{:S(2)}, u32[]{:S(2)}) collective-permute-start(bf16[2,2,256,128]{3,2,1,0:T(8,128)(2,1)S(1)} %get-tuple-element.46), channel_id=1, source_target_pairs={{0,24},{8,0},{16,8},{24,16},{1,25},{9,1},{17,9},{25,17},{2,26},{10... | collective-permute-start | bytes 786440 | tf_op jit(solution)/shard_map/ppermute | solution.py:34
  8.6 2.0 %collective-permute-start.2 = (bf16[2,2,256,128]{3,2,1,0:T(8,128)(2,1)S(1)}, bf16[2,2,256,128]{3,2,1,0:T(8,128)(2,1)S(1)}, u32[]{:S(2)}, u32[]{:S(2)}) collective-permute-start(bf16[2,2,256,128]{3,2,1,0:T(8,128)(2,1)S(1)} %get-tuple-element.45), channel_id=1, source_target_pairs={{0,16},{8,24},{16,0},{24,8},{1,17},{9,25},{17,1},{25,9},{2,18},{10... | collective-permute-start | bytes 786440 | tf_op jit(solution)/shard_map/ppermute | solution.py:34
  10.6 4.4 %collective-permute-done.1.refs_2_.first.refs_1_ = bf16[2,2,256,128]{3,2,1,0:T(8,128)(2,1)S(1)} collective-permute-done((bf16[2,2,256,128]{3,2,1,0:T(8,128)(2,1)S(1)}, bf16[2,2,256,128]{3,2,1,0:T(8,128)(2,1)S(1)}, u32[]{:S(2)}, u32[]{:S(2)}) %collective-permute-start.1) | collective-permute-done | bytes 262176 | tf_op jit(solution)/shard_map/ppermute | solution.py:34
  15.0 5.0 %collective-permute-done.3.refs_4_.second.refs_3_ = bf16[2,2,256,128]{3,2,1,0:T(8,128)(2,1)S(1)} collective-permute-done((bf16[2,2,256,128]{3,2,1,0:T(8,128)(2,1)S(1)}, bf16[2,2,256,128]{3,2,1,0:T(8,128)(2,1)S(1)}, u32[]{:S(2)}, u32[]{:S(2)}) %collective-permute-start.3) | collective-permute-done | bytes 262176 | tf_op jit(solution)/shard_map/ppermute | solution.py:34
  20.0 2.0 %collective-permute-start.8 = (bf16[2,2,2,256,128]{4,3,2,1,0:T(8,128)(2,1)S(1)}, bf16[2,2,2,256,128]{4,3,2,1,0:T(8,128)(2,1)S(1)}, u32[]{:S(2)}, u32[]{:S(2)}) collective-permute-start(bf16[2,2,2,256,128]{4,3,2,1,0:T(8,128)(2,1)S(1)} %pack.1), channel_id=1, source_target_pairs={{0,32},{32,64},{64,96},{96,128},{128,160},{160,192},{192,224},{224... | collective-permute-start | bytes 1572872 | tf_op jit(solution)/shard_map/ppermute | solution.py:34
  22.0 5.1 %collective-permute-start.5 = (bf16[2,256,128]{2,1,0:T(8,128)(2,1)S(1)}, bf16[2,256,128]{2,1,0:T(8,128)(2,1)S(1)}, u32[]{:S(2)}, u32[]{:S(2)}) collective-permute-start(bf16[2,256,128]{2,1,0:T(8,128)(2,1)S(1)} %get-tuple-element.49), channel_id=1, source_target_pairs={{0,16},{8,24},{16,0},{24,8},{1,17},{9,25},{17,1},{25,9},{2,18},{10... | collective-permute-start | bytes 393224 | tf_op jit(solution)/shard_map/ppermute | solution.py:34
  28.6 4.8 %collective-permute-start.7 = (bf16[2,2,256,128]{3,2,1,0:T(8,128)(2,1)S(1)}, bf16[2,2,256,128]{3,2,1,0:T(8,128)(2,1)S(1)}, u32[]{:S(2)}, u32[]{:S(2)}) collective-permute-start(bf16[2,2,256,128]{3,2,1,0:T(8,128)(2,1)S(1)} %get-tuple-element.43.refs_1_.refs_0_), channel_id=1, source_target_pairs={{0,32},{32,64},{64,96},{96,128},{128,160},{160,192},{192,224},{224... | collective-permute-start | bytes 786440 | tf_op jit(solution)/shard_map/ppermute | solution.py:34
  36.0 4.5 %own_first.1 = (bf16[2048,128]{1,0:T(8,128)(2,1)S(1)}, bf16[2048,256]{1,0:T(8,128)(2,1)S(1)}, bf16[2048,128]{1,0:T(8,128)(2,1)S(1)}, f32[1536,256]{1,0:T(8,128)S...) custom-call(s32[4]{0:T(128)S(1)} %get-tuple-element.81.here_ref.refs_0_.place_ref, ...), custom_call_target="tpu_custom_call" | custom-call | flops 1409286144 | bytes 5242880 | tf_op jit(solution)/shard_map/own_first/pallas_call | solution.py:226
  41.3 1.7 %own_second.1 = (f32[512,256]{1,0:T(8,128)S(1)}, f32[512,128]{1,0:T(8,128)S(1)}) custom-call(bf16[2048,128]{1,0:T(8,128)(2,1)S(1)} %get-tuple-element.54.keys, bf16[2048,256]{1,0:T(8,128)(2,1)S(1)} %get-tuple-element.55.values, bf16[2048,128]{1,0:T(8,128)(2,1)S(1)} %get-tuple-element.51.query.refs_4_.refs_2_), custom_call_target="tpu_custom_call" | custom-call | flops 1006632960 | bytes 3145728 | tf_op jit(solution)/shard_map/own_second/pallas_call | solution.py:250
  43.0 4.3 %collective-permute-done.11.after = bf16[136,128]{1,0:T(8,128)(2,1)S(1)} collective-permute-done((bf16[136,128]{1,0:T(8,128)(2,1)S(1)}, bf16[136,128]{1,0:T(8,128)(2,1)S(1)}, u32[]{:S(2)}, u32[]{:S(2)}) %collective-permute-start.11) | collective-permute-done | bytes 34848 | tf_op jit(solution)/shard_map/ppermute | solution.py:34
  47.4 3.0 %collective-permute-start.12 = (bf16[136,128]{1,0:T(8,128)(2,1)S(1)}, bf16[136,128]{1,0:T(8,128)(2,1)S(1)}, u32[]{:S(2)}, u32[]{:S(2)}) collective-permute-start(bf16[136,128]{1,0:T(8,128)(2,1)S(1)} %get-tuple-element.63), channel_id=1, source_target_pairs={{0,128},{32,160},{64,192},{96,224},{128,0},{160,32},{192,64},{224,... | collective-permute-start | bytes 104456 | tf_op jit(solution)/shard_map/ppermute | solution.py:34
  50.4 4.6 %past.1.refs_3_ = f32[2048,128]{1,0:T(8,128)S(1)} custom-call(s32[4]{0:T(128)S(1)} %get-tuple-element.81.here_ref.refs_0_.place_ref, bf16[2,2,256,128]{3,2,1,0:T(8,128)(2,1)S(1)} %collective-permute-done.7.refs_1_, bf16[2,2,2,256,128]{4,3,2,1,0:T(8,128)(2,1)S(1)} %collective-permute-done.8.refs_2_, ...), custom_call_target="tpu_custom_call" | custom-call | flops 2415919104 | bytes 6291456 | tf_op jit(solution)/shard_map/past/pallas_call | solution.py:393
  56.5 2.1 %collective-permute-start.13 = (bf16[2,256,128]{2,1,0:T(8,128)(2,1)S(1)}, bf16[2,256,128]{2,1,0:T(8,128)(2,1)S(1)}, u32[]{:S(2)}, u32[]{:S(2)}) collective-permute-start(bf16[2,256,128]{2,1,0:T(8,128)(2,1)S(1)} %get-tuple-element.65), channel_id=1, source_target_pairs={{0,24},{8,0},{16,8},{24,16},{1,25},{9,1},{17,9},{25,17},{2,26},{10... | collective-permute-start | bytes 393224 | tf_op jit(solution)/shard_map/ppermute | solution.py:34
  59.6 2.9 %collective-permute-done.13.refs_2_ = bf16[2,256,128]{2,1,0:T(8,128)(2,1)S(1)} collective-permute-done((bf16[2,256,128]{2,1,0:T(8,128)(2,1)S(1)}, bf16[2,256,128]{2,1,0:T(8,128)(2,1)S(1)}, u32[]{:S(2)}, u32[]{:S(2)}) %collective-permute-start.13) | collective-permute-done | bytes 131104 | tf_op jit(solution)/shard_map/ppermute | solution.py:34
  62.6 2.6 %collective-permute-done.14.refs_3_ = bf16[2,256,128]{2,1,0:T(8,128)(2,1)S(1)} collective-permute-done((bf16[2,256,128]{2,1,0:T(8,128)(2,1)S(1)}, bf16[2,256,128]{2,1,0:T(8,128)(2,1)S(1)}, u32[]{:S(2)}, u32[]{:S(2)}) %collective-permute-start.14) | collective-permute-done | bytes 131104 | tf_op jit(solution)/shard_map/ppermute | solution.py:34
  67.2 1.5 %collective-permute-done.16.refs_5_ = bf16[4,256,128]{2,1,0:T(8,128)(2,1)S(1)} collective-permute-done((bf16[4,256,128]{2,1,0:T(8,128)(2,1)S(1)}, bf16[4,256,128]{2,1,0:T(8,128)(2,1)S(1)}, u32[]{:S(2)}, u32[]{:S(2)}) %collective-permute-start.16) | collective-permute-done | bytes 262176 | tf_op jit(solution)/shard_map/ppermute | solution.py:34
  70.1 2.8 %collective-permute-start.21 = (bf16[128,1024]{1,0:T(8,128)(2,1)S(1)}, bf16[128,1024]{1,0:T(8,128)(2,1)S(1)}, u32[]{:S(2)}, u32[]{:S(2)}) collective-permute-start(bf16[128,1024]{1,0:T(8,128)(2,1)S(1)} %get-tuple-element.76), channel_id=1, source_target_pairs={{0,3},{1,0},{2,1},{3,2},{4,7},{5,4},{6,5},{7,6},{8,11},{9,8},{10,9... | collective-permute-start | bytes 786440 | tf_op jit(solution)/shard_map/ppermute | solution.py:34
  76.8 2.6 %collective-permute-start.17 = (bf16[128,1024]{1,0:T(8,128)(2,1)S(1)}, bf16[128,1024]{1,0:T(8,128)(2,1)S(1)}, u32[]{:S(2)}, u32[]{:S(2)}) collective-permute-start(bf16[128,1024]{1,0:T(8,128)(2,1)S(1)} %get-tuple-element.71), channel_id=1, source_target_pairs={{0,3},{1,0},{2,1},{3,2},{4,7},{5,4},{6,5},{7,6},{8,11},{9,8},{10,9... | collective-permute-start | bytes 786440 | tf_op jit(solution)/shard_map/ppermute | solution.py:34
  79.4 3.2 %collective-permute-start.22 = (bf16[128,1024]{1,0:T(8,128)(2,1)S(1)}, bf16[128,1024]{1,0:T(8,128)(2,1)S(1)}, u32[]{:S(2)}, u32[]{:S(2)}) collective-permute-start(bf16[128,1024]{1,0:T(8,128)(2,1)S(1)} %added.3), channel_id=1, source_target_pairs={{0,3},{1,0},{2,1},{3,2},{4,7},{5,4},{6,5},{7,6},{8,11},{9,8},{10,9... | collective-permute-start | bytes 786440 | tf_op jit(solution)/shard_map/ppermute | solution.py:34
  84.9 4.1 %collective-permute-done.20.low_a = bf16[128,1024]{1,0:T(8,128)(2,1)S(1)} collective-permute-done((bf16[128,1024]{1,0:T(8,128)(2,1)S(1)}, bf16[128,1024]{1,0:T(8,128)(2,1)S(1)}, u32[]{:S(2)}, u32[]{:S(2)}) %collective-permute-start.20) | collective-permute-done | bytes 262176 | tf_op jit(solution)/shard_map/ppermute | solution.py:34
  90.3 3.2 %collective-permute-done.19.up_b = bf16[128,1024]{1,0:T(8,128)(2,1)S(1)} collective-permute-done((bf16[128,1024]{1,0:T(8,128)(2,1)S(1)}, bf16[128,1024]{1,0:T(8,128)(2,1)S(1)}, u32[]{:S(2)}, u32[]{:S(2)}) %collective-permute-start.19) | collective-permute-done | bytes 262176 | tf_op jit(solution)/shard_map/ppermute | solution.py:34
  (44 shorter events, 20.2 us)
Async XLA Ops:
  2.2 2.4 %collective-permute-start = (bf16[4,3,256,128]{3,2,1,0:T(8,128)(2,1)S(1)}, bf16[4,3,256,128]{3,2,1,0:T(8,128)(2,1)S(1)}, u32[]{:S(2)}, u32[]{:S(2)}) collective-permute-start(bf16[4,3,256,128]{3,2,1,0:T(8,128)(2,1)S(1)} %get-tuple-element.42), channel_id=1, source_target_pairs={{0,4},{4,0},{1,5},{5,1},{2,6},{6,2},{3,7},{7,3},{8,12},{12,8},{9,1... | collective-permute-start | bytes 2359304 | tf_op jit(solution)/shard_map/ppermute | solution.py:34
  5.3 9.7 %collective-permute-start.1 = (bf16[2,2,256,128]{3,2,1,0:T(8,128)(2,1)S(1)}, bf16[2,2,256,128]{3,2,1,0:T(8,128)(2,1)S(1)}, u32[]{:S(2)}, u32[]{:S(2)}) collective-permute-start(bf16[2,2,256,128]{3,2,1,0:T(8,128)(2,1)S(1)} %get-tuple-element.44), channel_id=1, source_target_pairs={{0,8},{8,16},{16,24},{24,0},{1,9},{9,17},{17,25},{25,1},{2,10},{10... | collective-permute-start | bytes 786440 | tf_op jit(solution)/shard_map/ppermute | solution.py:34
  6.9 13.0 %collective-permute-start.3 = (bf16[2,2,256,128]{3,2,1,0:T(8,128)(2,1)S(1)}, bf16[2,2,256,128]{3,2,1,0:T(8,128)(2,1)S(1)}, u32[]{:S(2)}, u32[]{:S(2)}) collective-permute-start(bf16[2,2,256,128]{3,2,1,0:T(8,128)(2,1)S(1)} %get-tuple-element.46), channel_id=1, source_target_pairs={{0,24},{8,0},{16,8},{24,16},{1,25},{9,1},{17,9},{25,17},{2,26},{10... | collective-permute-start | bytes 786440 | tf_op jit(solution)/shard_map/ppermute | solution.py:34
  8.6 24.8 %collective-permute-start.2 = (bf16[2,2,256,128]{3,2,1,0:T(8,128)(2,1)S(1)}, bf16[2,2,256,128]{3,2,1,0:T(8,128)(2,1)S(1)}, u32[]{:S(2)}, u32[]{:S(2)}) collective-permute-start(bf16[2,2,256,128]{3,2,1,0:T(8,128)(2,1)S(1)} %get-tuple-element.45), channel_id=1, source_target_pairs={{0,16},{8,24},{16,0},{24,8},{1,17},{9,25},{17,1},{25,9},{2,18},{10... | collective-permute-start | bytes 786440 | tf_op jit(solution)/shard_map/ppermute | solution.py:34
  20.0 30.4 %collective-permute-start.8 = (bf16[2,2,2,256,128]{4,3,2,1,0:T(8,128)(2,1)S(1)}, bf16[2,2,2,256,128]{4,3,2,1,0:T(8,128)(2,1)S(1)}, u32[]{:S(2)}, u32[]{:S(2)}) collective-permute-start(bf16[2,2,2,256,128]{4,3,2,1,0:T(8,128)(2,1)S(1)} %pack.1), channel_id=1, source_target_pairs={{0,32},{32,64},{64,96},{96,128},{128,160},{160,192},{192,224},{224... | collective-permute-start | bytes 1572872 | tf_op jit(solution)/shard_map/ppermute | solution.py:34
  22.0 6.6 %collective-permute-start.4 = (bf16[2,256,128]{2,1,0:T(8,128)(2,1)S(1)}, bf16[2,256,128]{2,1,0:T(8,128)(2,1)S(1)}, u32[]{:S(2)}, u32[]{:S(2)}) collective-permute-start(bf16[2,256,128]{2,1,0:T(8,128)(2,1)S(1)} %get-tuple-element.48), channel_id=1, source_target_pairs={{0,8},{8,16},{16,24},{24,0},{1,9},{9,17},{17,25},{25,1},{2,10},{10... | collective-permute-start | bytes 393224 | tf_op jit(solution)/shard_map/ppermute | solution.py:34
  22.0 12.9 %collective-permute-start.5 = (bf16[2,256,128]{2,1,0:T(8,128)(2,1)S(1)}, bf16[2,256,128]{2,1,0:T(8,128)(2,1)S(1)}, u32[]{:S(2)}, u32[]{:S(2)}) collective-permute-start(bf16[2,256,128]{2,1,0:T(8,128)(2,1)S(1)} %get-tuple-element.49), channel_id=1, source_target_pairs={{0,16},{8,24},{16,0},{24,8},{1,17},{9,25},{17,1},{25,9},{2,18},{10... | collective-permute-start | bytes 393224 | tf_op jit(solution)/shard_map/ppermute | solution.py:34
  27.1 8.9 %collective-permute-start.6 = (bf16[2,256,128]{2,1,0:T(8,128)(2,1)S(1)}, bf16[2,256,128]{2,1,0:T(8,128)(2,1)S(1)}, u32[]{:S(2)}, u32[]{:S(2)}) collective-permute-start(bf16[2,256,128]{2,1,0:T(8,128)(2,1)S(1)} %get-tuple-element.50), channel_id=1, source_target_pairs={{0,24},{8,0},{16,8},{24,16},{1,25},{9,1},{17,9},{25,17},{2,26},{10... | collective-permute-start | bytes 393224 | tf_op jit(solution)/shard_map/ppermute | solution.py:34
  28.6 21.8 %collective-permute-start.7 = (bf16[2,2,256,128]{3,2,1,0:T(8,128)(2,1)S(1)}, bf16[2,2,256,128]{3,2,1,0:T(8,128)(2,1)S(1)}, u32[]{:S(2)}, u32[]{:S(2)}) collective-permute-start(bf16[2,2,256,128]{3,2,1,0:T(8,128)(2,1)S(1)} %get-tuple-element.43.refs_1_.refs_0_), channel_id=1, source_target_pairs={{0,32},{32,64},{64,96},{96,128},{128,160},{160,192},{192,224},{224... | collective-permute-start | bytes 786440 | tf_op jit(solution)/shard_map/ppermute | solution.py:34
  33.4 17.0 %collective-permute-start.9 = (bf16[2,2,256,128]{3,2,1,0:T(8,128)(2,1)S(1)}, bf16[2,2,256,128]{3,2,1,0:T(8,128)(2,1)S(1)}, u32[]{:S(2)}, u32[]{:S(2)}) collective-permute-start(bf16[2,2,256,128]{3,2,1,0:T(8,128)(2,1)S(1)} %collective-permute-done.2.refs_3_.refs_2_), channel_id=1, source_target_pairs={{0,32},{32,64},{64,96},{96,128},{128,160},{160,192},{192,224},{224... | collective-permute-start | bytes 786440 | tf_op jit(solution)/shard_map/ppermute | solution.py:34
  34.9 5.6 %collective-permute-start.10 = (bf16[136,128]{1,0:T(8,128)(2,1)S(1)}, bf16[136,128]{1,0:T(8,128)(2,1)S(1)}, u32[]{:S(2)}, u32[]{:S(2)}) collective-permute-start(bf16[136,128]{1,0:T(8,128)(2,1)S(1)} %get-tuple-element.59), channel_id=1, source_target_pairs={{0,224},{32,0},{64,32},{96,64},{128,96},{160,128},{192,160},{224,1... | collective-permute-start | bytes 104456 | tf_op jit(solution)/shard_map/ppermute | solution.py:34
  40.4 14.8 %copy-start = (f32[8]{0:T(128)S(1)}, f32[8]{0:T(128)}, u32[]{:S(2)}) copy-start(f32[8]{0:T(128)} %refs_1_.1) | copy-start | bytes 100
  41.0 6.3 %collective-permute-start.11 = (bf16[136,128]{1,0:T(8,128)(2,1)S(1)}, bf16[136,128]{1,0:T(8,128)(2,1)S(1)}, u32[]{:S(2)}, u32[]{:S(2)}) collective-permute-start(bf16[136,128]{1,0:T(8,128)(2,1)S(1)} %get-tuple-element.61), channel_id=1, source_target_pairs={{0,192},{32,224},{64,0},{96,32},{128,64},{160,96},{192,128},{224,1... | collective-permute-start | bytes 104456 | tf_op jit(solution)/shard_map/ppermute | solution.py:34
  47.4 7.9 %collective-permute-start.12 = (bf16[136,128]{1,0:T(8,128)(2,1)S(1)}, bf16[136,128]{1,0:T(8,128)(2,1)S(1)}, u32[]{:S(2)}, u32[]{:S(2)}) collective-permute-start(bf16[136,128]{1,0:T(8,128)(2,1)S(1)} %get-tuple-element.63), channel_id=1, source_target_pairs={{0,128},{32,160},{64,192},{96,224},{128,0},{160,32},{192,64},{224,... | collective-permute-start | bytes 104456 | tf_op jit(solution)/shard_map/ppermute | solution.py:34
  56.5 6.0 %collective-permute-start.13 = (bf16[2,256,128]{2,1,0:T(8,128)(2,1)S(1)}, bf16[2,256,128]{2,1,0:T(8,128)(2,1)S(1)}, u32[]{:S(2)}, u32[]{:S(2)}) collective-permute-start(bf16[2,256,128]{2,1,0:T(8,128)(2,1)S(1)} %get-tuple-element.65), channel_id=1, source_target_pairs={{0,24},{8,0},{16,8},{24,16},{1,25},{9,1},{17,9},{25,17},{2,26},{10... | collective-permute-start | bytes 393224 | tf_op jit(solution)/shard_map/ppermute | solution.py:34
  58.6 6.6 %collective-permute-start.14 = (bf16[2,256,128]{2,1,0:T(8,128)(2,1)S(1)}, bf16[2,256,128]{2,1,0:T(8,128)(2,1)S(1)}, u32[]{:S(2)}, u32[]{:S(2)}) collective-permute-start(bf16[2,256,128]{2,1,0:T(8,128)(2,1)S(1)} %get-tuple-element.66), channel_id=1, source_target_pairs={{0,16},{8,24},{16,0},{24,8},{1,17},{9,25},{17,1},{25,9},{2,18},{10... | collective-permute-start | bytes 393224 | tf_op jit(solution)/shard_map/ppermute | solution.py:34
  59.2 7.3 %collective-permute-start.15 = (bf16[2,256,128]{2,1,0:T(8,128)(2,1)S(1)}, bf16[2,256,128]{2,1,0:T(8,128)(2,1)S(1)}, u32[]{:S(2)}, u32[]{:S(2)}) collective-permute-start(bf16[2,256,128]{2,1,0:T(8,128)(2,1)S(1)} %get-tuple-element.67), channel_id=1, source_target_pairs={{0,8},{8,16},{16,24},{24,0},{1,9},{9,17},{17,25},{25,1},{2,10},{10... | collective-permute-start | bytes 393224 | tf_op jit(solution)/shard_map/ppermute | solution.py:34
  67.1 1.6 %collective-permute-start.16 = (bf16[4,256,128]{2,1,0:T(8,128)(2,1)S(1)}, bf16[4,256,128]{2,1,0:T(8,128)(2,1)S(1)}, u32[]{:S(2)}, u32[]{:S(2)}) collective-permute-start(bf16[4,256,128]{2,1,0:T(8,128)(2,1)S(1)} %turn.1), channel_id=1, source_target_pairs={{0,4},{4,0},{1,5},{5,1},{2,6},{6,2},{3,7},{7,3},{8,12},{12,8},{9,1... | collective-permute-start | bytes 786440 | tf_op jit(solution)/shard_map/ppermute | solution.py:34
  70.1 9.3 %collective-permute-start.21 = (bf16[128,1024]{1,0:T(8,128)(2,1)S(1)}, bf16[128,1024]{1,0:T(8,128)(2,1)S(1)}, u32[]{:S(2)}, u32[]{:S(2)}) collective-permute-start(bf16[128,1024]{1,0:T(8,128)(2,1)S(1)} %get-tuple-element.76), channel_id=1, source_target_pairs={{0,3},{1,0},{2,1},{3,2},{4,7},{5,4},{6,5},{7,6},{8,11},{9,8},{10,9... | collective-permute-start | bytes 786440 | tf_op jit(solution)/shard_map/ppermute | solution.py:34
  72.9 10.4 %collective-permute-start.18 = (bf16[128,1024]{1,0:T(8,128)(2,1)S(1)}, bf16[128,1024]{1,0:T(8,128)(2,1)S(1)}, u32[]{:S(2)}, u32[]{:S(2)}) collective-permute-start(bf16[128,1024]{1,0:T(8,128)(2,1)S(1)} %get-tuple-element.73), channel_id=1, source_target_pairs={{0,1},{1,2},{2,3},{3,0},{4,5},{5,6},{6,7},{7,4},{8,9},{9,10},{10,1... | collective-permute-start | bytes 786440 | tf_op jit(solution)/shard_map/ppermute | solution.py:34
  74.3 14.6 %collective-permute-start.20 = (bf16[128,1024]{1,0:T(8,128)(2,1)S(1)}, bf16[128,1024]{1,0:T(8,128)(2,1)S(1)}, u32[]{:S(2)}, u32[]{:S(2)}) collective-permute-start(bf16[128,1024]{1,0:T(8,128)(2,1)S(1)} %get-tuple-element.74), channel_id=1, source_target_pairs={{0,1},{1,2},{2,3},{3,0},{4,5},{5,6},{6,7},{7,4},{8,9},{9,10},{10,1... | collective-permute-start | bytes 786440 | tf_op jit(solution)/shard_map/ppermute | solution.py:34
  76.8 12.1 %collective-permute-start.17 = (bf16[128,1024]{1,0:T(8,128)(2,1)S(1)}, bf16[128,1024]{1,0:T(8,128)(2,1)S(1)}, u32[]{:S(2)}, u32[]{:S(2)}) collective-permute-start(bf16[128,1024]{1,0:T(8,128)(2,1)S(1)} %get-tuple-element.71), channel_id=1, source_target_pairs={{0,3},{1,0},{2,1},{3,2},{4,7},{5,4},{6,5},{7,6},{8,11},{9,8},{10,9... | collective-permute-start | bytes 786440 | tf_op jit(solution)/shard_map/ppermute | solution.py:34
  79.4 10.9 %collective-permute-start.22 = (bf16[128,1024]{1,0:T(8,128)(2,1)S(1)}, bf16[128,1024]{1,0:T(8,128)(2,1)S(1)}, u32[]{:S(2)}, u32[]{:S(2)}) collective-permute-start(bf16[128,1024]{1,0:T(8,128)(2,1)S(1)} %added.3), channel_id=1, source_target_pairs={{0,3},{1,0},{2,1},{3,2},{4,7},{5,4},{6,5},{7,6},{8,11},{9,8},{10,9... | collective-permute-start | bytes 786440 | tf_op jit(solution)/shard_map/ppermute | solution.py:34
  83.4 10.1 %collective-permute-start.19 = (bf16[128,1024]{1,0:T(8,128)(2,1)S(1)}, bf16[128,1024]{1,0:T(8,128)(2,1)S(1)}, u32[]{:S(2)}, u32[]{:S(2)}) collective-permute-start(bf16[128,1024]{1,0:T(8,128)(2,1)S(1)} %added.2), channel_id=1, source_target_pairs={{0,1},{1,2},{2,3},{3,0},{4,5},{5,6},{6,7},{7,4},{8,9},{9,10},{10,1... | collective-permute-start | bytes 786440 | tf_op jit(solution)/shard_map/ppermute | solution.py:34

commit v4 on v3

--- a/solution.py
+++ b/solution.py
@@ -201,10 +201,8 @@
 
 def own_first_kernel(*refs):
     here_ref, kvs, qs = refs[0], refs[1 : 1 + NY], refs[1 + NY : 1 + 2 * NY]
-    weight, keys, values, query, acc_out, peak_out, weight_out = refs[1 + 2 * NY : 8 + 2 * NY]
-    scores_a, scores_b, sem = refs[8 + 2 * NY :]
-    fetch = pltpu.make_async_copy(weight, weight_out, sem)
-    fetch.start()
+    keys, values, query, acc_out, peak_out = refs[1 + 2 * NY : 6 + 2 * NY]
+    scores_a, scores_b = refs[6 + 2 * NY :]
     here = here_ref[0]
     for step in range(NY):
         for half in range(2):
@@ -214,14 +212,13 @@
             query[rows, :] = qs[step][half]
     values[:, HD:] = jnp.ones((NB * BLK, HD), BF16)
     own_blocks(range(SPLIT), query, keys, values, (scores_a, scores_b), acc_out, peak_out)
-    fetch.wait()
 
 
 def own_second_kernel(keys, values, query, acc_out, peak_out, scores_a, scores_b):
     own_blocks(range(SPLIT, NB), query, keys, values, (scores_a, scores_b), acc_out, peak_out)
 
 
-def own_first(here, kvs, qs, weight):
+def own_first(here, kvs, qs):
     rows = NB * BLK
     return pl.pallas_call(
         own_first_kernel,
@@ -231,18 +228,16 @@
             jax.ShapeDtypeStruct((rows, HD), BF16),
             jax.ShapeDtypeStruct((SPLIT * BLK, 2 * HD), F32),
             jax.ShapeDtypeStruct((SPLIT * BLK, HD), F32),
-            jax.ShapeDtypeStruct(weight.shape, BF16),
         ),
-        in_specs=[SMEM] + [VMEM] * (2 * NY) + [HBM],
-        out_specs=(VMEM,) * 6,
+        in_specs=[SMEM] + [VMEM] * (2 * NY),
+        out_specs=(VMEM,) * 5,
         scratch_shapes=[
             pltpu.VMEM((BLK, SPLIT * BLK), F32),
             pltpu.VMEM((BLK, SPLIT * BLK), F32),
-            pltpu.SemaphoreType.DMA,
         ],
         name="own_first",
         **params(21 * BLK * BLK * HD * 8, 5 << 20),
-    )(here, *kvs, *qs, weight)
+    )(here, *kvs, *qs)
 
 
 def own_second(keys, values, query):
@@ -318,8 +313,10 @@
 
 def past_kernel(*refs):
     here_ref, same, near, far, query = refs[:5]
-    acc_a, peak_a, acc_b, peak_b, local_out = refs[5:10]
-    keys, values, scores_a, scores_b, acc_buf = refs[10:]
+    acc_a, peak_a, acc_b, peak_b, weight, local_out, weight_out = refs[5:12]
+    keys, values, scores_a, scores_b, acc_buf, sem = refs[12:]
+    fetch = pltpu.make_async_copy(weight, weight_out, sem)
+    fetch.start()
     here, segment = here_ref[0], here_ref[1]
 
     def own(b):
@@ -362,6 +359,7 @@
             acc_buf[rows, HD:] = acc[:, HD:] + acc_in[own_rows, HD:] * fade
 
     local_out[...] = acc_buf[:, :HD] / acc_buf[:, HD:]
+    fetch.wait()
 
 
 def blend_kernel(*refs):
@@ -388,23 +386,27 @@
             outs[step][half] = result[pair_rows(here, step, half), :]
 
 
-def past_part(here, past, query, own):
+def past_part(here, past, query, own, weight):
     rows = NB * BLK
     return pl.pallas_call(
         past_kernel,
-        out_shape=jax.ShapeDtypeStruct((rows, HD), F32),
-        in_specs=[SMEM] + [VMEM] * 8,
-        out_specs=VMEM,
+        out_shape=(
+            jax.ShapeDtypeStruct((rows, HD), F32),
+            jax.ShapeDtypeStruct(weight.shape, BF16),
+        ),
+        in_specs=[SMEM] + [VMEM] * 8 + [HBM],
+        out_specs=(VMEM, VMEM),
         scratch_shapes=[
             pltpu.VMEM((rows, HD), BF16),
             pltpu.VMEM((rows, 2 * HD), BF16),
             pltpu.VMEM((BLK, rows), F32),
             pltpu.VMEM((BLK, rows), F32),
             pltpu.VMEM((rows, 2 * HD), F32),
+            pltpu.SemaphoreType.DMA,
         ],
         name="past",
         **params(36 * BLK * BLK * HD * 8, 6 << 20, 24),
-    )(here, *past, query, *own)
+    )(here, *past, query, *own, weight)
 
 
 def blend(here, beta, query, local, memory):
@@ -518,10 +520,10 @@
     window, wire = window_step(kept, after)
     after = shifted(wire, "seq_0", -4)
 
-    k_all, v_all, q_all, acc_a, peak_a, weight = own_first(place(0), kvs, qs, w_out)
+    k_all, v_all, q_all, acc_a, peak_a = own_first(place(0), kvs, qs)
     acc_b, peak_b = own_second(k_all, v_all, q_all)
     own = (acc_a, peak_a, acc_b, peak_b)
-    local = past_part(place(0), past, q_all, own)
+    local, weight = past_part(place(0), past, q_all, own, w_out)
     attended = blend(place(0), beta, q_all, local, (window, after))
     heads = list(attended)
     for step in LEAVE:

time: 94.5 us -> 91.9 us (0.972)
  waiting for transfers between devices: 35.5 us -> 32.3 us
    ppermute x23, waiting for transfers between devices: 35.5 us -> 32.3 us  [shifted(): return lax.ppermute(block, axis, route)]
    pallas_call x1, Pallas kernels: 4.48 us -> 3.52 us  [own_first(): pl.pallas_call(own_first_kernel, out_shape=(jax.ShapeDtypeStruct((rows, H...]
where the time goes in v4:
time: 91.9 us; the launch traced here: 91 us
  starting transfers between devices  36.3 us (39%)
  waiting for transfers between devices  32.3 us (35%)
  Pallas kernels  22 us (24%)
    ppermute x23, starting transfers between devices, shifted(): return lax.ppermute(block, axis, route)  36.3 us
    ppermute x23, waiting for transfers between devices, shifted(): return lax.ppermute(block, axis, route)  32.3 us
    pallas_call x4, Pallas kernels, project(): pl.pallas_call(project_kernel, in_specs=[SMEM] + [VMEM] * (2 + NY), out_s...  5.57 us
    pallas_call x1, Pallas kernels, past_part(): pl.pallas_call(past_kernel, out_shape=(jax.ShapeDtypeStruct((rows, HD), F...  4.56 us
    pallas_call x1, Pallas kernels, own_first(): pl.pallas_call(own_first_kernel, out_shape=(jax.ShapeDtypeStruct((rows, H...  3.52 us
    pallas_call x1, Pallas kernels, split_heads(): pl.pallas_call(split_kernel, out_shape=(half, half), in_specs=[SMEM] + [H...  2.06 us
  transfers between devices with their start and end apart: 23, of which 14 were waited for; matrix products, arithmetic and copies ran while one was open for 0% of the time, Pallas kernels for 17%

profile of v4, /device:TPU:64, one launch (start us, length us, event | category | flops | bytes accessed | tf_op | source)
XLA Modules:
  0.0 91.0 jit_solution(12240941946304509789)
XLA Ops:
  0.2 2.1 %split.1 = (bf16[4,3,256,128]{3,2,1,0:T(8,128)(2,1)S(1)}, bf16[4,3,256,128]{3,2,1,0:T(8,128)(2,1)S(1)}) custom-call(s32[4]{0:T(128)S(1)} %get-tuple-element.83.here_ref.refs_0_.place_ref, bf16[256,1024]{1,0:T(8,128)(2,1)} %keys.1, bf16[256,1024]{1,0:T(8,128)(2,1)} %values.1, bf16[256,1024]{1,0:T(8,128)(2,1)} %queries.1), custom_call_target="tpu_custom_call" | custom-call | bytes 3145728 | tf_op jit(solution)/shard_map/split/pallas_call | solution.py:73
  2.3 2.3 %collective-permute-done.refs_2_ = bf16[4,3,256,128]{3,2,1,0:T(8,128)(2,1)S(1)} collective-permute-done((bf16[4,3,256,128]{3,2,1,0:T(8,128)(2,1)S(1)}, bf16[4,3,256,128]{3,2,1,0:T(8,128)(2,1)S(1)}, u32[]{:S(2)}, u32[]{:S(2)}) %collective-permute-start) | collective-permute-done | bytes 786464 | tf_op jit(solution)/shard_map/ppermute | solution.py:34
  5.3 1.7 %collective-permute-start.1 = (bf16[2,2,256,128]{3,2,1,0:T(8,128)(2,1)S(1)}, bf16[2,2,256,128]{3,2,1,0:T(8,128)(2,1)S(1)}, u32[]{:S(2)}, u32[]{:S(2)}) collective-permute-start(bf16[2,2,256,128]{3,2,1,0:T(8,128)(2,1)S(1)} %get-tuple-element.45), channel_id=1, source_target_pairs={{0,8},{8,16},{16,24},{24,0},{1,9},{9,17},{17,25},{25,1},{2,10},{10... | collective-permute-start | bytes 786440 | tf_op jit(solution)/shard_map/ppermute | solution.py:34
  6.9 1.7 %collective-permute-start.3 = (bf16[2,2,256,128]{3,2,1,0:T(8,128)(2,1)S(1)}, bf16[2,2,256,128]{3,2,1,0:T(8,128)(2,1)S(1)}, u32[]{:S(2)}, u32[]{:S(2)}) collective-permute-start(bf16[2,2,256,128]{3,2,1,0:T(8,128)(2,1)S(1)} %get-tuple-element.47), channel_id=1, source_target_pairs={{0,24},{8,0},{16,8},{24,16},{1,25},{9,1},{17,9},{25,17},{2,26},{10... | collective-permute-start | bytes 786440 | tf_op jit(solution)/shard_map/ppermute | solution.py:34
  8.6 2.0 %collective-permute-start.2 = (bf16[2,2,256,128]{3,2,1,0:T(8,128)(2,1)S(1)}, bf16[2,2,256,128]{3,2,1,0:T(8,128)(2,1)S(1)}, u32[]{:S(2)}, u32[]{:S(2)}) collective-permute-start(bf16[2,2,256,128]{3,2,1,0:T(8,128)(2,1)S(1)} %get-tuple-element.46), channel_id=1, source_target_pairs={{0,16},{8,24},{16,0},{24,8},{1,17},{9,25},{17,1},{25,9},{2,18},{10... | collective-permute-start | bytes 786440 | tf_op jit(solution)/shard_map/ppermute | solution.py:34
  10.6 4.4 %collective-permute-done.1.refs_2_.first.refs_1_ = bf16[2,2,256,128]{3,2,1,0:T(8,128)(2,1)S(1)} collective-permute-done((bf16[2,2,256,128]{3,2,1,0:T(8,128)(2,1)S(1)}, bf16[2,2,256,128]{3,2,1,0:T(8,128)(2,1)S(1)}, u32[]{:S(2)}, u32[]{:S(2)}) %collective-permute-start.1) | collective-permute-done | bytes 262176 | tf_op jit(solution)/shard_map/ppermute | solution.py:34
  15.0 5.0 %collective-permute-done.3.refs_4_.second.refs_3_ = bf16[2,2,256,128]{3,2,1,0:T(8,128)(2,1)S(1)} collective-permute-done((bf16[2,2,256,128]{3,2,1,0:T(8,128)(2,1)S(1)}, bf16[2,2,256,128]{3,2,1,0:T(8,128)(2,1)S(1)}, u32[]{:S(2)}, u32[]{:S(2)}) %collective-permute-start.3) | collective-permute-done | bytes 262176 | tf_op jit(solution)/shard_map/ppermute | solution.py:34
  20.0 2.0 %collective-permute-start.8 = (bf16[2,2,2,256,128]{4,3,2,1,0:T(8,128)(2,1)S(1)}, bf16[2,2,2,256,128]{4,3,2,1,0:T(8,128)(2,1)S(1)}, u32[]{:S(2)}, u32[]{:S(2)}) collective-permute-start(bf16[2,2,2,256,128]{4,3,2,1,0:T(8,128)(2,1)S(1)} %pack.1), channel_id=1, source_target_pairs={{0,32},{32,64},{64,96},{96,128},{128,160},{160,192},{192,224},{224... | collective-permute-start | bytes 1572872 | tf_op jit(solution)/shard_map/ppermute | solution.py:34
  22.0 5.1 %collective-permute-start.5 = (bf16[2,256,128]{2,1,0:T(8,128)(2,1)S(1)}, bf16[2,256,128]{2,1,0:T(8,128)(2,1)S(1)}, u32[]{:S(2)}, u32[]{:S(2)}) collective-permute-start(bf16[2,256,128]{2,1,0:T(8,128)(2,1)S(1)} %get-tuple-element.50), channel_id=1, source_target_pairs={{0,16},{8,24},{16,0},{24,8},{1,17},{9,25},{17,1},{25,9},{2,18},{10... | collective-permute-start | bytes 393224 | tf_op jit(solution)/shard_map/ppermute | solution.py:34
  28.6 4.8 %collective-permute-start.7 = (bf16[2,2,256,128]{3,2,1,0:T(8,128)(2,1)S(1)}, bf16[2,2,256,128]{3,2,1,0:T(8,128)(2,1)S(1)}, u32[]{:S(2)}, u32[]{:S(2)}) collective-permute-start(bf16[2,2,256,128]{3,2,1,0:T(8,128)(2,1)S(1)} %get-tuple-element.44.refs_1_.refs_0_), channel_id=1, source_target_pairs={{0,32},{32,64},{64,96},{96,128},{128,160},{160,192},{192,224},{224... | collective-permute-start | bytes 786440 | tf_op jit(solution)/shard_map/ppermute | solution.py:34
  36.0 3.5 %own_first.1 = (bf16[2048,128]{1,0:T(8,128)(2,1)S(1)}, bf16[2048,256]{1,0:T(8,128)(2,1)S(1)}, bf16[2048,128]{1,0:T(8,128)(2,1)S(1)}, f32[1536,256]{1,0:T(8,128)S(1)}, f32[1536,128]{1,0:T(8,128)S(1)}) custom-call(s32[4]{0:T(128)S(1)} %get-tuple-element.83.here_ref.refs_0_.place_ref, bf16[2,2,256,128]{3,2,1,0:T(8,128)(2,1)S(1)} %get-tuple-element.44.refs_1_.refs_0_, ...), custom_call_target="tpu_custom_call" | custom-call | flops 1409286144 | bytes 5242880 | tf_op jit(solution)/shard_map/own_first/pallas_call | solution.py:223
  40.4 1.7 %own_second.1 = (f32[512,256]{1,0:T(8,128)S(1)}, f32[512,128]{1,0:T(8,128)S(1)}) custom-call(bf16[2048,128]{1,0:T(8,128)(2,1)S(1)} %get-tuple-element.55.keys, bf16[2048,256]{1,0:T(8,128)(2,1)S(1)} %get-tuple-element.56.values, bf16[2048,128]{1,0:T(8,128)(2,1)S(1)} %get-tuple-element.52.query.refs_4_.refs_2_), custom_call_target="tpu_custom_call" | custom-call | flops 1006632960 | bytes 3145728 | tf_op jit(solution)/shard_map/own_second/pallas_call | solution.py:245
  42.1 4.3 %collective-permute-done.11.after = bf16[136,128]{1,0:T(8,128)(2,1)S(1)} collective-permute-done((bf16[136,128]{1,0:T(8,128)(2,1)S(1)}, bf16[136,128]{1,0:T(8,128)(2,1)S(1)}, u32[]{:S(2)}, u32[]{:S(2)}) %collective-permute-start.11) | collective-permute-done | bytes 34848 | tf_op jit(solution)/shard_map/ppermute | solution.py:34
  46.4 3.0 %collective-permute-start.12 = (bf16[136,128]{1,0:T(8,128)(2,1)S(1)}, bf16[136,128]{1,0:T(8,128)(2,1)S(1)}, u32[]{:S(2)}, u32[]{:S(2)}) collective-permute-start(bf16[136,128]{1,0:T(8,128)(2,1)S(1)} %get-tuple-element.65), channel_id=1, source_target_pairs={{0,128},{32,160},{64,192},{96,224},{128,0},{160,32},{192,64},{224,... | collective-permute-start | bytes 104456 | tf_op jit(solution)/shard_map/ppermute | solution.py:34
  49.4 4.6 %past.1 = (f32[2048,128]{1,0:T(8,128)S(1)}, bf16[1024,4096]{1,0:T(8,128)(2,1)S(1)}) custom-call(s32[4]{0:T(128)S(1)} %get-tuple-element.83.here_ref.refs_0_.place_ref, bf16[2,2,256,128]{3,2,1,0:T(8,128)(2,1)S(1)} %collective-permute-done.7.refs_1_, bf16[2,2,2,256,128]{4,3,2,1,0:T(8,128)(2,1)S(1)} %collective-permute-done.8.refs_2_, ...), custom_call_target="tpu_custom_call" | custom-call | flops 2415919104 | bytes 6291456 | tf_op jit(solution)/shard_map/past/pallas_call | solution.py:391
  55.5 2.1 %collective-permute-start.13 = (bf16[2,256,128]{2,1,0:T(8,128)(2,1)S(1)}, bf16[2,256,128]{2,1,0:T(8,128)(2,1)S(1)}, u32[]{:S(2)}, u32[]{:S(2)}) collective-permute-start(bf16[2,256,128]{2,1,0:T(8,128)(2,1)S(1)} %get-tuple-element.67), channel_id=1, source_target_pairs={{0,24},{8,0},{16,8},{24,16},{1,25},{9,1},{17,9},{25,17},{2,26},{10... | collective-permute-start | bytes 393224 | tf_op jit(solution)/shard_map/ppermute | solution.py:34
  58.7 2.8 %collective-permute-done.13.refs_2_ = bf16[2,256,128]{2,1,0:T(8,128)(2,1)S(1)} collective-permute-done((bf16[2,256,128]{2,1,0:T(8,128)(2,1)S(1)}, bf16[2,256,128]{2,1,0:T(8,128)(2,1)S(1)}, u32[]{:S(2)}, u32[]{:S(2)}) %collective-permute-start.13) | collective-permute-done | bytes 131104 | tf_op jit(solution)/shard_map/ppermute | solution.py:34
  61.6 2.6 %collective-permute-done.14.refs_3_ = bf16[2,256,128]{2,1,0:T(8,128)(2,1)S(1)} collective-permute-done((bf16[2,256,128]{2,1,0:T(8,128)(2,1)S(1)}, bf16[2,256,128]{2,1,0:T(8,128)(2,1)S(1)}, u32[]{:S(2)}, u32[]{:S(2)}) %collective-permute-start.14) | collective-permute-done | bytes 131104 | tf_op jit(solution)/shard_map/ppermute | solution.py:34
  66.2 1.5 %collective-permute-done.16.refs_5_ = bf16[4,256,128]{2,1,0:T(8,128)(2,1)S(1)} collective-permute-done((bf16[4,256,128]{2,1,0:T(8,128)(2,1)S(1)}, bf16[4,256,128]{2,1,0:T(8,128)(2,1)S(1)}, u32[]{:S(2)}, u32[]{:S(2)}) %collective-permute-start.16) | collective-permute-done | bytes 262176 | tf_op jit(solution)/shard_map/ppermute | solution.py:34
  69.1 1.6 %collective-permute-start.18 = (bf16[128,1024]{1,0:T(8,128)(2,1)S(1)}, bf16[128,1024]{1,0:T(8,128)(2,1)S(1)}, u32[]{:S(2)}, u32[]{:S(2)}) collective-permute-start(bf16[128,1024]{1,0:T(8,128)(2,1)S(1)} %get-tuple-element.75), channel_id=1, source_target_pairs={{0,1},{1,2},{2,3},{3,0},{4,5},{5,6},{6,7},{7,4},{8,9},{9,10},{10,1... | collective-permute-start | bytes 786440 | tf_op jit(solution)/shard_map/ppermute | solution.py:34
  70.7 1.7 %collective-permute-start.21 = (bf16[128,1024]{1,0:T(8,128)(2,1)S(1)}, bf16[128,1024]{1,0:T(8,128)(2,1)S(1)}, u32[]{:S(2)}, u32[]{:S(2)}) collective-permute-start(bf16[128,1024]{1,0:T(8,128)(2,1)S(1)} %get-tuple-element.78), channel_id=1, source_target_pairs={{0,3},{1,0},{2,1},{3,2},{4,7},{5,4},{6,5},{7,6},{8,11},{9,8},{10,9... | collective-permute-start | bytes 786440 | tf_op jit(solution)/shard_map/ppermute | solution.py:34
  75.8 3.0 %collective-permute-start.17 = (bf16[128,1024]{1,0:T(8,128)(2,1)S(1)}, bf16[128,1024]{1,0:T(8,128)(2,1)S(1)}, u32[]{:S(2)}, u32[]{:S(2)}) collective-permute-start(bf16[128,1024]{1,0:T(8,128)(2,1)S(1)} %get-tuple-element.73), channel_id=1, source_target_pairs={{0,3},{1,0},{2,1},{3,2},{4,7},{5,4},{6,5},{7,6},{8,11},{9,8},{10,9... | collective-permute-start | bytes 786440 | tf_op jit(solution)/shard_map/ppermute | solution.py:34
  80.1 3.0 %collective-permute-start.22 = (bf16[128,1024]{1,0:T(8,128)(2,1)S(1)}, bf16[128,1024]{1,0:T(8,128)(2,1)S(1)}, u32[]{:S(2)}, u32[]{:S(2)}) collective-permute-start(bf16[128,1024]{1,0:T(8,128)(2,1)S(1)} %added.3), channel_id=1, source_target_pairs={{0,3},{1,0},{2,1},{3,2},{4,7},{5,4},{6,5},{7,6},{8,11},{9,8},{10,9... | collective-permute-start | bytes 786440 | tf_op jit(solution)/shard_map/ppermute | solution.py:34
  85.6 4.5 %collective-permute-done.19.up_b = bf16[128,1024]{1,0:T(8,128)(2,1)S(1)} collective-permute-done((bf16[128,1024]{1,0:T(8,128)(2,1)S(1)}, bf16[128,1024]{1,0:T(8,128)(2,1)S(1)}, u32[]{:S(2)}, u32[]{:S(2)}) %collective-permute-start.19) | collective-permute-done | bytes 262176 | tf_op jit(solution)/shard_map/ppermute | solution.py:34
  (44 shorter events, 19.8 us)
Async XLA Ops:
  2.2 2.4 %collective-permute-start = (bf16[4,3,256,128]{3,2,1,0:T(8,128)(2,1)S(1)}, bf16[4,3,256,128]{3,2,1,0:T(8,128)(2,1)S(1)}, u32[]{:S(2)}, u32[]{:S(2)}) collective-permute-start(bf16[4,3,256,128]{3,2,1,0:T(8,128)(2,1)S(1)} %get-tuple-element.43), channel_id=1, source_target_pairs={{0,4},{4,0},{1,5},{5,1},{2,6},{6,2},{3,7},{7,3},{8,12},{12,8},{9,1... | collective-permute-start | bytes 2359304 | tf_op jit(solution)/shard_map/ppermute | solution.py:34
  5.3 9.7 %collective-permute-start.1 = (bf16[2,2,256,128]{3,2,1,0:T(8,128)(2,1)S(1)}, bf16[2,2,256,128]{3,2,1,0:T(8,128)(2,1)S(1)}, u32[]{:S(2)}, u32[]{:S(2)}) collective-permute-start(bf16[2,2,256,128]{3,2,1,0:T(8,128)(2,1)S(1)} %get-tuple-element.45), channel_id=1, source_target_pairs={{0,8},{8,16},{16,24},{24,0},{1,9},{9,17},{17,25},{25,1},{2,10},{10... | collective-permute-start | bytes 786440 | tf_op jit(solution)/shard_map/ppermute | solution.py:34
  6.9 13.0 %collective-permute-start.3 = (bf16[2,2,256,128]{3,2,1,0:T(8,128)(2,1)S(1)}, bf16[2,2,256,128]{3,2,1,0:T(8,128)(2,1)S(1)}, u32[]{:S(2)}, u32[]{:S(2)}) collective-permute-start(bf16[2,2,256,128]{3,2,1,0:T(8,128)(2,1)S(1)} %get-tuple-element.47), channel_id=1, source_target_pairs={{0,24},{8,0},{16,8},{24,16},{1,25},{9,1},{17,9},{25,17},{2,26},{10... | collective-permute-start | bytes 786440 | tf_op jit(solution)/shard_map/ppermute | solution.py:34
  8.6 24.8 %collective-permute-start.2 = (bf16[2,2,256,128]{3,2,1,0:T(8,128)(2,1)S(1)}, bf16[2,2,256,128]{3,2,1,0:T(8,128)(2,1)S(1)}, u32[]{:S(2)}, u32[]{:S(2)}) collective-permute-start(bf16[2,2,256,128]{3,2,1,0:T(8,128)(2,1)S(1)} %get-tuple-element.46), channel_id=1, source_target_pairs={{0,16},{8,24},{16,0},{24,8},{1,17},{9,25},{17,1},{25,9},{2,18},{10... | collective-permute-start | bytes 786440 | tf_op jit(solution)/shard_map/ppermute | solution.py:34
  20.0 29.4 %collective-permute-start.8 = (bf16[2,2,2,256,128]{4,3,2,1,0:T(8,128)(2,1)S(1)}, bf16[2,2,2,256,128]{4,3,2,1,0:T(8,128)(2,1)S(1)}, u32[]{:S(2)}, u32[]{:S(2)}) collective-permute-start(bf16[2,2,2,256,128]{4,3,2,1,0:T(8,128)(2,1)S(1)} %pack.1), channel_id=1, source_target_pairs={{0,32},{32,64},{64,96},{96,128},{128,160},{160,192},{192,224},{224... | collective-permute-start | bytes 1572872 | tf_op jit(solution)/shard_map/ppermute | solution.py:34
  22.0 6.6 %collective-permute-start.4 = (bf16[2,256,128]{2,1,0:T(8,128)(2,1)S(1)}, bf16[2,256,128]{2,1,0:T(8,128)(2,1)S(1)}, u32[]{:S(2)}, u32[]{:S(2)}) collective-permute-start(bf16[2,256,128]{2,1,0:T(8,128)(2,1)S(1)} %get-tuple-element.49), channel_id=1, source_target_pairs={{0,8},{8,16},{16,24},{24,0},{1,9},{9,17},{17,25},{25,1},{2,10},{10... | collective-permute-start | bytes 393224 | tf_op jit(solution)/shard_map/ppermute | solution.py:34
  22.0 12.9 %collective-permute-start.5 = (bf16[2,256,128]{2,1,0:T(8,128)(2,1)S(1)}, bf16[2,256,128]{2,1,0:T(8,128)(2,1)S(1)}, u32[]{:S(2)}, u32[]{:S(2)}) collective-permute-start(bf16[2,256,128]{2,1,0:T(8,128)(2,1)S(1)} %get-tuple-element.50), channel_id=1, source_target_pairs={{0,16},{8,24},{16,0},{24,8},{1,17},{9,25},{17,1},{25,9},{2,18},{10... | collective-permute-start | bytes 393224 | tf_op jit(solution)/shard_map/ppermute | solution.py:34
  27.1 8.9 %collective-permute-start.6 = (bf16[2,256,128]{2,1,0:T(8,128)(2,1)S(1)}, bf16[2,256,128]{2,1,0:T(8,128)(2,1)S(1)}, u32[]{:S(2)}, u32[]{:S(2)}) collective-permute-start(bf16[2,256,128]{2,1,0:T(8,128)(2,1)S(1)} %get-tuple-element.51), channel_id=1, source_target_pairs={{0,24},{8,0},{16,8},{24,16},{1,25},{9,1},{17,9},{25,17},{2,26},{10... | collective-permute-start | bytes 393224 | tf_op jit(solution)/shard_map/ppermute | solution.py:34
  28.6 20.8 %collective-permute-start.7 = (bf16[2,2,256,128]{3,2,1,0:T(8,128)(2,1)S(1)}, bf16[2,2,256,128]{3,2,1,0:T(8,128)(2,1)S(1)}, u32[]{:S(2)}, u32[]{:S(2)}) collective-permute-start(bf16[2,2,256,128]{3,2,1,0:T(8,128)(2,1)S(1)} %get-tuple-element.44.refs_1_.refs_0_), channel_id=1, source_target_pairs={{0,32},{32,64},{64,96},{96,128},{128,160},{160,192},{192,224},{224... | collective-permute-start | bytes 786440 | tf_op jit(solution)/shard_map/ppermute | solution.py:34
  33.4 16.0 %collective-permute-start.9 = (bf16[2,2,256,128]{3,2,1,0:T(8,128)(2,1)S(1)}, bf16[2,2,256,128]{3,2,1,0:T(8,128)(2,1)S(1)}, u32[]{:S(2)}, u32[]{:S(2)}) collective-permute-start(bf16[2,2,256,128]{3,2,1,0:T(8,128)(2,1)S(1)} %collective-permute-done.2.refs_3_.refs_2_), channel_id=1, source_target_pairs={{0,32},{32,64},{64,96},{96,128},{128,160},{160,192},{192,224},{224... | collective-permute-start | bytes 786440 | tf_op jit(solution)/shard_map/ppermute | solution.py:34
  34.9 4.6 %collective-permute-start.10 = (bf16[136,128]{1,0:T(8,128)(2,1)S(1)}, bf16[136,128]{1,0:T(8,128)(2,1)S(1)}, u32[]{:S(2)}, u32[]{:S(2)}) collective-permute-start(bf16[136,128]{1,0:T(8,128)(2,1)S(1)} %get-tuple-element.61), channel_id=1, source_target_pairs={{0,224},{32,0},{64,32},{96,64},{128,96},{160,128},{192,160},{224,1... | collective-permute-start | bytes 104456 | tf_op jit(solution)/shard_map/ppermute | solution.py:34
  40.1 6.3 %collective-permute-start.11 = (bf16[136,128]{1,0:T(8,128)(2,1)S(1)}, bf16[136,128]{1,0:T(8,128)(2,1)S(1)}, u32[]{:S(2)}, u32[]{:S(2)}) collective-permute-start(bf16[136,128]{1,0:T(8,128)(2,1)S(1)} %get-tuple-element.63), channel_id=1, source_target_pairs={{0,192},{32,224},{64,0},{96,32},{128,64},{160,96},{192,128},{224,1... | collective-permute-start | bytes 104456 | tf_op jit(solution)/shard_map/ppermute | solution.py:34
  40.3 14.0 %copy-start = (f32[8]{0:T(128)S(1)}, f32[8]{0:T(128)}, u32[]{:S(2)}) copy-start(f32[8]{0:T(128)} %refs_1_.1) | copy-start | bytes 100
  46.4 7.9 %collective-permute-start.12 = (bf16[136,128]{1,0:T(8,128)(2,1)S(1)}, bf16[136,128]{1,0:T(8,128)(2,1)S(1)}, u32[]{:S(2)}, u32[]{:S(2)}) collective-permute-start(bf16[136,128]{1,0:T(8,128)(2,1)S(1)} %get-tuple-element.65), channel_id=1, source_target_pairs={{0,128},{32,160},{64,192},{96,224},{128,0},{160,32},{192,64},{224,... | collective-permute-start | bytes 104456 | tf_op jit(solution)/shard_map/ppermute | solution.py:34
  55.5 6.0 %collective-permute-start.13 = (bf16[2,256,128]{2,1,0:T(8,128)(2,1)S(1)}, bf16[2,256,128]{2,1,0:T(8,128)(2,1)S(1)}, u32[]{:S(2)}, u32[]{:S(2)}) collective-permute-start(bf16[2,256,128]{2,1,0:T(8,128)(2,1)S(1)} %get-tuple-element.67), channel_id=1, source_target_pairs={{0,24},{8,0},{16,8},{24,16},{1,25},{9,1},{17,9},{25,17},{2,26},{10... | collective-permute-start | bytes 393224 | tf_op jit(solution)/shard_map/ppermute | solution.py:34
  57.7 6.6 %collective-permute-start.14 = (bf16[2,256,128]{2,1,0:T(8,128)(2,1)S(1)}, bf16[2,256,128]{2,1,0:T(8,128)(2,1)S(1)}, u32[]{:S(2)}, u32[]{:S(2)}) collective-permute-start(bf16[2,256,128]{2,1,0:T(8,128)(2,1)S(1)} %get-tuple-element.68), channel_id=1, source_target_pairs={{0,16},{8,24},{16,0},{24,8},{1,17},{9,25},{17,1},{25,9},{2,18},{10... | collective-permute-start | bytes 393224 | tf_op jit(solution)/shard_map/ppermute | solution.py:34
  58.2 7.3 %collective-permute-start.15 = (bf16[2,256,128]{2,1,0:T(8,128)(2,1)S(1)}, bf16[2,256,128]{2,1,0:T(8,128)(2,1)S(1)}, u32[]{:S(2)}, u32[]{:S(2)}) collective-permute-start(bf16[2,256,128]{2,1,0:T(8,128)(2,1)S(1)} %get-tuple-element.69), channel_id=1, source_target_pairs={{0,8},{8,16},{16,24},{24,0},{1,9},{9,17},{17,25},{25,1},{2,10},{10... | collective-permute-start | bytes 393224 | tf_op jit(solution)/shard_map/ppermute | solution.py:34
  66.1 1.6 %collective-permute-start.16 = (bf16[4,256,128]{2,1,0:T(8,128)(2,1)S(1)}, bf16[4,256,128]{2,1,0:T(8,128)(2,1)S(1)}, u32[]{:S(2)}, u32[]{:S(2)}) collective-permute-start(bf16[4,256,128]{2,1,0:T(8,128)(2,1)S(1)} %turn.1), channel_id=1, source_target_pairs={{0,4},{4,0},{1,5},{5,1},{2,6},{6,2},{3,7},{7,3},{8,12},{12,8},{9,1... | collective-permute-start | bytes 786440 | tf_op jit(solution)/shard_map/ppermute | solution.py:34
  69.1 10.5 %collective-permute-start.18 = (bf16[128,1024]{1,0:T(8,128)(2,1)S(1)}, bf16[128,1024]{1,0:T(8,128)(2,1)S(1)}, u32[]{:S(2)}, u32[]{:S(2)}) collective-permute-start(bf16[128,1024]{1,0:T(8,128)(2,1)S(1)} %get-tuple-element.75), channel_id=1, source_target_pairs={{0,1},{1,2},{2,3},{3,0},{4,5},{5,6},{6,7},{7,4},{8,9},{9,10},{10,1... | collective-permute-start | bytes 786440 | tf_op jit(solution)/shard_map/ppermute | solution.py:34
  70.7 9.3 %collective-permute-start.21 = (bf16[128,1024]{1,0:T(8,128)(2,1)S(1)}, bf16[128,1024]{1,0:T(8,128)(2,1)S(1)}, u32[]{:S(2)}, u32[]{:S(2)}) collective-permute-start(bf16[128,1024]{1,0:T(8,128)(2,1)S(1)} %get-tuple-element.78), channel_id=1, source_target_pairs={{0,3},{1,0},{2,1},{3,2},{4,7},{5,4},{6,5},{7,6},{8,11},{9,8},{10,9... | collective-permute-start | bytes 786440 | tf_op jit(solution)/shard_map/ppermute | solution.py:34
  73.8 11.4 %collective-permute-start.20 = (bf16[128,1024]{1,0:T(8,128)(2,1)S(1)}, bf16[128,1024]{1,0:T(8,128)(2,1)S(1)}, u32[]{:S(2)}, u32[]{:S(2)}) collective-permute-start(bf16[128,1024]{1,0:T(8,128)(2,1)S(1)} %get-tuple-element.76), channel_id=1, source_target_pairs={{0,1},{1,2},{2,3},{3,0},{4,5},{5,6},{6,7},{7,4},{8,9},{9,10},{10,1... | collective-permute-start | bytes 786440 | tf_op jit(solution)/shard_map/ppermute | solution.py:34
  75.8 9.7 %collective-permute-start.17 = (bf16[128,1024]{1,0:T(8,128)(2,1)S(1)}, bf16[128,1024]{1,0:T(8,128)(2,1)S(1)}, u32[]{:S(2)}, u32[]{:S(2)}) collective-permute-start(bf16[128,1024]{1,0:T(8,128)(2,1)S(1)} %get-tuple-element.73), channel_id=1, source_target_pairs={{0,3},{1,0},{2,1},{3,2},{4,7},{5,4},{6,5},{7,6},{8,11},{9,8},{10,9... | collective-permute-start | bytes 786440 | tf_op jit(solution)/shard_map/ppermute | solution.py:34
  79.6 10.4 %collective-permute-start.19 = (bf16[128,1024]{1,0:T(8,128)(2,1)S(1)}, bf16[128,1024]{1,0:T(8,128)(2,1)S(1)}, u32[]{:S(2)}, u32[]{:S(2)}) collective-permute-start(bf16[128,1024]{1,0:T(8,128)(2,1)S(1)} %added.2), channel_id=1, source_target_pairs={{0,1},{1,2},{2,3},{3,0},{4,5},{5,6},{6,7},{7,4},{8,9},{9,10},{10,1... | collective-permute-start | bytes 786440 | tf_op jit(solution)/shard_map/ppermute | solution.py:34
  80.1 10.0 %collective-permute-start.22 = (bf16[128,1024]{1,0:T(8,128)(2,1)S(1)}, bf16[128,1024]{1,0:T(8,128)(2,1)S(1)}, u32[]{:S(2)}, u32[]{:S(2)}) collective-permute-start(bf16[128,1024]{1,0:T(8,128)(2,1)S(1)} %added.3), channel_id=1, source_target_pairs={{0,3},{1,0},{2,1},{3,2},{4,7},{5,4},{6,5},{7,6},{8,11},{9,8},{10,9... | collective-permute-start | bytes 786440 | tf_op jit(solution)/shard_map/ppermute | solution.py:34

commit v5 on v4

--- a/solution.py
+++ b/solution.py
@@ -50,7 +50,7 @@
     )
 
 
-def split_kernel(here_ref, keys, values, queries, stay, leave, whole, sems):
+def split_kernel(here_ref, keys, values, queries, whole, leave, sems):
     here = here_ref[0]
     copies = [
         pltpu.make_async_copy(array, whole.at[n], sems.at[n])
@@ -63,35 +63,36 @@
         copy.wait()
         for step in range(NY):
             pair = lax.rem(here // 2 + step, NY) * 2
-            for out, core in ((leave, 1 - own_core), (stay, own_core)):
-                cols = pl.ds(pl.multiple_of((pair + core) * HD, HD), HD)
-                out[step, n] = whole[n, :, cols]
+            cols = pl.ds(pl.multiple_of((pair + 1 - own_core) * HD, HD), HD)
+            leave[step, n] = whole[n, :, cols]
 
 
 def split_heads(here, keys, values, queries):
-    half = jax.ShapeDtypeStruct((NY, 3, BLK, HD), BF16)
     return pl.pallas_call(
         split_kernel,
-        out_shape=(half, half),
+        out_shape=(
+            jax.ShapeDtypeStruct((3, BLK, NB * HD), BF16),
+            jax.ShapeDtypeStruct((NY, 3, BLK, HD), BF16),
+        ),
         in_specs=[SMEM] + [HBM] * 3,
         out_specs=(VMEM, VMEM),
-        scratch_shapes=[
-            pltpu.VMEM((3, BLK, NB * HD), BF16),
-            pltpu.SemaphoreType.DMA((3,)),
-        ],
+        scratch_shapes=[pltpu.SemaphoreType.DMA((3,))],
         name="split",
         **params(0, 3 << 20),
     )(here, keys, values, queries)
 
 
 def pair_kernel(*refs):
-    here_ref, stay, got = refs[:3]
+    here_ref, whole, got = refs[:3]
     kvs, qs = refs[3 : 3 + NY], refs[3 + NY : 3 + 2 * NY]
     core = lax.rem(here_ref[0], 2)
     for step in range(NY):
-        for part, half in ((stay, core), (got, 1 - core)):
-            kvs[step][half] = part[step, 0:2]
-            qs[step][half] = part[step, 2]
+        pair = lax.rem(here_ref[0] // 2 + step, NY) * 2
+        cols = pl.ds(pl.multiple_of((pair + core) * HD, HD), HD)
+        kvs[step][core] = whole[0:2, :, cols]
+        qs[step][core] = whole[2, :, cols]
+        kvs[step][1 - core] = got[step, 0:2]
+        qs[step][1 - core] = got[step, 2]
 
 
 def pair_up(here, stay, got):

time: 91.9 us -> 92 us (level)
  no operation moved by 1% of the time
where the time goes in v5:
time: 92 us; the launch traced here: 91.1 us
  starting transfers between devices  36.3 us (39%)
  waiting for transfers between devices  32.3 us (35%)
  Pallas kernels  22.1 us (24%)
    ppermute x23, starting transfers between devices, shifted(): return lax.ppermute(block, axis, route)  36.3 us
    ppermute x23, waiting for transfers between devices, shifted(): return lax.ppermute(block, axis, route)  32.3 us
    pallas_call x4, Pallas kernels, project(): pl.pallas_call(project_kernel, in_specs=[SMEM] + [VMEM] * (2 + NY), out_s...  5.57 us
    pallas_call x1, Pallas kernels, past_part(): pl.pallas_call(past_kernel, out_shape=(jax.ShapeDtypeStruct((rows, HD), F...  4.56 us
    pallas_call x1, Pallas kernels, own_first(): pl.pallas_call(own_first_kernel, out_shape=(jax.ShapeDtypeStruct((rows, H...  3.54 us
    pallas_call x1, Pallas kernels, split_heads(): pl.pallas_call(split_kernel, out_shape=(jax.ShapeDtypeStruct((3, BLK, NB...  1.99 us
  transfers between devices with their start and end apart: 23, of which 14 were waited for; matrix products, arithmetic and copies ran while one was open for 0% of the time, Pallas kernels for 17%

profile of v5, /device:TPU:64, one launch (start us, length us, event | category | flops | bytes accessed | tf_op | source)
XLA Modules:
  0.0 91.1 jit_solution(10100878965470661654)
XLA Ops:
  0.2 2.0 %split.1 = (bf16[3,256,1024]{2,1,0:T(8,128)(2,1)S(1)}, bf16[4,3,256,128]{3,2,1,0:T(8,128)(2,1)S(1)}) custom-call(s32[4]{0:T(128)S(1)} %get-tuple-element.83.here_ref.refs_0_.place_ref, bf16[256,1024]{1,0:T(8,128)(2,1)} %keys.1, bf16[256,1024]{1,0:T(8,128)(2,1)} %values.1, bf16[256,1024]{1,0:T(8,128)(2,1)} %queries.1), custom_call_target="tpu_custom_call" | custom-call | bytes 3145728 | tf_op jit(solution)/shard_map/split/pallas_call | solution.py:71
  2.3 2.3 %collective-permute-done.refs_2_ = bf16[4,3,256,128]{3,2,1,0:T(8,128)(2,1)S(1)} collective-permute-done((bf16[4,3,256,128]{3,2,1,0:T(8,128)(2,1)S(1)}, bf16[4,3,256,128]{3,2,1,0:T(8,128)(2,1)S(1)}, u32[]{:S(2)}, u32[]{:S(2)}) %collective-permute-start) | collective-permute-done | bytes 786464 | tf_op jit(solution)/shard_map/ppermute | solution.py:34
  5.3 1.6 %collective-permute-start.1 = (bf16[2,2,256,128]{3,2,1,0:T(8,128)(2,1)S(1)}, bf16[2,2,256,128]{3,2,1,0:T(8,128)(2,1)S(1)}, u32[]{:S(2)}, u32[]{:S(2)}) collective-permute-start(bf16[2,2,256,128]{3,2,1,0:T(8,128)(2,1)S(1)} %get-tuple-element.45), channel_id=1, source_target_pairs={{0,8},{8,16},{16,24},{24,0},{1,9},{9,17},{17,25},{25,1},{2,10},{10... | collective-permute-start | bytes 786440 | tf_op jit(solution)/shard_map/ppermute | solution.py:34
  7.0 1.7 %collective-permute-start.3 = (bf16[2,2,256,128]{3,2,1,0:T(8,128)(2,1)S(1)}, bf16[2,2,256,128]{3,2,1,0:T(8,128)(2,1)S(1)}, u32[]{:S(2)}, u32[]{:S(2)}) collective-permute-start(bf16[2,2,256,128]{3,2,1,0:T(8,128)(2,1)S(1)} %get-tuple-element.47), channel_id=1, source_target_pairs={{0,24},{8,0},{16,8},{24,16},{1,25},{9,1},{17,9},{25,17},{2,26},{10... | collective-permute-start | bytes 786440 | tf_op jit(solution)/shard_map/ppermute | solution.py:34
  8.7 2.0 %collective-permute-start.2 = (bf16[2,2,256,128]{3,2,1,0:T(8,128)(2,1)S(1)}, bf16[2,2,256,128]{3,2,1,0:T(8,128)(2,1)S(1)}, u32[]{:S(2)}, u32[]{:S(2)}) collective-permute-start(bf16[2,2,256,128]{3,2,1,0:T(8,128)(2,1)S(1)} %get-tuple-element.46), channel_id=1, source_target_pairs={{0,16},{8,24},{16,0},{24,8},{1,17},{9,25},{17,1},{25,9},{2,18},{10... | collective-permute-start | bytes 786440 | tf_op jit(solution)/shard_map/ppermute | solution.py:34
  10.6 4.4 %collective-permute-done.1.refs_2_.first.refs_1_ = bf16[2,2,256,128]{3,2,1,0:T(8,128)(2,1)S(1)} collective-permute-done((bf16[2,2,256,128]{3,2,1,0:T(8,128)(2,1)S(1)}, bf16[2,2,256,128]{3,2,1,0:T(8,128)(2,1)S(1)}, u32[]{:S(2)}, u32[]{:S(2)}) %collective-permute-start.1) | collective-permute-done | bytes 262176 | tf_op jit(solution)/shard_map/ppermute | solution.py:34
  15.0 5.0 %collective-permute-done.3.refs_4_.second.refs_3_ = bf16[2,2,256,128]{3,2,1,0:T(8,128)(2,1)S(1)} collective-permute-done((bf16[2,2,256,128]{3,2,1,0:T(8,128)(2,1)S(1)}, bf16[2,2,256,128]{3,2,1,0:T(8,128)(2,1)S(1)}, u32[]{:S(2)}, u32[]{:S(2)}) %collective-permute-start.3) | collective-permute-done | bytes 262176 | tf_op jit(solution)/shard_map/ppermute | solution.py:34
  20.1 2.0 %collective-permute-start.8 = (bf16[2,2,2,256,128]{4,3,2,1,0:T(8,128)(2,1)S(1)}, bf16[2,2,2,256,128]{4,3,2,1,0:T(8,128)(2,1)S(1)}, u32[]{:S(2)}, u32[]{:S(2)}) collective-permute-start(bf16[2,2,2,256,128]{4,3,2,1,0:T(8,128)(2,1)S(1)} %pack.1), channel_id=1, source_target_pairs={{0,32},{32,64},{64,96},{96,128},{128,160},{160,192},{192,224},{224... | collective-permute-start | bytes 1572872 | tf_op jit(solution)/shard_map/ppermute | solution.py:34
  22.1 5.1 %collective-permute-start.5 = (bf16[2,256,128]{2,1,0:T(8,128)(2,1)S(1)}, bf16[2,256,128]{2,1,0:T(8,128)(2,1)S(1)}, u32[]{:S(2)}, u32[]{:S(2)}) collective-permute-start(bf16[2,256,128]{2,1,0:T(8,128)(2,1)S(1)} %get-tuple-element.50), channel_id=1, source_target_pairs={{0,16},{8,24},{16,0},{24,8},{1,17},{9,25},{17,1},{25,9},{2,18},{10... | collective-permute-start | bytes 393224 | tf_op jit(solution)/shard_map/ppermute | solution.py:34
  28.7 4.8 %collective-permute-start.7 = (bf16[2,2,256,128]{3,2,1,0:T(8,128)(2,1)S(1)}, bf16[2,2,256,128]{3,2,1,0:T(8,128)(2,1)S(1)}, u32[]{:S(2)}, u32[]{:S(2)}) collective-permute-start(bf16[2,2,256,128]{3,2,1,0:T(8,128)(2,1)S(1)} %get-tuple-element.44.refs_1_.refs_0_), channel_id=1, source_target_pairs={{0,32},{32,64},{64,96},{96,128},{128,160},{160,192},{192,224},{224... | collective-permute-start | bytes 786440 | tf_op jit(solution)/shard_map/ppermute | solution.py:34
  36.0 3.5 %own_first.1 = (bf16[2048,128]{1,0:T(8,128)(2,1)S(1)}, bf16[2048,256]{1,0:T(8,128)(2,1)S(1)}, bf16[2048,128]{1,0:T(8,128)(2,1)S(1)}, f32[1536,256]{1,0:T(8,128)S(1)}, f32[1536,128]{1,0:T(8,128)S(1)}) custom-call(s32[4]{0:T(128)S(1)} %get-tuple-element.83.here_ref.refs_0_.place_ref, bf16[2,2,256,128]{3,2,1,0:T(8,128)(2,1)S(1)} %get-tuple-element.44.refs_1_.refs_0_, ...), custom_call_target="tpu_custom_call" | custom-call | flops 1409286144 | bytes 5242880 | tf_op jit(solution)/shard_map/own_first/pallas_call | solution.py:224
  40.5 1.7 %own_second.1 = (f32[512,256]{1,0:T(8,128)S(1)}, f32[512,128]{1,0:T(8,128)S(1)}) custom-call(bf16[2048,128]{1,0:T(8,128)(2,1)S(1)} %get-tuple-element.55.keys, bf16[2048,256]{1,0:T(8,128)(2,1)S(1)} %get-tuple-element.56.values, bf16[2048,128]{1,0:T(8,128)(2,1)S(1)} %get-tuple-element.52.query.refs_4_.refs_2_), custom_call_target="tpu_custom_call" | custom-call | flops 1006632960 | bytes 3145728 | tf_op jit(solution)/shard_map/own_second/pallas_call | solution.py:246
  42.2 4.3 %collective-permute-done.11.after = bf16[136,128]{1,0:T(8,128)(2,1)S(1)} collective-permute-done((bf16[136,128]{1,0:T(8,128)(2,1)S(1)}, bf16[136,128]{1,0:T(8,128)(2,1)S(1)}, u32[]{:S(2)}, u32[]{:S(2)}) %collective-permute-start.11) | collective-permute-done | bytes 34848 | tf_op jit(solution)/shard_map/ppermute | solution.py:34
  46.5 3.0 %collective-permute-start.12 = (bf16[136,128]{1,0:T(8,128)(2,1)S(1)}, bf16[136,128]{1,0:T(8,128)(2,1)S(1)}, u32[]{:S(2)}, u32[]{:S(2)}) collective-permute-start(bf16[136,128]{1,0:T(8,128)(2,1)S(1)} %get-tuple-element.65), channel_id=1, source_target_pairs={{0,128},{32,160},{64,192},{96,224},{128,0},{160,32},{192,64},{224,... | collective-permute-start | bytes 104456 | tf_op jit(solution)/shard_map/ppermute | solution.py:34
  49.5 4.6 %past.1 = (f32[2048,128]{1,0:T(8,128)S(1)}, bf16[1024,4096]{1,0:T(8,128)(2,1)S(1)}) custom-call(s32[4]{0:T(128)S(1)} %get-tuple-element.83.here_ref.refs_0_.place_ref, bf16[2,2,256,128]{3,2,1,0:T(8,128)(2,1)S(1)} %collective-permute-done.7.refs_1_, bf16[2,2,2,256,128]{4,3,2,1,0:T(8,128)(2,1)S(1)} %collective-permute-done.8.refs_2_, ...), custom_call_target="tpu_custom_call" | custom-call | flops 2415919104 | bytes 6291456 | tf_op jit(solution)/shard_map/past/pallas_call | solution.py:392
  55.6 2.1 %collective-permute-start.13 = (bf16[2,256,128]{2,1,0:T(8,128)(2,1)S(1)}, bf16[2,256,128]{2,1,0:T(8,128)(2,1)S(1)}, u32[]{:S(2)}, u32[]{:S(2)}) collective-permute-start(bf16[2,256,128]{2,1,0:T(8,128)(2,1)S(1)} %get-tuple-element.67), channel_id=1, source_target_pairs={{0,24},{8,0},{16,8},{24,16},{1,25},{9,1},{17,9},{25,17},{2,26},{10... | collective-permute-start | bytes 393224 | tf_op jit(solution)/shard_map/ppermute | solution.py:34
  58.8 2.9 %collective-permute-done.13.refs_2_ = bf16[2,256,128]{2,1,0:T(8,128)(2,1)S(1)} collective-permute-done((bf16[2,256,128]{2,1,0:T(8,128)(2,1)S(1)}, bf16[2,256,128]{2,1,0:T(8,128)(2,1)S(1)}, u32[]{:S(2)}, u32[]{:S(2)}) %collective-permute-start.13) | collective-permute-done | bytes 131104 | tf_op jit(solution)/shard_map/ppermute | solution.py:34
  61.7 2.6 %collective-permute-done.14.refs_3_ = bf16[2,256,128]{2,1,0:T(8,128)(2,1)S(1)} collective-permute-done((bf16[2,256,128]{2,1,0:T(8,128)(2,1)S(1)}, bf16[2,256,128]{2,1,0:T(8,128)(2,1)S(1)}, u32[]{:S(2)}, u32[]{:S(2)}) %collective-permute-start.14) | collective-permute-done | bytes 131104 | tf_op jit(solution)/shard_map/ppermute | solution.py:34
  66.3 1.5 %collective-permute-done.16.refs_5_ = bf16[4,256,128]{2,1,0:T(8,128)(2,1)S(1)} collective-permute-done((bf16[4,256,128]{2,1,0:T(8,128)(2,1)S(1)}, bf16[4,256,128]{2,1,0:T(8,128)(2,1)S(1)}, u32[]{:S(2)}, u32[]{:S(2)}) %collective-permute-start.16) | collective-permute-done | bytes 262176 | tf_op jit(solution)/shard_map/ppermute | solution.py:34
  69.2 1.6 %collective-permute-start.18 = (bf16[128,1024]{1,0:T(8,128)(2,1)S(1)}, bf16[128,1024]{1,0:T(8,128)(2,1)S(1)}, u32[]{:S(2)}, u32[]{:S(2)}) collective-permute-start(bf16[128,1024]{1,0:T(8,128)(2,1)S(1)} %get-tuple-element.75), channel_id=1, source_target_pairs={{0,1},{1,2},{2,3},{3,0},{4,5},{5,6},{6,7},{7,4},{8,9},{9,10},{10,1... | collective-permute-start | bytes 786440 | tf_op jit(solution)/shard_map/ppermute | solution.py:34
  70.8 1.7 %collective-permute-start.21 = (bf16[128,1024]{1,0:T(8,128)(2,1)S(1)}, bf16[128,1024]{1,0:T(8,128)(2,1)S(1)}, u32[]{:S(2)}, u32[]{:S(2)}) collective-permute-start(bf16[128,1024]{1,0:T(8,128)(2,1)S(1)} %get-tuple-element.78), channel_id=1, source_target_pairs={{0,3},{1,0},{2,1},{3,2},{4,7},{5,4},{6,5},{7,6},{8,11},{9,8},{10,9... | collective-permute-start | bytes 786440 | tf_op jit(solution)/shard_map/ppermute | solution.py:34
  75.9 3.0 %collective-permute-start.17 = (bf16[128,1024]{1,0:T(8,128)(2,1)S(1)}, bf16[128,1024]{1,0:T(8,128)(2,1)S(1)}, u32[]{:S(2)}, u32[]{:S(2)}) collective-permute-start(bf16[128,1024]{1,0:T(8,128)(2,1)S(1)} %get-tuple-element.73), channel_id=1, source_target_pairs={{0,3},{1,0},{2,1},{3,2},{4,7},{5,4},{6,5},{7,6},{8,11},{9,8},{10,9... | collective-permute-start | bytes 786440 | tf_op jit(solution)/shard_map/ppermute | solution.py:34
  80.2 3.0 %collective-permute-start.22 = (bf16[128,1024]{1,0:T(8,128)(2,1)S(1)}, bf16[128,1024]{1,0:T(8,128)(2,1)S(1)}, u32[]{:S(2)}, u32[]{:S(2)}) collective-permute-start(bf16[128,1024]{1,0:T(8,128)(2,1)S(1)} %added.3), channel_id=1, source_target_pairs={{0,3},{1,0},{2,1},{3,2},{4,7},{5,4},{6,5},{7,6},{8,11},{9,8},{10,9... | collective-permute-start | bytes 786440 | tf_op jit(solution)/shard_map/ppermute | solution.py:34
  85.7 4.5 %collective-permute-done.19.up_b = bf16[128,1024]{1,0:T(8,128)(2,1)S(1)} collective-permute-done((bf16[128,1024]{1,0:T(8,128)(2,1)S(1)}, bf16[128,1024]{1,0:T(8,128)(2,1)S(1)}, u32[]{:S(2)}, u32[]{:S(2)}) %collective-permute-start.19) | collective-permute-done | bytes 262176 | tf_op jit(solution)/shard_map/ppermute | solution.py:34
  (44 shorter events, 20.0 us)
Async XLA Ops:
  2.2 2.4 %collective-permute-start = (bf16[4,3,256,128]{3,2,1,0:T(8,128)(2,1)S(1)}, bf16[4,3,256,128]{3,2,1,0:T(8,128)(2,1)S(1)}, u32[]{:S(2)}, u32[]{:S(2)}) collective-permute-start(bf16[4,3,256,128]{3,2,1,0:T(8,128)(2,1)S(1)} %get-tuple-element.43), channel_id=1, source_target_pairs={{0,4},{4,0},{1,5},{5,1},{2,6},{6,2},{3,7},{7,3},{8,12},{12,8},{9,1... | collective-permute-start | bytes 2359304 | tf_op jit(solution)/shard_map/ppermute | solution.py:34
  5.3 9.7 %collective-permute-start.1 = (bf16[2,2,256,128]{3,2,1,0:T(8,128)(2,1)S(1)}, bf16[2,2,256,128]{3,2,1,0:T(8,128)(2,1)S(1)}, u32[]{:S(2)}, u32[]{:S(2)}) collective-permute-start(bf16[2,2,256,128]{3,2,1,0:T(8,128)(2,1)S(1)} %get-tuple-element.45), channel_id=1, source_target_pairs={{0,8},{8,16},{16,24},{24,0},{1,9},{9,17},{17,25},{25,1},{2,10},{10... | collective-permute-start | bytes 786440 | tf_op jit(solution)/shard_map/ppermute | solution.py:34
  7.0 13.1 %collective-permute-start.3 = (bf16[2,2,256,128]{3,2,1,0:T(8,128)(2,1)S(1)}, bf16[2,2,256,128]{3,2,1,0:T(8,128)(2,1)S(1)}, u32[]{:S(2)}, u32[]{:S(2)}) collective-permute-start(bf16[2,2,256,128]{3,2,1,0:T(8,128)(2,1)S(1)} %get-tuple-element.47), channel_id=1, source_target_pairs={{0,24},{8,0},{16,8},{24,16},{1,25},{9,1},{17,9},{25,17},{2,26},{10... | collective-permute-start | bytes 786440 | tf_op jit(solution)/shard_map/ppermute | solution.py:34
  8.7 24.8 %collective-permute-start.2 = (bf16[2,2,256,128]{3,2,1,0:T(8,128)(2,1)S(1)}, bf16[2,2,256,128]{3,2,1,0:T(8,128)(2,1)S(1)}, u32[]{:S(2)}, u32[]{:S(2)}) collective-permute-start(bf16[2,2,256,128]{3,2,1,0:T(8,128)(2,1)S(1)} %get-tuple-element.46), channel_id=1, source_target_pairs={{0,16},{8,24},{16,0},{24,8},{1,17},{9,25},{17,1},{25,9},{2,18},{10... | collective-permute-start | bytes 786440 | tf_op jit(solution)/shard_map/ppermute | solution.py:34
  20.1 29.4 %collective-permute-start.8 = (bf16[2,2,2,256,128]{4,3,2,1,0:T(8,128)(2,1)S(1)}, bf16[2,2,2,256,128]{4,3,2,1,0:T(8,128)(2,1)S(1)}, u32[]{:S(2)}, u32[]{:S(2)}) collective-permute-start(bf16[2,2,2,256,128]{4,3,2,1,0:T(8,128)(2,1)S(1)} %pack.1), channel_id=1, source_target_pairs={{0,32},{32,64},{64,96},{96,128},{128,160},{160,192},{192,224},{224... | collective-permute-start | bytes 1572872 | tf_op jit(solution)/shard_map/ppermute | solution.py:34
  22.1 6.6 %collective-permute-start.4 = (bf16[2,256,128]{2,1,0:T(8,128)(2,1)S(1)}, bf16[2,256,128]{2,1,0:T(8,128)(2,1)S(1)}, u32[]{:S(2)}, u32[]{:S(2)}) collective-permute-start(bf16[2,256,128]{2,1,0:T(8,128)(2,1)S(1)} %get-tuple-element.49), channel_id=1, source_target_pairs={{0,8},{8,16},{16,24},{24,0},{1,9},{9,17},{17,25},{25,1},{2,10},{10... | collective-permute-start | bytes 393224 | tf_op jit(solution)/shard_map/ppermute | solution.py:34
  22.1 12.9 %collective-permute-start.5 = (bf16[2,256,128]{2,1,0:T(8,128)(2,1)S(1)}, bf16[2,256,128]{2,1,0:T(8,128)(2,1)S(1)}, u32[]{:S(2)}, u32[]{:S(2)}) collective-permute-start(bf16[2,256,128]{2,1,0:T(8,128)(2,1)S(1)} %get-tuple-element.50), channel_id=1, source_target_pairs={{0,16},{8,24},{16,0},{24,8},{1,17},{9,25},{17,1},{25,9},{2,18},{10... | collective-permute-start | bytes 393224 | tf_op jit(solution)/shard_map/ppermute | solution.py:34
  27.2 8.9 %collective-permute-start.6 = (bf16[2,256,128]{2,1,0:T(8,128)(2,1)S(1)}, bf16[2,256,128]{2,1,0:T(8,128)(2,1)S(1)}, u32[]{:S(2)}, u32[]{:S(2)}) collective-permute-start(bf16[2,256,128]{2,1,0:T(8,128)(2,1)S(1)} %get-tuple-element.51), channel_id=1, source_target_pairs={{0,24},{8,0},{16,8},{24,16},{1,25},{9,1},{17,9},{25,17},{2,26},{10... | collective-permute-start | bytes 393224 | tf_op jit(solution)/shard_map/ppermute | solution.py:34
  28.7 20.8 %collective-permute-start.7 = (bf16[2,2,256,128]{3,2,1,0:T(8,128)(2,1)S(1)}, bf16[2,2,256,128]{3,2,1,0:T(8,128)(2,1)S(1)}, u32[]{:S(2)}, u32[]{:S(2)}) collective-permute-start(bf16[2,2,256,128]{3,2,1,0:T(8,128)(2,1)S(1)} %get-tuple-element.44.refs_1_.refs_0_), channel_id=1, source_target_pairs={{0,32},{32,64},{64,96},{96,128},{128,160},{160,192},{192,224},{224... | collective-permute-start | bytes 786440 | tf_op jit(solution)/shard_map/ppermute | solution.py:34
  33.5 16.0 %collective-permute-start.9 = (bf16[2,2,256,128]{3,2,1,0:T(8,128)(2,1)S(1)}, bf16[2,2,256,128]{3,2,1,0:T(8,128)(2,1)S(1)}, u32[]{:S(2)}, u32[]{:S(2)}) collective-permute-start(bf16[2,2,256,128]{3,2,1,0:T(8,128)(2,1)S(1)} %collective-permute-done.2.refs_3_.refs_2_), channel_id=1, source_target_pairs={{0,32},{32,64},{64,96},{96,128},{128,160},{160,192},{192,224},{224... | collective-permute-start | bytes 786440 | tf_op jit(solution)/shard_map/ppermute | solution.py:34
  35.0 4.6 %collective-permute-start.10 = (bf16[136,128]{1,0:T(8,128)(2,1)S(1)}, bf16[136,128]{1,0:T(8,128)(2,1)S(1)}, u32[]{:S(2)}, u32[]{:S(2)}) collective-permute-start(bf16[136,128]{1,0:T(8,128)(2,1)S(1)} %get-tuple-element.61), channel_id=1, source_target_pairs={{0,224},{32,0},{64,32},{96,64},{128,96},{160,128},{192,160},{224,1... | collective-permute-start | bytes 104456 | tf_op jit(solution)/shard_map/ppermute | solution.py:34
  40.2 6.3 %collective-permute-start.11 = (bf16[136,128]{1,0:T(8,128)(2,1)S(1)}, bf16[136,128]{1,0:T(8,128)(2,1)S(1)}, u32[]{:S(2)}, u32[]{:S(2)}) collective-permute-start(bf16[136,128]{1,0:T(8,128)(2,1)S(1)} %get-tuple-element.63), channel_id=1, source_target_pairs={{0,192},{32,224},{64,0},{96,32},{128,64},{160,96},{192,128},{224,1... | collective-permute-start | bytes 104456 | tf_op jit(solution)/shard_map/ppermute | solution.py:34
  40.4 14.0 %copy-start = (f32[8]{0:T(128)S(1)}, f32[8]{0:T(128)}, u32[]{:S(2)}) copy-start(f32[8]{0:T(128)} %refs_1_.1) | copy-start | bytes 100
  46.5 7.9 %collective-permute-start.12 = (bf16[136,128]{1,0:T(8,128)(2,1)S(1)}, bf16[136,128]{1,0:T(8,128)(2,1)S(1)}, u32[]{:S(2)}, u32[]{:S(2)}) collective-permute-start(bf16[136,128]{1,0:T(8,128)(2,1)S(1)} %get-tuple-element.65), channel_id=1, source_target_pairs={{0,128},{32,160},{64,192},{96,224},{128,0},{160,32},{192,64},{224,... | collective-permute-start | bytes 104456 | tf_op jit(solution)/shard_map/ppermute | solution.py:34
  55.6 6.0 %collective-permute-start.13 = (bf16[2,256,128]{2,1,0:T(8,128)(2,1)S(1)}, bf16[2,256,128]{2,1,0:T(8,128)(2,1)S(1)}, u32[]{:S(2)}, u32[]{:S(2)}) collective-permute-start(bf16[2,256,128]{2,1,0:T(8,128)(2,1)S(1)} %get-tuple-element.67), channel_id=1, source_target_pairs={{0,24},{8,0},{16,8},{24,16},{1,25},{9,1},{17,9},{25,17},{2,26},{10... | collective-permute-start | bytes 393224 | tf_op jit(solution)/shard_map/ppermute | solution.py:34
  57.8 6.6 %collective-permute-start.14 = (bf16[2,256,128]{2,1,0:T(8,128)(2,1)S(1)}, bf16[2,256,128]{2,1,0:T(8,128)(2,1)S(1)}, u32[]{:S(2)}, u32[]{:S(2)}) collective-permute-start(bf16[2,256,128]{2,1,0:T(8,128)(2,1)S(1)} %get-tuple-element.68), channel_id=1, source_target_pairs={{0,16},{8,24},{16,0},{24,8},{1,17},{9,25},{17,1},{25,9},{2,18},{10... | collective-permute-start | bytes 393224 | tf_op jit(solution)/shard_map/ppermute | solution.py:34
  58.3 7.3 %collective-permute-start.15 = (bf16[2,256,128]{2,1,0:T(8,128)(2,1)S(1)}, bf16[2,256,128]{2,1,0:T(8,128)(2,1)S(1)}, u32[]{:S(2)}, u32[]{:S(2)}) collective-permute-start(bf16[2,256,128]{2,1,0:T(8,128)(2,1)S(1)} %get-tuple-element.69), channel_id=1, source_target_pairs={{0,8},{8,16},{16,24},{24,0},{1,9},{9,17},{17,25},{25,1},{2,10},{10... | collective-permute-start | bytes 393224 | tf_op jit(solution)/shard_map/ppermute | solution.py:34
  66.2 1.6 %collective-permute-start.16 = (bf16[4,256,128]{2,1,0:T(8,128)(2,1)S(1)}, bf16[4,256,128]{2,1,0:T(8,128)(2,1)S(1)}, u32[]{:S(2)}, u32[]{:S(2)}) collective-permute-start(bf16[4,256,128]{2,1,0:T(8,128)(2,1)S(1)} %turn.1), channel_id=1, source_target_pairs={{0,4},{4,0},{1,5},{5,1},{2,6},{6,2},{3,7},{7,3},{8,12},{12,8},{9,1... | collective-permute-start | bytes 786440 | tf_op jit(solution)/shard_map/ppermute | solution.py:34
  69.2 10.5 %collective-permute-start.18 = (bf16[128,1024]{1,0:T(8,128)(2,1)S(1)}, bf16[128,1024]{1,0:T(8,128)(2,1)S(1)}, u32[]{:S(2)}, u32[]{:S(2)}) collective-permute-start(bf16[128,1024]{1,0:T(8,128)(2,1)S(1)} %get-tuple-element.75), channel_id=1, source_target_pairs={{0,1},{1,2},{2,3},{3,0},{4,5},{5,6},{6,7},{7,4},{8,9},{9,10},{10,1... | collective-permute-start | bytes 786440 | tf_op jit(solution)/shard_map/ppermute | solution.py:34
  70.8 9.3 %collective-permute-start.21 = (bf16[128,1024]{1,0:T(8,128)(2,1)S(1)}, bf16[128,1024]{1,0:T(8,128)(2,1)S(1)}, u32[]{:S(2)}, u32[]{:S(2)}) collective-permute-start(bf16[128,1024]{1,0:T(8,128)(2,1)S(1)} %get-tuple-element.78), channel_id=1, source_target_pairs={{0,3},{1,0},{2,1},{3,2},{4,7},{5,4},{6,5},{7,6},{8,11},{9,8},{10,9... | collective-permute-start | bytes 786440 | tf_op jit(solution)/shard_map/ppermute | solution.py:34
  74.0 11.4 %collective-permute-start.20 = (bf16[128,1024]{1,0:T(8,128)(2,1)S(1)}, bf16[128,1024]{1,0:T(8,128)(2,1)S(1)}, u32[]{:S(2)}, u32[]{:S(2)}) collective-permute-start(bf16[128,1024]{1,0:T(8,128)(2,1)S(1)} %get-tuple-element.76), channel_id=1, source_target_pairs={{0,1},{1,2},{2,3},{3,0},{4,5},{5,6},{6,7},{7,4},{8,9},{9,10},{10,1... | collective-permute-start | bytes 786440 | tf_op jit(solution)/shard_map/ppermute | solution.py:34
  75.9 9.7 %collective-permute-start.17 = (bf16[128,1024]{1,0:T(8,128)(2,1)S(1)}, bf16[128,1024]{1,0:T(8,128)(2,1)S(1)}, u32[]{:S(2)}, u32[]{:S(2)}) collective-permute-start(bf16[128,1024]{1,0:T(8,128)(2,1)S(1)} %get-tuple-element.73), channel_id=1, source_target_pairs={{0,3},{1,0},{2,1},{3,2},{4,7},{5,4},{6,5},{7,6},{8,11},{9,8},{10,9... | collective-permute-start | bytes 786440 | tf_op jit(solution)/shard_map/ppermute | solution.py:34
  79.7 10.4 %collective-permute-start.19 = (bf16[128,1024]{1,0:T(8,128)(2,1)S(1)}, bf16[128,1024]{1,0:T(8,128)(2,1)S(1)}, u32[]{:S(2)}, u32[]{:S(2)}) collective-permute-start(bf16[128,1024]{1,0:T(8,128)(2,1)S(1)} %added.2), channel_id=1, source_target_pairs={{0,1},{1,2},{2,3},{3,0},{4,5},{5,6},{6,7},{7,4},{8,9},{9,10},{10,1... | collective-permute-start | bytes 786440 | tf_op jit(solution)/shard_map/ppermute | solution.py:34
  80.2 10.0 %collective-permute-start.22 = (bf16[128,1024]{1,0:T(8,128)(2,1)S(1)}, bf16[128,1024]{1,0:T(8,128)(2,1)S(1)}, u32[]{:S(2)}, u32[]{:S(2)}) collective-permute-start(bf16[128,1024]{1,0:T(8,128)(2,1)S(1)} %added.3), channel_id=1, source_target_pairs={{0,3},{1,0},{2,1},{3,2},{4,7},{5,4},{6,5},{7,6},{8,11},{9,8},{10,9... | collective-permute-start | bytes 786440 | tf_op jit(solution)/shard_map/ppermute | solution.py:34
